TPU v7x, 256 devices: a whole 4x4x8 slice. The times are simulated.
256 devices in a mesh: seq: 64 (over y, x_lo, z), dp: 4 (over x_hi, core).
Axes of the slice: x: 4 (x_hi: 2, x_lo: 2; x = x_hi * 2 + x_lo), y: 4, z: 8, core: 2. Of those that a mesh axis runs over, the one named last changes fastest.
Arguments:
- queries: bfloat16 [4, 16384, 2048], P('dp', 'seq'), may hold values from -12 to 12
- keys: bfloat16 [4, 16384, 1024], P('dp', 'seq'), may hold values from -6 to 6
- values: bfloat16 [4, 16384, 1024], P('dp', 'seq'), may hold values from -6 to 6
- out_grad: bfloat16 [4, 16384, 1792], P('dp', 'seq'), may hold values from -6 to 6
- out_weight: bfloat16 [2048, 1792], P('seq'), may hold values from -0.125 to 0.125
- seq_len: int32 [4], P('dp'), may hold values from 4096 to 16384, as said below
Outputs:
- query_grad: bfloat16 [4, 16384, 2048], P('dp', 'seq')
- key_grad: bfloat16 [4, 16384, 1024], P('dp', 'seq')
- value_grad: bfloat16 [4, 16384, 1024], P('dp', 'seq')
- weight_grad: float32 [2048, 1792], P('seq')
- grad_rms: float32 [], replicated
Inputs may be any that keep to these rules, and one draw needn't show every extreme that they name: `seq_len`: at least one sequence has the full length 16384.
All inputs are finite; a program needn't handle non-finite values.
Results may differ from a plain program's by a relative error of at most 0.014.
Values may be sent and summed in bfloat16 or wider, within the bound.
No kernel may reach another device: no remote copies, remote signals or barrier semaphores. Data moves between devices by JAX's collectives and lax.ppermute only.
A program may use at most 128 MiB of HBM per device.

v0:
```python
import math

import jax
import jax.numpy as jnp
from jax import lax
from jax.experimental import pallas as pl
from jax.experimental.pallas import tpu as pltpu
from jax.sharding import Mesh
from jax.sharding import PartitionSpec as P


HEADS = 8
KV_HEADS = 4
GROUP = HEADS // KV_HEADS
HEAD_DIM = 256
D_OUT = 1792
HALF = D_OUT // 2
TOK_DEV = 256
WIDTH = HEADS * HEAD_DIM
SEQ = ("seq_0", "seq_1", "seq_2")
DP = ("dp_0", "dp_1")
X_AXES = ("seq_1", "dp_0")
SCALE = 0.0625
CAP = 50.0
EXP_MUL = CAP * math.log2(math.e)
BF16 = jnp.bfloat16
F32 = jnp.float32


def shifted(value, steps):
    count = lax.axis_size(SEQ)
    initial, last = (max(0, -steps), min(count, count - steps))
    return lax.ppermute(value, SEQ, [(source, source + steps) for source in range(initial, last)])


def ring(value, axis, steps):
    count = lax.axis_size(axis)
    return lax.ppermute(value, axis, [(s, (s + steps) % count) for s in range(count)])


def ring_x(value, steps):
    at = lambda x: (x % 2) * 2 + x // 2
    return lax.ppermute(value, X_AXES, [(at(s), at((s + steps) % 4)) for s in range(4)])


def swap(value, axis):
    return lax.ppermute(value, axis, [(0, 1), (1, 0)])


def for_each(value, axis):
    size = lax.axis_size(axis)
    return lax.all_to_all(
        jnp.broadcast_to(value[None], (size, *value.shape)), axis, 0, 0, tiled=True
    )


def dot(a, b, dims):
    return lax.dot_general(a, b, (dims, ((), ())), preferred_element_type=F32)


NT = ((1,), (1,))
NN = ((1,), (0,))
TN = ((0,), (0,))


def squashed(k, q):
    t = jnp.tanh(dot(k, q, NT) * (SCALE / CAP))
    return t, jnp.exp2(t * EXP_MUL)


def places():
    shape = (TOK_DEV, GROUP * TOK_DEV)
    key = lax.broadcasted_iota(jnp.int32, shape, 0)
    query = lax.broadcasted_iota(jnp.int32, shape, 1) & (TOK_DEV - 1)
    return key, query


def two_heads(q_ref):
    return jnp.concatenate([q_ref[:, h * HEAD_DIM : (h + 1) * HEAD_DIM] for h in range(GROUP)], 0)


def row_sum(e):
    return jnp.sum(e, axis=0, keepdims=True)


def near_kernel(at_ref, q_ref, k0_ref, v0_ref, h1_ref, p_ref, pf_ref, acc_ref, tot_ref):
    q = two_heads(q_ref)
    key, query = places()
    t, e = squashed(h1_ref[:TOK_DEV], q)
    e = e * jnp.where(at_ref[0] >= 1, 1.0, 0.0)
    p1 = e.astype(BF16)
    p_ref[0, :TOK_DEV] = p1
    pf_ref[0, :TOK_DEV] = (e * (1.0 - t * t)).astype(BF16)
    total = row_sum(e)
    t, e = squashed(k0_ref[...], q)
    e = jnp.where(key <= query, e, 0.0)
    p0 = e.astype(BF16)
    p_ref[0, TOK_DEV:] = p0
    pf_ref[0, TOK_DEV:] = (e * (1.0 - t * t)).astype(BF16)
    total = total + row_sum(e)
    acc_ref[0] = dot(h1_ref[TOK_DEV:], p1, TN) + dot(v0_ref[...], p0, TN)
    tot_ref[0] = jnp.broadcast_to(total, tot_ref.shape[1:])


def far_kernel(at_ref, q_ref, h2_ref, acc_ref, tot_ref, p_ref, pf_ref, attn_ref, inv_ref):
    key, query = places()
    t, e = squashed(h2_ref[:TOK_DEV], two_heads(q_ref))
    e = jnp.where(key > query + jnp.where(at_ref[0] >= 2, 0, 4 * TOK_DEV), e, 0.0)
    p = e.astype(BF16)
    p_ref[0] = p
    pf_ref[0] = (e * (1.0 - t * t)).astype(BF16)
    inverse = 1.0 / (tot_ref[0, :1] + row_sum(e))
    inv_ref[0] = jnp.broadcast_to(inverse, inv_ref.shape[1:])
    out = ((acc_ref[0] + dot(h2_ref[TOK_DEV:], p, TN)) * inverse).astype(BF16)
    for h in range(GROUP):
        attn_ref[h * HEAD_DIM : (h + 1) * HEAD_DIM, :] = out[:, h * TOK_DEV : (h + 1) * TOK_DEV]


def terms(k, v, q, p, pf, g, delta):
    dscore = (pf.astype(F32) * (dot(v, g, NN) - delta)).astype(BF16)
    return dot(k, dscore, TN), dot(dscore, q, NN), dot(p, g, NT)


def far_grad_kernel(
    at_ref, scale_ref, q_ref, h2_ref, p_ref, pf_ref, inv_ref, attn_ref, m_own_ref, m_oth_ref,
    wa_ref, wc_ref, wbl_ref, wbh_ref, wdl_ref, wdh_ref,
    d2_ref, g_ref, delta_ref, dq_ref, raw_ref,
):
    act_scale = scale_ref[0]
    own = pl.multiple_of(at_ref[2] * TOK_DEV, TOK_DEV)
    oth = pl.multiple_of((1 - at_ref[2]) * TOK_DEV, TOK_DEV)
    m_own = m_own_ref[...]
    m_oth = m_oth_ref[...]
    half = HEAD_DIM // 2
    raw_ref[:, pl.ds(own, TOK_DEV)] = dot(wa_ref[0], m_own, NT) + dot(wc_ref[0], m_oth, NT)
    raw_ref[:half, pl.ds(oth, TOK_DEV)] = dot(wbl_ref[0], m_own, NT) + dot(wdl_ref[0], m_oth, NT)
    raw_ref[half:, pl.ds(oth, TOK_DEV)] = dot(wbh_ref[0], m_own, NT) + dot(wdh_ref[0], m_oth, NT)
    g = (raw_ref[...] * inv_ref[0, :1]).astype(BF16)
    g_ref[0] = g
    attn = jnp.concatenate(
        [attn_ref[h * HEAD_DIM : (h + 1) * HEAD_DIM, :] for h in range(GROUP)], 1
    )
    delta = row_sum(g.astype(F32) * attn.astype(F32))
    delta_ref[0] = jnp.broadcast_to(delta, delta_ref.shape[1:])
    dq, dk, dv = terms(
        h2_ref[:TOK_DEV], h2_ref[TOK_DEV:], two_heads(q_ref), p_ref[0], pf_ref[0], g, delta
    )
    dq_ref[0] = dq
    d2_ref[:TOK_DEV] = (dk * (SCALE * act_scale)).astype(BF16)
    d2_ref[TOK_DEV:] = (dv * act_scale).astype(BF16)


def near_grad_kernel(
    scale_ref, q_ref, k0_ref, v0_ref, h1_ref, p_ref, pf_ref, g_ref, delta_ref, far_ref,
    dq_ref, d0_ref, d1_ref, sq_ref,
):
    act_scale = scale_ref[0]
    q = two_heads(q_ref)
    g = g_ref[0]
    delta = delta_ref[0, :1]
    dq = far_ref[0]
    for k, v, at, out in (
        (h1_ref[:TOK_DEV], h1_ref[TOK_DEV:], 0, d1_ref),
        (k0_ref[...], v0_ref[...], TOK_DEV, d0_ref),
    ):
        piece, dk, dv = terms(
            k, v, q, p_ref[0, at : at + TOK_DEV], pf_ref[0, at : at + TOK_DEV], g, delta
        )
        dq = dq + piece
        out[:TOK_DEV] = (dk * (SCALE * act_scale)).astype(out.dtype)
        out[TOK_DEV:] = (dv * act_scale).astype(out.dtype)
    dq = dq * (SCALE * act_scale)
    sq_ref[...] = jnp.broadcast_to(jnp.sum(dq * dq), sq_ref.shape)
    for h in range(GROUP):
        dq_ref[:, h * HEAD_DIM : (h + 1) * HEAD_DIM] = dq[
            :, h * TOK_DEV : (h + 1) * TOK_DEV
        ].T.astype(BF16)


def weight_kernel(at_ref, a_own_ref, a_oth_ref, m0_ref, m1_ref, m3_ref, m2a_ref, m2b_ref, out_ref):
    acc = None
    for back, (own, oth) in enumerate(
        (
            (m0_ref[:TOK_DEV], m0_ref[TOK_DEV:]),
            (m1_ref[:TOK_DEV], m1_ref[TOK_DEV:]),
            (m2a_ref[...], m2b_ref[...]),
            (m3_ref[:TOK_DEV], m3_ref[TOK_DEV:]),
        )
    ):
        place = (at_ref[1] + 4 - back) % 4
        both = dot(a_own_ref[place], own, NN) + dot(a_oth_ref[place], oth, NN)
        acc = both if acc is None else acc + both
    acc = acc.reshape(2, 8, 2, 16, HALF)
    for low in range(2):
        for high in range(2):
            away = (2 * high + low + 4 - at_ref[3]) % 4
            out_ref[away] = acc[low, :, high].reshape(128, HALF).astype(BF16)


D = HEAD_DIM
SCORES = GROUP * TOK_DEV
HEAD_COLS = pl.BlockSpec((TOK_DEV, GROUP * D), lambda h, *_: (0, h))
KV_COLS = pl.BlockSpec((TOK_DEV, D), lambda h, *_: (0, h))
BOTH_COLS = pl.BlockSpec((2 * TOK_DEV, D), lambda h, *_: (0, h))
ATTN_ROWS = pl.BlockSpec((GROUP * D, TOK_DEV), lambda h, *_: (h, 0))


def of_head(rows, columns=SCORES):
    return pl.BlockSpec((1, rows, columns), lambda h, *_: (h, 0, 0))


def per_head(rows, dtype):
    return jax.ShapeDtypeStruct((KV_HEADS, rows, SCORES), dtype)


def flat(rows, dtype):
    return jax.ShapeDtypeStruct((rows, KV_HEADS * D), dtype)


def call(kernel, scalars, in_specs, out_specs, out_shape, products, mib, scratch=()):
    return pl.pallas_call(
        kernel,
        grid_spec=pltpu.PrefetchScalarGridSpec(
            num_scalar_prefetch=scalars,
            grid=(KV_HEADS,),
            in_specs=in_specs,
            out_specs=out_specs,
            scratch_shapes=scratch,
        ),
        out_shape=out_shape,
        cost_estimate=pl.CostEstimate(
            flops=products * 2 * HEADS * TOK_DEV**3, transcendentals=0, bytes_accessed=mib << 20
        ),
    )


def near_forward(where, q, k, v, h1):
    return call(
        near_kernel, 1,
        [HEAD_COLS, KV_COLS, KV_COLS, BOTH_COLS],
        [of_head(2 * TOK_DEV), of_head(2 * TOK_DEV), of_head(D), of_head(8)],
        [per_head(2 * TOK_DEV, BF16), per_head(2 * TOK_DEV, BF16), per_head(D, F32),
         per_head(8, F32)],
        4, 9,
    )(where, q, k, v, h1)


def far_forward(where, q, h2, acc, tot):
    return call(
        far_kernel, 1,
        [HEAD_COLS, BOTH_COLS, of_head(D), of_head(8)],
        [of_head(TOK_DEV), of_head(TOK_DEV), ATTN_ROWS, of_head(8)],
        [per_head(TOK_DEV, BF16), per_head(TOK_DEV, BF16),
         jax.ShapeDtypeStruct((WIDTH, TOK_DEV), BF16), per_head(8, F32)],
        2, 7,
    )(where, q, h2, acc, tot)


def far_backward(where, scale, q, h2, p, pf, inv, attn, m_own, m_oth, weights):
    full = pl.BlockSpec((TOK_DEV, HALF), lambda h, *_: (0, 0))
    rel = lambda rows: pl.BlockSpec((1, rows, HALF), lambda h, at, *_: ((at[1] + 4 - h) % 4, 0, 0))
    return call(
        far_grad_kernel, 2,
        [HEAD_COLS, BOTH_COLS, of_head(TOK_DEV), of_head(TOK_DEV), of_head(8), ATTN_ROWS, full,
         full, rel(D), rel(D)] + [rel(D // 2)] * 4,
        [BOTH_COLS, of_head(D), of_head(8), of_head(D)],
        [flat(2 * TOK_DEV, BF16), per_head(D, BF16), per_head(8, F32), per_head(D, F32)],
        4 + 7, 16, [pltpu.VMEM((D, SCORES), F32)],
    )(where, scale, q, h2, p, pf, inv, attn, m_own, m_oth, *weights)


def near_backward(scale, q, k, v, h1, p, pf, g, delta, far):
    return call(
        near_grad_kernel, 1,
        [HEAD_COLS, KV_COLS, KV_COLS, BOTH_COLS, of_head(2 * TOK_DEV), of_head(2 * TOK_DEV),
         of_head(D), of_head(8), of_head(D)],
        [HEAD_COLS, BOTH_COLS, BOTH_COLS, pl.BlockSpec((8, 128), lambda h, *_: (h, 0))],
        [jax.ShapeDtypeStruct((TOK_DEV, WIDTH), BF16), flat(2 * TOK_DEV, F32),
         flat(2 * TOK_DEV, BF16), jax.ShapeDtypeStruct((8 * KV_HEADS, 128), F32)],
        8, 14,
    )(scale, q, k, v, h1, p, pf, g, delta, far)


def weight_product(where, a_own, a_oth, m0, m1, m3, m2a, m2b):
    vmem = pl.BlockSpec(memory_space=pltpu.VMEM)
    return pl.pallas_call(
        weight_kernel,
        in_specs=[pl.BlockSpec(memory_space=pltpu.SMEM)] + [vmem] * 7,
        out_specs=vmem,
        out_shape=jax.ShapeDtypeStruct((4, 128, HALF), BF16),
        cost_estimate=pl.CostEstimate(
            flops=2 * 512 * HALF * 2048, transcendentals=0, bytes_accessed=7 << 20
        ),
        name="weight_product",
    )(where, a_own, a_oth, m0, m1, m3, m2a, m2b)


def all_steps(queries, keys, values, out_grad, out_weight, seq_len):
    q_rows = queries[0]
    k_rows = keys[0]
    v_rows = values[0]
    length = seq_len[0]
    core = lax.axis_index("dp_1")
    x_hi = lax.axis_index("dp_0")
    x_lo = lax.axis_index("seq_1")
    index = lax.axis_index(SEQ)
    start = index * TOK_DEV
    where = jnp.stack([index, lax.axis_index("seq_0"), x_lo, 2 * x_hi + x_lo]).astype(jnp.int32)

    kv = jnp.concatenate([k_rows, v_rows], 0)
    h1 = shifted(kv, 1)
    h2 = shifted(h1, 1)

    slots = TOK_DEV * lax.axis_size(SEQ) * lax.axis_size(DP)
    count = jnp.clip(length, 0, TOK_DEV * lax.axis_size(SEQ)).astype(F32).reshape(1)
    count = count + swap(count, "dp_1")
    count = count + swap(count, "dp_0")
    act_scale = slots / count
    weight_scale = lax.rsqrt(count[0])

    half_of = lambda a, c: lax.dynamic_slice_in_dim(a, c * HALF, HALF, 1)
    valid = (start + jnp.arange(TOK_DEV, dtype=jnp.int32)) < length
    masked = jnp.where(valid[:, None], out_grad[0], jnp.zeros((), BF16))
    m_own = half_of(masked, core)
    m_oth = half_of(masked, 1 - core)
    m0 = jnp.concatenate([m_own, swap(m_oth, "dp_1")], 0)
    m1 = ring(m0, "seq_0", 1)
    m3 = ring(m0, "seq_0", -1)
    m2a = ring(m1[:TOK_DEV], "seq_0", 1)
    m2b = ring(m3[TOK_DEV:], "seq_0", -1)

    w_z = for_each(half_of(out_weight, core), "seq_2").reshape(HEAD_DIM, HALF)
    w_up = ring(w_z, "seq_0", 1)
    w_down = ring(w_z, "seq_0", -1)
    mid = HEAD_DIM // 2
    w_far = [ring(w_up[:mid], "seq_0", 1), ring(w_down[mid:], "seq_0", -1)]
    wa = jnp.stack([w_z, w_up, jnp.concatenate(w_far, 0), w_down])
    wbl = ring_x(wa[:, :mid], 1)
    wbh = ring_x(wa[:, mid:], -1)
    wc = swap(wa, "dp_1")
    wdl = swap(wbl, "dp_1")
    wdh = swap(wbh, "dp_1")

    p, pf, acc, tot = near_forward(where, q_rows, k_rows, v_rows, h1)
    p2, pf2, attn, inv = far_forward(where, q_rows, h2, acc, tot)
    a_own = lax.all_to_all(attn, "seq_0", 0, 0, tiled=True)
    a_oth = swap(a_own, "dp_1")

    d2, g, delta, far = far_backward(
        where, act_scale, q_rows, h2, p2, pf2, inv, attn, m_own, m_oth,
        (wa, wc, wbl, wbh, wdl, wdh),
    )
    r1 = shifted(d2, -1)
    dq, d0, d1, dq_sq = near_backward(
        act_scale, q_rows, k_rows, v_rows, h1, p, pf, g, delta, far
    )
    r2 = shifted((d1.astype(F32) + r1.astype(F32)).astype(BF16), -1)
    dkv = d0 + r2.astype(F32)
    square = jnp.sum(dkv * dkv) + jnp.sum(dq_sq.reshape(KV_HEADS, 8, 128)[:, 0, 0])
    dkv = dkv.astype(BF16)

    part = weight_product(
        where, a_own.reshape(4, 512, TOK_DEV), a_oth.reshape(4, 512, TOK_DEV), m0, m1, m3, m2a, m2b
    )
    part = (
        part[0].astype(F32)
        + ring_x(part[1], 1).astype(F32)
        + ring_x(part[2], 2).astype(F32)
        + ring_x(part[3], -1).astype(F32)
    ).astype(BF16)
    pieces = lax.all_to_all(part, "seq_2", 0, 0, tiled=True)
    piece = jnp.sum(pieces.reshape(8, 16, HALF).astype(F32), axis=0) * weight_scale
    square = square + jnp.sum(piece * piece)

    other = swap(piece, "dp_1")
    row = jnp.where(
        core == 0, jnp.concatenate([piece, other], 1), jnp.concatenate([other, piece], 1)
    )
    other = swap(row, "dp_0")
    weight_grad = jnp.where(
        x_hi == 0, jnp.concatenate([row, other], 0), jnp.concatenate([other, row], 0)
    )

    square = jnp.full((8, 128), square, F32)
    square = for_each(square, ("dp_0", "seq_1", "dp_1"))
    square = jnp.full((8, 128), jnp.sum(square[:, 0], axis=0)[0], F32)
    square = for_each(square, ("seq_0", "seq_2"))
    square = jnp.sum(square[:, 0], axis=0)[0]
    entries = slots * (HEADS + 2 * KV_HEADS) * HEAD_DIM + WIDTH * D_OUT
    grad_rms = jnp.sqrt(square / entries)
    return (dq[None], dkv[:TOK_DEV][None], dkv[TOK_DEV:][None], weight_grad, grad_rms)


def solution(mesh):
    split = Mesh(mesh.devices.reshape(4, 2, 8, 2, 2), ("seq_0", "seq_1", "seq_2", "dp_0", "dp_1"))
    placed = (
        P(DP, SEQ, None),
        P(DP, SEQ, None),
        P(DP, SEQ, None),
        P(DP, SEQ, None),
        P(SEQ, None),
        P(DP),
    )
    return jax.shard_map(
        all_steps,
        mesh=split,
        in_specs=placed,
        out_specs=(P(DP, SEQ, None), P(DP, SEQ, None), P(DP, SEQ, None), P(SEQ, None), P()),
        check_vma=False,
    )
```

profile of v0, /device:TPU:1, one launch (start us, length us, event | category | flops | bytes accessed | tf_op | source)
XLA Modules:
  0.0 258.4 jit_solution(1763565041578379599)
XLA Ops:
  0.7 0.9 copy-done
  1.5 0.8 broadcast_in_dim.30
  2.3 9.1 %all-to-all-start = ((bf16[8,32,896]{2,1,0:T(8,128)(2,1)}), bf16[8,32,896]{2,1,0:T(8,128)(2,1)S(1)}, u32[]{:S(2)}, u32[]{:S(2)}) async-start(bf16[8,32,896]{2,1,0:T(8,128)(2,1)} %broadcast_in_dim.30), calls=%async_computation | async-start | bytes 917504 | tf_op jit(solution)/shard_map/all_to_all | solution.py:52
  11.5 1.3 pad_maximum_fusion.1
  12.8 4.4 %collective-permute-start.2 = (bf16[512,1024]{1,0:T(8,128)(2,1)S(1)}, bf16[512,1024]{1,0:T(8,128)(2,1)}, u32[]{:S(2)}, u32[]{:S(2)}) collective-permute-start(bf16[512,1024]{1,0:T(8,128)(2,1)S(1)} %pad_maximum_fusion.1), channel_id=1, source_target_pairs={{0,4},{4,8},{8,12},{12,16},{16,20},{20,24},{24,28},{28,32},{32,36}... | collective-permute-start | bytes 3145736 | tf_op jit(solution)/shard_map/ppermute | solution.py:33
  17.1 10.5 %all-to-all-done = bf16[8,32,896]{2,1,0:T(8,128)(2,1)S(1)} async-done(((bf16[8,32,896]{2,1,0:T(8,128)(2,1)}), bf16[8,32,896]{2,1,0:T(8,128)(2,1)S(1)}, u32[]{:S(2)}, u32[]{:S(2)}) %all-to-all-start) | async-done | bytes 458784 | tf_op jit(solution)/shard_map/all_to_all | solution.py:52
  27.6 2.7 %collective-permute-start.6 = (bf16[256,896]{1,0:T(8,128)(2,1)S(1)}, bf16[256,896]{1,0:T(8,128)(2,1)S(1)}, u32[]{:S(2)}, u32[]{:S(2)}) collective-permute-start(bf16[256,896]{1,0:T(8,128)(2,1)S(1)} %bitcast.58), channel_id=1, source_target_pairs={{0,192},{64,0},{128,64},{192,128},{1,193},{65,1},{129,65},{193,129... | collective-permute-start | bytes 1376264 | tf_op jit(solution)/shard_map/ppermute | solution.py:38
  31.0 8.2 %collective-permute-done.6 = bf16[256,896]{1,0:T(8,128)(2,1)S(1)} collective-permute-done((bf16[256,896]{1,0:T(8,128)(2,1)S(1)}, bf16[256,896]{1,0:T(8,128)(2,1)S(1)}, u32[]{:S(2)}, u32[]{:S(2)}) %collective-permute-start.6) | collective-permute-done | bytes 458784 | tf_op jit(solution)/shard_map/ppermute | solution.py:38
  39.3 0.8 slice.69
  40.0 3.5 %collective-permute-start.7 = (bf16[128,896]{1,0:T(8,128)(2,1)}, bf16[128,896]{1,0:T(8,128)(2,1)}, u32[]{:S(2)}, u32[]{:S(2)}) collective-permute-start(bf16[128,896]{1,0:T(8,128)(2,1)} %slice.69), channel_id=1, source_target_pairs={{0,192},{64,0},{128,64},{192,128},{1,193},{65,1},{129,65},{193,129... | collective-permute-start | bytes 688136 | tf_op jit(solution)/shard_map/ppermute | solution.py:38
  43.5 14.0 %collective-permute-done.4 = bf16[256,896]{1,0:T(8,128)(2,1)S(1)} collective-permute-done((bf16[256,896]{1,0:T(8,128)(2,1)S(1)}, bf16[256,896]{1,0:T(8,128)(2,1)S(1)}, u32[]{:S(2)}, u32[]{:S(2)}) %collective-permute-start.4) | collective-permute-done | bytes 458784 | tf_op jit(solution)/shard_map/ppermute | solution.py:38
  57.6 0.8 slice.68
  58.4 2.2 collective-permute-start.5
  60.8 1.5 collective-permute-start.3
  62.3 0.9 constant_dynamic-slice_fusion.1
  63.2 0.7 collective-permute-start.16
  63.9 4.2 %collective-permute-done.5 = bf16[128,896]{1,0:T(8,128)(2,1)} collective-permute-done((bf16[128,896]{1,0:T(8,128)(2,1)}, bf16[128,896]{1,0:T(8,128)(2,1)}, u32[]{:S(2)}, u32[]{:S(2)}) %collective-permute-start.5) | collective-permute-done | bytes 229408 | tf_op jit(solution)/shard_map/ppermute | solution.py:38
  68.2 1.1 maximum_bitcast_fusion
  69.3 1.3 pad_maximum_fusion.wa_ref
  70.6 1.2 collective-permute-start.8
  71.7 1.5 fusion.4
  73.3 2.7 %collective-permute-start.10 = (bf16[4,128,896]{2,1,0:T(8,128)(2,1)}, bf16[4,128,896]{2,1,0:T(8,128)(2,1)}, u32[]{:S(2)}, u32[]{:S(2)}) collective-permute-start(bf16[4,128,896]{2,1,0:T(8,128)(2,1)} %get-tuple-element.41), channel_id=1, source_target_pairs={{0,34},{32,0},{2,32},{34,2},{1,35},{33,1},{3,33},{35,3},{4,38},{36... | collective-permute-start | bytes 2752520 | tf_op jit(solution)/shard_map/ppermute | solution.py:43
  75.9 0.6 pad_add_fusion.at_ref
  76.6 2.0 pad_maximum_fusion.2.m0_ref
  78.6 6.8 %shard_map.101 = (bf16[4,512,512]{2,1,0:T(8,128)(2,1)}, bf16[4,512,512]{2,1,0:T(8,128)(2,1)}, f32[4,256,512]{2,1,0:T(8,128)}, f32[4,8,512]{2,1,0:T(8,128)}) custom-call(s32[4]{0:T(128)} %pad_add_fusion.at_ref, bf16[256,2048]{1,0:T(8,128)(2,1)} %bitcast.47, bf16[256,1024]{1,0:T(8,128)(2,1)} %bitcast.53, bf16[256,1024]{1,0:T(8,128)(2,1)} %bitcast.56, ...), custom_call_target="tpu_custom_call" | custom-call | flops 1073741824 | bytes 9437184 | tf_op jit(solution)/shard_map/pallas_call | solution.py:238
  85.5 1.0 copy-done.2
  86.5 5.9 %shard_map.102 = (bf16[4,256,512]{2,1,0:T(8,128)(2,1)}, bf16[4,256,512]{2,1,0:T(8,128)(2,1)}, bf16[2048,256]{1,0:T(8,128)(2,1)}, f32[4,8,512]{2,1,0:T(8,128)}) custom-call(s32[4]{0:T(128)} %pad_add_fusion.at_ref, bf16[256,2048]{1,0:T(8,128)(2,1)} %bitcast.48, bf16[512,1024]{1,0:T(8,128)(2,1)} %copy-done.2, f32[4,256,512]{2,1,0:T(8,128)} %get-tuple-element.23.acc_ref, ...), custom_call_target="tpu_custom_call" | custom-call | flops 536870912 | bytes 7340032 | tf_op jit(solution)/shard_map/pallas_call | solution.py:249
  92.4 8.8 %all-to-all-start.1 = ((bf16[4,512,256]{2,1,0:T(8,128)(2,1)}), bf16[4,512,256]{2,1,0:T(8,128)(2,1)S(1)}, u32[]{:S(2)}, u32[]{:S(2)}) async-start(bf16[4,512,256]{2,1,0:T(8,128)(2,1)} %bitcast.51), calls=%async_computation.1 | async-start | bytes 2097152 | tf_op jit(solution)/shard_map/all_to_all | solution.py:346
  101.1 3.0 %collective-permute-start = (f32[1]{0:T(128)}, f32[1]{0:T(128)}, u32[]{:S(2)}, u32[]{:S(2)}) collective-permute-start(f32[1]{0:T(128)} %bitcast.1), channel_id=1, source_target_pairs={{0,1},{1,0},{2,3},{3,2},{4,5},{5,4},{6,7},{7,6},{8,9},{9,8},{10,11... | collective-permute-start | bytes 20 | tf_op jit(solution)/shard_map/ppermute | solution.py:47
  104.1 3.0 %collective-permute-start.18 = (bf16[512,896]{1,0:T(8,128)(2,1)}, bf16[512,896]{1,0:T(8,128)(2,1)}, u32[]{:S(2)}, u32[]{:S(2)}) collective-permute-start(bf16[512,896]{1,0:T(8,128)(2,1)} %pad_maximum_fusion.2.m0_ref), channel_id=1, source_target_pairs={{0,192},{64,0},{128,64},{192,128},{1,193},{65,1},{129,65},{193,129... | collective-permute-start | bytes 2752520 | tf_op jit(solution)/shard_map/ppermute | solution.py:38
  107.7 3.4 %collective-permute-done.10.wbh_ref = bf16[4,128,896]{2,1,0:T(8,128)(2,1)} collective-permute-done((bf16[4,128,896]{2,1,0:T(8,128)(2,1)}, bf16[4,128,896]{2,1,0:T(8,128)(2,1)}, u32[]{:S(2)}, u32[]{:S(2)}) %collective-permute-start.10) | collective-permute-done | bytes 917536 | tf_op jit(solution)/shard_map/ppermute | solution.py:43
  111.5 12.1 %all-to-all-done.1.a_own_ref = bf16[4,512,256]{2,1,0:T(8,128)(2,1)S(1)} async-done(((bf16[4,512,256]{2,1,0:T(8,128)(2,1)}), bf16[4,512,256]{2,1,0:T(8,128)(2,1)S(1)}, u32[]{:S(2)}, u32[]{:S(2)}) %all-to-all-start.1) | async-done | bytes 1048608 | tf_op jit(solution)/shard_map/all_to_all | solution.py:346
  124.6 1.1 slice.74
  125.7 6.9 %collective-permute-done.18.m3_ref = bf16[512,896]{1,0:T(8,128)(2,1)} collective-permute-done((bf16[512,896]{1,0:T(8,128)(2,1)}, bf16[512,896]{1,0:T(8,128)(2,1)}, u32[]{:S(2)}, u32[]{:S(2)}) %collective-permute-start.18) | collective-permute-done | bytes 917536 | tf_op jit(solution)/shard_map/ppermute | solution.py:38
  132.6 3.2 %collective-permute-start.1 = (f32[1]{0:T(128)}, f32[1]{0:T(128)}, u32[]{:S(2)}, u32[]{:S(2)}) collective-permute-start(f32[1]{0:T(128)} %add.53), channel_id=1, source_target_pairs={{0,2},{2,0},{1,3},{3,1},{4,6},{6,4},{5,7},{7,5},{8,10},{10,8},{9,1... | collective-permute-start | bytes 20 | tf_op jit(solution)/shard_map/ppermute | solution.py:47
  135.7 1.9 slice.75
  137.6 1.6 collective-permute-start.19
  139.2 1.7 collective-permute-start.20
  141.6 12.0 %shard_map.103 = (bf16[512,1024]{1,0:T(8,128)(2,1)}, bf16[4,256,512]{2,1,0:T(8,128)(2,1)}, f32[4,8,512]{2,1,0:T(8,128)}, f32[4,256,512]{2,1,0:T(8,128)}) custom-call(s32[4]{0:T(128)} %pad_add_fusion.at_ref, f32[1]{0:T(128)S(6)} %div.6.scale_ref, bf16[256,2048]{1,0:T(8,128)(2,1)} %bitcast.49, bf16[512,1024]{1,0:T(8,128)(2,1)} %copy-done.2, ...), custom_call_target="tpu_custom_call" | custom-call | flops 2952790016 | bytes 16777216 | tf_op jit(solution)/shard_map/pallas_call | solution.py:262
  153.7 1.3 collective-permute-start.13
  155.0 0.7 copy-done.13
  155.8 5.9 %weight_product.1 = bf16[4,128,896]{2,1,0:T(8,128)(2,1)} custom-call(s32[4]{0:T(128)} %pad_add_fusion.at_ref, bf16[4,512,256]{2,1,0:T(8,128)(2,1)} %copy-done.7, bf16[4,512,256]{2,1,0:T(8,128)(2,1)} %bitcast.20.a_oth_ref, bf16[512,896]{1,0:T(8,128)(2,1)} %pad_maximum_fusion.2.m0_ref, bf16[512,896]{1,0:T(8,128)(2,1)} %collective-permute-done.17.m1_ref, ...), custom_call_target="tpu_custom_call" | custom-call | flops 1879048192 | bytes 7340032 | tf_op jit(solution)/shard_map/weight_product/pallas_call | solution.py:286
  161.7 1.2 slice_bitcast_fusion.4
  163.0 1.5 collective-permute-start.22
  164.4 0.8 collective-permute-start.21
  165.2 8.2 %shard_map.104 = (bf16[256,2048]{1,0:T(8,128)(2,1)}, f32[512,1024]{1,0:T(8,128)}, bf16[512,1024]{1,0:T(8,128)(2,1)}, f32[32,128]{1,0:T(8,128)}) custom-call(f32[1]{0:T(128)S(6)} %div.6.scale_ref, bf16[256,2048]{1,0:T(8,128)(2,1)} %bitcast.50, bf16[256,1024]{1,0:T(8,128)(2,1)} %bitcast.54, bf16[256,1024]{1,0:T(8,128)(2,1)} %bitcast.57, ...), custom_call_target="tpu_custom_call" | custom-call | flops 2147483648 | bytes 14680064 | tf_op jit(solution)/shard_map/pallas_call | solution.py:273
  173.4 1.7 fusion.3
  175.2 10.8 %all-to-all-start.2 = ((bf16[8,16,896]{2,1,0:T(8,128)(2,1)}), bf16[8,16,896]{2,1,0:T(8,128)(2,1)S(1)}, u32[]{:S(2)}, u32[]{:S(2)}) async-start(bf16[8,16,896]{2,1,0:T(8,128)(2,1)} %bitcast.64), calls=%async_computation.2 | async-start | bytes 458752 | tf_op jit(solution)/shard_map/all_to_all | solution.py:371
  186.0 2.6 %add_convert_fusion = bf16[512,1024]{1,0:T(8,128)(2,1)} fusion(bf16[512,1024]{1,0:T(8,128)(2,1)S(1)} %collective-permute-done.13, bf16[512,1024]{1,0:T(8,128)(2,1)} %get-tuple-element.34), kind=kLoop, calls=%fused_computation.2 | loop fusion | flops 2097152 | bytes 3145728 | tf_op jit(solution)/shard_map/convert_element_type | solution.py:357
  188.6 1.3 collective-permute-start.14
  190.0 5.9 %all-to-all-done.2 = bf16[8,16,896]{2,1,0:T(8,128)(2,1)S(1)} async-done(((bf16[8,16,896]{2,1,0:T(8,128)(2,1)}), bf16[8,16,896]{2,1,0:T(8,128)(2,1)S(1)}, u32[]{:S(2)}, u32[]{:S(2)}) %all-to-all-start.2) | async-done | bytes 229408 | tf_op jit(solution)/shard_map/all_to_all | solution.py:371
  196.5 2.3 collective-permute-start.24
  198.8 1.3 slice_reduce_fusion
  200.1 1.6 collective-permute-start.25
  201.7 13.6 %collective-permute-done.14 = bf16[512,1024]{1,0:T(8,128)(2,1)S(1)} collective-permute-done((bf16[512,1024]{1,0:T(8,128)(2,1)}, bf16[512,1024]{1,0:T(8,128)(2,1)S(1)}, u32[]{:S(2)}, u32[]{:S(2)}) %collective-permute-start.14) | collective-permute-done | bytes 1048608 | tf_op jit(solution)/shard_map/ppermute | solution.py:33
  215.4 1.0 copy-done.6
  216.4 2.4 multiply_reduce_fusion
  221.3 10.2 %all-to-all-start.3 = ((f32[8,8,128]{2,1,0:T(8,128)}), f32[8,8,128]{2,1,0:T(8,128)S(1)}, u32[]{:S(2)}, u32[]{:S(2)}) async-start(f32[8,8,128]{2,1,0:T(8,128)} %broadcast_in_dim_broadcast_in_dim_broadcast_in_dim.6), calls=%async_computation.3 | async-start | bytes 65536 | tf_op jit(solution)/shard_map/all_to_all | solution.py:52
  231.5 0.7 maximum_select_fusion
  232.2 4.0 %all-to-all-done.3 = f32[8,8,128]{2,1,0:T(8,128)S(1)} async-done(((f32[8,8,128]{2,1,0:T(8,128)}), f32[8,8,128]{2,1,0:T(8,128)S(1)}, u32[]{:S(2)}, u32[]{:S(2)}) %all-to-all-start.3) | async-done | bytes 32800 | tf_op jit(solution)/shard_map/all_to_all | solution.py:52
  236.2 0.7 broadcast_in_dim_broadcast_in_dim_broadcast_in_dim.7
  236.9 11.1 %all-to-all-start.4 = ((f32[32,8,128]{2,1,0:T(8,128)}), f32[32,8,128]{2,1,0:T(8,128)S(1)}, u32[]{:S(2)}, u32[]{:S(2)}) async-start(f32[32,8,128]{2,1,0:T(8,128)} %broadcast_in_dim_broadcast_in_dim_broadcast_in_dim.7), calls=%async_computation.4 | async-start | bytes 262144 | tf_op jit(solution)/shard_map/all_to_all | solution.py:52
  248.0 1.0 slice_bitcast_fusion
  249.1 8.1 %all-to-all-done.4 = f32[32,8,128]{2,1,0:T(8,128)S(1)} async-done(((f32[32,8,128]{2,1,0:T(8,128)}), f32[32,8,128]{2,1,0:T(8,128)S(1)}, u32[]{:S(2)}, u32[]{:S(2)}) %all-to-all-start.4) | async-done | bytes 131104 | tf_op jit(solution)/shard_map/all_to_all | solution.py:52
  (62 shorter events, 3.3 us)
Async XLA Ops:
  0.6 0.9 copy-start
  2.3 58.3 %copy-start.12 = (bf16[1,256,1792]{2,1,0:T(8,128)(2,1)S(1)}, bf16[1,256,1792]{2,1,0:T(8,128)(2,1)}, u32[]{:S(2)}) copy-start(bf16[1,256,1792]{2,1,0:T(8,128)(2,1)} %param.9) | copy-start | bytes 2752516
  2.3 25.3 %all-to-all-start = ((bf16[8,32,896]{2,1,0:T(8,128)(2,1)}), bf16[8,32,896]{2,1,0:T(8,128)(2,1)S(1)}, u32[]{:S(2)}, u32[]{:S(2)}) async-start(bf16[8,32,896]{2,1,0:T(8,128)(2,1)} %broadcast_in_dim.30), calls=%async_computation | async-start | bytes 917504 | tf_op jit(solution)/shard_map/all_to_all | solution.py:52
  12.8 48.0 %collective-permute-start.2 = (bf16[512,1024]{1,0:T(8,128)(2,1)S(1)}, bf16[512,1024]{1,0:T(8,128)(2,1)}, u32[]{:S(2)}, u32[]{:S(2)}) collective-permute-start(bf16[512,1024]{1,0:T(8,128)(2,1)S(1)} %pad_maximum_fusion.1), channel_id=1, source_target_pairs={{0,4},{4,8},{8,12},{12,16},{16,20},{20,24},{24,28},{28,32},{32,36}... | collective-permute-start | bytes 3145736 | tf_op jit(solution)/shard_map/ppermute | solution.py:33
  27.6 35.6 %copy-start.5 = (bf16[8,32,896]{2,1,0:T(8,128)(2,1)}, bf16[8,32,896]{2,1,0:T(8,128)(2,1)S(1)}, u32[]{:S(2)}) copy-start(bf16[8,32,896]{2,1,0:T(8,128)(2,1)S(1)} %all-to-all-done) | copy-start | bytes 1376260
  27.6 11.6 %collective-permute-start.6 = (bf16[256,896]{1,0:T(8,128)(2,1)S(1)}, bf16[256,896]{1,0:T(8,128)(2,1)S(1)}, u32[]{:S(2)}, u32[]{:S(2)}) collective-permute-start(bf16[256,896]{1,0:T(8,128)(2,1)S(1)} %bitcast.58), channel_id=1, source_target_pairs={{0,192},{64,0},{128,64},{192,128},{1,193},{65,1},{129,65},{193,129... | collective-permute-start | bytes 1376264 | tf_op jit(solution)/shard_map/ppermute | solution.py:38
  30.3 27.2 %collective-permute-start.4 = (bf16[256,896]{1,0:T(8,128)(2,1)S(1)}, bf16[256,896]{1,0:T(8,128)(2,1)S(1)}, u32[]{:S(2)}, u32[]{:S(2)}) collective-permute-start(bf16[256,896]{1,0:T(8,128)(2,1)S(1)} %bitcast.59), channel_id=1, source_target_pairs={{0,64},{64,128},{128,192},{192,0},{1,65},{65,129},{129,193},{193,1... | collective-permute-start | bytes 1376264 | tf_op jit(solution)/shard_map/ppermute | solution.py:38
  39.3 19.1 %copy-start.8 = (bf16[256,896]{1,0:T(8,128)(2,1)}, bf16[256,896]{1,0:T(8,128)(2,1)S(1)}, u32[]{:S(2)}) copy-start(bf16[256,896]{1,0:T(8,128)(2,1)S(1)} %collective-permute-done.6) | copy-start | bytes 1376260
  40.0 23.9 %collective-permute-start.7 = (bf16[128,896]{1,0:T(8,128)(2,1)}, bf16[128,896]{1,0:T(8,128)(2,1)}, u32[]{:S(2)}, u32[]{:S(2)}) collective-permute-start(bf16[128,896]{1,0:T(8,128)(2,1)} %slice.69), channel_id=1, source_target_pairs={{0,192},{64,0},{128,64},{192,128},{1,193},{65,1},{129,65},{193,129... | collective-permute-start | bytes 688136 | tf_op jit(solution)/shard_map/ppermute | solution.py:38
  57.6 0.9 copy-start.10
  58.4 9.7 %collective-permute-start.5 = (bf16[128,896]{1,0:T(8,128)(2,1)}, bf16[128,896]{1,0:T(8,128)(2,1)}, u32[]{:S(2)}, u32[]{:S(2)}) collective-permute-start(bf16[128,896]{1,0:T(8,128)(2,1)} %slice.68), channel_id=1, source_target_pairs={{0,64},{64,128},{128,192},{192,0},{1,65},{65,129},{129,193},{193,1... | collective-permute-start | bytes 688136 | tf_op jit(solution)/shard_map/ppermute | solution.py:38
  60.8 8.5 %copy-start.9 = (bf16[256,896]{1,0:T(8,128)(2,1)S(1)}, bf16[256,896]{1,0:T(8,128)(2,1)}, u32[]{:S(2)}) copy-start(bf16[256,896]{1,0:T(8,128)(2,1)} %copy-done.8) | copy-start | bytes 1376260
  60.8 8.5 %copy-start.11 = (bf16[256,896]{1,0:T(8,128)(2,1)S(1)}, bf16[256,896]{1,0:T(8,128)(2,1)}, u32[]{:S(2)}) copy-start(bf16[256,896]{1,0:T(8,128)(2,1)} %copy-done.10) | copy-start | bytes 1376260
  60.8 24.7 %collective-permute-start.3 = (bf16[512,1024]{1,0:T(8,128)(2,1)}, bf16[512,1024]{1,0:T(8,128)(2,1)S(1)}, u32[]{:S(2)}, u32[]{:S(2)}) collective-permute-start(bf16[512,1024]{1,0:T(8,128)(2,1)} %collective-permute-done.2.h1_ref), channel_id=1, source_target_pairs={{0,4},{4,8},{8,12},{12,16},{16,20},{20,24},{24,28},{28,32},{32,36}... | collective-permute-start | bytes 3145736 | tf_op jit(solution)/shard_map/ppermute | solution.py:33
  63.2 13.4 %copy-start.3 = (bf16[256,896]{1,0:T(8,128)(2,1)}, bf16[256,896]{1,0:T(8,128)(2,1)S(1)}, u32[]{:S(2)}) copy-start(bf16[256,896]{1,0:T(8,128)(2,1)S(1)} %get-tuple-element.49.m_own_ref) | copy-start | bytes 1376260
  63.2 13.4 %collective-permute-start.16 = (bf16[256,896]{1,0:T(8,128)(2,1)}, bf16[256,896]{1,0:T(8,128)(2,1)}, u32[]{:S(2)}, u32[]{:S(2)}) collective-permute-start(bf16[256,896]{1,0:T(8,128)(2,1)} %get-tuple-element.48.m_oth_ref), channel_id=1, source_target_pairs={{0,1},{1,0},{2,3},{3,2},{4,5},{5,4},{6,7},{7,6},{8,9},{9,8},{10,11... | collective-permute-start | bytes 1376264 | tf_op jit(solution)/shard_map/ppermute | solution.py:47
  70.6 8.1 %copy-start.1 = (bf16[4,256,896]{2,1,0:T(8,128)(2,1)}, bf16[4,256,896]{2,1,0:T(8,128)(2,1)S(1)}, u32[]{:S(2)}) copy-start(bf16[4,256,896]{2,1,0:T(8,128)(2,1)S(1)} %pad_maximum_fusion.wa_ref) | copy-start | bytes 5505028
  70.6 68.6 %collective-permute-start.8 = (bf16[4,256,896]{2,1,0:T(8,128)(2,1)S(1)}, bf16[4,256,896]{2,1,0:T(8,128)(2,1)}, u32[]{:S(2)}, u32[]{:S(2)}) collective-permute-start(bf16[4,256,896]{2,1,0:T(8,128)(2,1)S(1)} %pad_maximum_fusion.wa_ref), channel_id=1, source_target_pairs={{0,1},{1,0},{2,3},{3,2},{4,5},{5,4},{6,7},{7,6},{8,9},{9,8},{10,11... | collective-permute-start | bytes 5505032 | tf_op jit(solution)/shard_map/ppermute | solution.py:47
  73.3 33.8 %collective-permute-start.9 = (bf16[4,128,896]{2,1,0:T(8,128)(2,1)}, bf16[4,128,896]{2,1,0:T(8,128)(2,1)}, u32[]{:S(2)}, u32[]{:S(2)}) collective-permute-start(bf16[4,128,896]{2,1,0:T(8,128)(2,1)} %get-tuple-element.42), channel_id=1, source_target_pairs={{0,32},{32,2},{2,34},{34,0},{1,33},{33,3},{3,35},{35,1},{4,36},{36... | collective-permute-start | bytes 2752520 | tf_op jit(solution)/shard_map/ppermute | solution.py:43
  73.3 37.8 %collective-permute-start.10 = (bf16[4,128,896]{2,1,0:T(8,128)(2,1)}, bf16[4,128,896]{2,1,0:T(8,128)(2,1)}, u32[]{:S(2)}, u32[]{:S(2)}) collective-permute-start(bf16[4,128,896]{2,1,0:T(8,128)(2,1)} %get-tuple-element.41), channel_id=1, source_target_pairs={{0,34},{32,0},{2,32},{34,2},{1,35},{33,1},{3,33},{35,3},{4,38},{36... | collective-permute-start | bytes 2752520 | tf_op jit(solution)/shard_map/ppermute | solution.py:43
  78.6 32.9 %collective-permute-start.17 = (bf16[512,896]{1,0:T(8,128)(2,1)}, bf16[512,896]{1,0:T(8,128)(2,1)}, u32[]{:S(2)}, u32[]{:S(2)}) collective-permute-start(bf16[512,896]{1,0:T(8,128)(2,1)} %pad_maximum_fusion.2.m0_ref), channel_id=1, source_target_pairs={{0,64},{64,128},{128,192},{192,0},{1,65},{65,129},{129,193},{193,1... | collective-permute-start | bytes 2752520 | tf_op jit(solution)/shard_map/ppermute | solution.py:38
  85.5 1.0 copy-start.2
  92.4 31.2 %all-to-all-start.1 = ((bf16[4,512,256]{2,1,0:T(8,128)(2,1)}), bf16[4,512,256]{2,1,0:T(8,128)(2,1)S(1)}, u32[]{:S(2)}, u32[]{:S(2)}) async-start(bf16[4,512,256]{2,1,0:T(8,128)(2,1)} %bitcast.51), calls=%async_computation.1 | async-start | bytes 2097152 | tf_op jit(solution)/shard_map/all_to_all | solution.py:346
  101.1 3.0 %collective-permute-start = (f32[1]{0:T(128)}, f32[1]{0:T(128)}, u32[]{:S(2)}, u32[]{:S(2)}) collective-permute-start(f32[1]{0:T(128)} %bitcast.1), channel_id=1, source_target_pairs={{0,1},{1,0},{2,3},{3,2},{4,5},{5,4},{6,7},{7,6},{8,9},{9,8},{10,11... | collective-permute-start | bytes 20 | tf_op jit(solution)/shard_map/ppermute | solution.py:47
  104.1 28.5 %collective-permute-start.18 = (bf16[512,896]{1,0:T(8,128)(2,1)}, bf16[512,896]{1,0:T(8,128)(2,1)}, u32[]{:S(2)}, u32[]{:S(2)}) collective-permute-start(bf16[512,896]{1,0:T(8,128)(2,1)} %pad_maximum_fusion.2.m0_ref), channel_id=1, source_target_pairs={{0,192},{64,0},{128,64},{192,128},{1,193},{65,1},{129,65},{193,129... | collective-permute-start | bytes 2752520 | tf_op jit(solution)/shard_map/ppermute | solution.py:38
  107.1 34.5 %collective-permute-start.11 = (bf16[4,128,896]{2,1,0:T(8,128)(2,1)}, bf16[4,128,896]{2,1,0:T(8,128)(2,1)}, u32[]{:S(2)}, u32[]{:S(2)}) collective-permute-start(bf16[4,128,896]{2,1,0:T(8,128)(2,1)} %collective-permute-done.9.wbl_ref), channel_id=1, source_target_pairs={{0,1},{1,0},{2,3},{3,2},{4,5},{5,4},{6,7},{7,6},{8,9},{9,8},{10,11... | collective-permute-start | bytes 2752520 | tf_op jit(solution)/shard_map/ppermute | solution.py:47
  111.1 30.6 %collective-permute-start.12 = (bf16[4,128,896]{2,1,0:T(8,128)(2,1)}, bf16[4,128,896]{2,1,0:T(8,128)(2,1)}, u32[]{:S(2)}, u32[]{:S(2)}) collective-permute-start(bf16[4,128,896]{2,1,0:T(8,128)(2,1)} %collective-permute-done.10.wbh_ref), channel_id=1, source_target_pairs={{0,1},{1,0},{2,3},{3,2},{4,5},{5,4},{6,7},{7,6},{8,9},{9,8},{10,11... | collective-permute-start | bytes 2752520 | tf_op jit(solution)/shard_map/ppermute | solution.py:47
  123.6 30.1 %copy-start.7 = (bf16[4,512,256]{2,1,0:T(8,128)(2,1)}, bf16[4,512,256]{2,1,0:T(8,128)(2,1)S(1)}, u32[]{:S(2)}) copy-start(bf16[4,512,256]{2,1,0:T(8,128)(2,1)S(1)} %all-to-all-done.1.a_own_ref) | copy-start | bytes 3145732
  123.6 31.4 %collective-permute-start.15 = (bf16[2048,256]{1,0:T(8,128)(2,1)S(1)}, bf16[2048,256]{1,0:T(8,128)(2,1)}, u32[]{:S(2)}, u32[]{:S(2)}) collective-permute-start(bf16[2048,256]{1,0:T(8,128)(2,1)S(1)} %bitcast.61), channel_id=1, source_target_pairs={{0,1},{1,0},{2,3},{3,2},{4,5},{5,4},{6,7},{7,6},{8,9},{9,8},{10,11... | collective-permute-start | bytes 3145736 | tf_op jit(solution)/shard_map/ppermute | solution.py:47
  132.6 5.0 %collective-permute-start.1 = (f32[1]{0:T(128)}, f32[1]{0:T(128)}, u32[]{:S(2)}, u32[]{:S(2)}) collective-permute-start(f32[1]{0:T(128)} %add.53), channel_id=1, source_target_pairs={{0,2},{2,0},{1,3},{3,1},{4,6},{6,4},{5,7},{7,5},{8,10},{10,8},{9,1... | collective-permute-start | bytes 20 | tf_op jit(solution)/shard_map/ppermute | solution.py:47
  137.6 17.4 %collective-permute-start.19 = (bf16[256,896]{1,0:T(8,128)(2,1)S(1)}, bf16[256,896]{1,0:T(8,128)(2,1)}, u32[]{:S(2)}, u32[]{:S(2)}) collective-permute-start(bf16[256,896]{1,0:T(8,128)(2,1)S(1)} %slice.74), channel_id=1, source_target_pairs={{0,64},{64,128},{128,192},{192,0},{1,65},{65,129},{129,193},{193,1... | collective-permute-start | bytes 1376264 | tf_op jit(solution)/shard_map/ppermute | solution.py:38
  139.2 15.8 %collective-permute-start.20 = (bf16[256,896]{1,0:T(8,128)(2,1)}, bf16[256,896]{1,0:T(8,128)(2,1)S(1)}, u32[]{:S(2)}, u32[]{:S(2)}) collective-permute-start(bf16[256,896]{1,0:T(8,128)(2,1)} %slice.75), channel_id=1, source_target_pairs={{0,192},{64,0},{128,64},{192,128},{1,193},{65,1},{129,65},{193,129... | collective-permute-start | bytes 1376264 | tf_op jit(solution)/shard_map/ppermute | solution.py:38
  153.7 32.3 %collective-permute-start.13 = (bf16[512,1024]{1,0:T(8,128)(2,1)}, bf16[512,1024]{1,0:T(8,128)(2,1)S(1)}, u32[]{:S(2)}, u32[]{:S(2)}) collective-permute-start(bf16[512,1024]{1,0:T(8,128)(2,1)} %get-tuple-element.35), channel_id=1, source_target_pairs={{4,0},{8,4},{12,8},{16,12},{20,16},{24,20},{28,24},{32,28},{36,32}... | collective-permute-start | bytes 3145736 | tf_op jit(solution)/shard_map/ppermute | solution.py:33
  155.0 0.8 copy-start.13
  162.9 10.5 %collective-permute-start.23 = (bf16[128,896]{1,0:T(8,128)(2,1)S(1)}, bf16[128,896]{1,0:T(8,128)(2,1)S(1)}, u32[]{:S(2)}, u32[]{:S(2)}) collective-permute-start(bf16[128,896]{1,0:T(8,128)(2,1)S(1)} %get-tuple-element.46), channel_id=1, source_target_pairs={{0,34},{32,0},{2,32},{34,2},{1,35},{33,1},{3,33},{35,3},{4,38},{36... | collective-permute-start | bytes 688136 | tf_op jit(solution)/shard_map/ppermute | solution.py:43
  163.0 10.4 %collective-permute-start.22 = (bf16[128,896]{1,0:T(8,128)(2,1)S(1)}, bf16[128,896]{1,0:T(8,128)(2,1)S(1)}, u32[]{:S(2)}, u32[]{:S(2)}) collective-permute-start(bf16[128,896]{1,0:T(8,128)(2,1)S(1)} %get-tuple-element.47), channel_id=1, source_target_pairs={{0,2},{32,34},{2,0},{34,32},{1,3},{33,35},{3,1},{35,33},{4,6},{36,... | collective-permute-start | bytes 688136 | tf_op jit(solution)/shard_map/ppermute | solution.py:43
  164.4 9.0 %collective-permute-start.21 = (bf16[128,896]{1,0:T(8,128)(2,1)S(1)}, bf16[128,896]{1,0:T(8,128)(2,1)S(1)}, u32[]{:S(2)}, u32[]{:S(2)}) collective-permute-start(bf16[128,896]{1,0:T(8,128)(2,1)S(1)} %get-tuple-element.45), channel_id=1, source_target_pairs={{0,32},{32,2},{2,34},{34,0},{1,33},{33,3},{3,35},{35,1},{4,36},{36... | collective-permute-start | bytes 688136 | tf_op jit(solution)/shard_map/ppermute | solution.py:43
  175.2 41.2 %copy-start.4 = (f32[512,1024]{1,0:T(8,128)S(1)}, f32[512,1024]{1,0:T(8,128)}, u32[]{:S(2)}) copy-start(f32[512,1024]{1,0:T(8,128)} %get-tuple-element.33) | copy-start | bytes 6291460
  175.2 20.7 %all-to-all-start.2 = ((bf16[8,16,896]{2,1,0:T(8,128)(2,1)}), bf16[8,16,896]{2,1,0:T(8,128)(2,1)S(1)}, u32[]{:S(2)}, u32[]{:S(2)}) async-start(bf16[8,16,896]{2,1,0:T(8,128)(2,1)} %bitcast.64), calls=%async_computation.2 | async-start | bytes 458752 | tf_op jit(solution)/shard_map/all_to_all | solution.py:371
  188.6 26.7 %collective-permute-start.14 = (bf16[512,1024]{1,0:T(8,128)(2,1)}, bf16[512,1024]{1,0:T(8,128)(2,1)S(1)}, u32[]{:S(2)}, u32[]{:S(2)}) collective-permute-start(bf16[512,1024]{1,0:T(8,128)(2,1)} %add_convert_fusion), channel_id=1, source_target_pairs={{4,0},{8,4},{12,8},{16,12},{20,16},{24,20},{28,24},{32,28},{36,32}... | collective-permute-start | bytes 3145736 | tf_op jit(solution)/shard_map/ppermute | solution.py:33
  196.5 3.6 %collective-permute-start.24 = (f32[16,896]{1,0:T(8,128)S(1)}, f32[16,896]{1,0:T(8,128)S(1)}, u32[]{:S(2)}, u32[]{:S(2)}) collective-permute-start(f32[16,896]{1,0:T(8,128)S(1)} %get-tuple-element.38), channel_id=1, source_target_pairs={{0,1},{1,0},{2,3},{3,2},{4,5},{5,4},{6,7},{7,6},{8,9},{9,8},{10,11... | collective-permute-start | bytes 172040 | tf_op jit(solution)/shard_map/ppermute | solution.py:47
  200.1 31.4 %collective-permute-start.25 = (f32[16,1792]{1,0:T(8,128)S(1)}, f32[16,1792]{1,0:T(8,128)S(1)}, u32[]{:S(2)}, u32[]{:S(2)}) collective-permute-start(f32[16,1792]{1,0:T(8,128)S(1)} %maximum_select_fusion.1), channel_id=1, source_target_pairs={{0,2},{2,0},{1,3},{3,1},{4,6},{6,4},{5,7},{7,5},{8,10},{10,8},{9,1... | collective-permute-start | bytes 344072 | tf_op jit(solution)/shard_map/ppermute | solution.py:47
  215.4 1.0 copy-start.6
  221.3 14.9 %all-to-all-start.3 = ((f32[8,8,128]{2,1,0:T(8,128)}), f32[8,8,128]{2,1,0:T(8,128)S(1)}, u32[]{:S(2)}, u32[]{:S(2)}) async-start(f32[8,8,128]{2,1,0:T(8,128)} %broadcast_in_dim_broadcast_in_dim_broadcast_in_dim.6), calls=%async_computation.3 | async-start | bytes 65536 | tf_op jit(solution)/shard_map/all_to_all | solution.py:52
  236.9 20.3 %all-to-all-start.4 = ((f32[32,8,128]{2,1,0:T(8,128)}), f32[32,8,128]{2,1,0:T(8,128)S(1)}, u32[]{:S(2)}, u32[]{:S(2)}) async-start(f32[32,8,128]{2,1,0:T(8,128)} %broadcast_in_dim_broadcast_in_dim_broadcast_in_dim.7), calls=%async_computation.4 | async-start | bytes 262144 | tf_op jit(solution)/shard_map/all_to_all | solution.py:52
where the time goes:
time: 260 us; the launch traced here: 258 us
  starting transfers between devices  91.6 us (35%)
  waiting for transfers between devices  91 us (35%)
  Pallas kernels  38.9 us (15%)
  other arithmetic  16 us (6%)
  local copies, waits for them, and re-layouts  15 us (6%)
  between operations  6.07 us (2%)
    ppermute x8, waiting for transfers between devices, ring(): lax.ppermute(value, axis, [(s, (s + steps) % count) for s in range(count)])  33.4 us
    all_to_all x3, starting transfers between devices, for_each(): lax.all_to_all(jnp.broadcast_to(value[None], (size, *value.shape)), axis,...  30.4 us
    all_to_all x3, waiting for transfers between devices, for_each(): lax.all_to_all(jnp.broadcast_to(value[None], (size, *value.shape)), axis,...  22.6 us
    ppermute x8, starting transfers between devices, ring(): lax.ppermute(value, axis, [(s, (s + steps) % count) for s in range(count)])  14.7 us
    ppermute x4, waiting for transfers between devices, shifted(): lax.ppermute(value, SEQ, [(source, source + steps) for source in range(in...  13.6 us
    ppermute x9, starting transfers between devices, swap(): return lax.ppermute(value, axis, [(0, 1), (1, 0)])  13.5 us
    all_to_all x1, waiting for transfers between devices, all_steps(): a_own = lax.all_to_all(attn, 'seq_0', 0, 0, tiled=True)  12.1 us
    pallas_call x1, Pallas kernels, far_backward(): call(far_grad_kernel, 2, [HEAD_COLS, BOTH_COLS, of_head(TOK_DEV), of_head...  12 us
  transfers between devices with their start and end apart: 31, of which 11 were waited for; matrix products, arithmetic and copies ran while one was open for 10% of the time, Pallas kernels for 15%

commit v1 on v0

--- a/solution.py
+++ b/solution.py
@@ -41,6 +41,20 @@
 def ring_x(value, steps):
     at = lambda x: (x % 2) * 2 + x // 2
     return lax.ppermute(value, X_AXES, [(at(s), at((s + steps) % 4)) for s in range(4)])
+
+
+def across_x(value, steps):
+    pairs = []
+    depth = lax.axis_size("seq_2")
+    for low in range(2):
+        for z in range(depth):
+            for high in range(2):
+                step = steps if z else (1 if low else -1)
+                to = (2 * high + low + step) % 4
+                pairs.append(
+                    ((low * depth + z) * 2 + high, ((to % 2) * depth + z) * 2 + to // 2)
+                )
+    return lax.ppermute(value, ("seq_1", "seq_2", "dp_0"), pairs)
 
 
 def swap(value, axis):
@@ -113,62 +127,56 @@
     inv_ref[0] = jnp.broadcast_to(inverse, inv_ref.shape[1:])
     out = ((acc_ref[0] + dot(h2_ref[TOK_DEV:], p, TN)) * inverse).astype(BF16)
     for h in range(GROUP):
-        attn_ref[h * HEAD_DIM : (h + 1) * HEAD_DIM, :] = out[:, h * TOK_DEV : (h + 1) * TOK_DEV]
-
-
-def terms(k, v, q, p, pf, g, delta):
-    dscore = (pf.astype(F32) * (dot(v, g, NN) - delta)).astype(BF16)
-    return dot(k, dscore, TN), dot(dscore, q, NN), dot(p, g, NT)
+        attn_ref[0, h * HEAD_DIM : (h + 1) * HEAD_DIM, :] = out[:, h * TOK_DEV : (h + 1) * TOK_DEV]
+
+
+def score_terms(v, g, delta, pf):
+    return (pf.astype(F32) * (dot(v, g, NN) - delta)).astype(BF16)
 
 
 def far_grad_kernel(
     at_ref, scale_ref, q_ref, h2_ref, p_ref, pf_ref, inv_ref, attn_ref, m_own_ref, m_oth_ref,
     wa_ref, wc_ref, wbl_ref, wbh_ref, wdl_ref, wdh_ref,
-    d2_ref, g_ref, delta_ref, dq_ref, raw_ref,
+    d2_ref, g_ref, delta_ref, ds_ref, raw_ref,
 ):
     act_scale = scale_ref[0]
     own = pl.multiple_of(at_ref[2] * TOK_DEV, TOK_DEV)
     oth = pl.multiple_of((1 - at_ref[2]) * TOK_DEV, TOK_DEV)
-    m_own = m_own_ref[...]
-    m_oth = m_oth_ref[...]
-    half = HEAD_DIM // 2
-    raw_ref[:, pl.ds(own, TOK_DEV)] = dot(wa_ref[0], m_own, NT) + dot(wc_ref[0], m_oth, NT)
-    raw_ref[:half, pl.ds(oth, TOK_DEV)] = dot(wbl_ref[0], m_own, NT) + dot(wdl_ref[0], m_oth, NT)
-    raw_ref[half:, pl.ds(oth, TOK_DEV)] = dot(wbh_ref[0], m_own, NT) + dot(wdh_ref[0], m_oth, NT)
+    both = dot(
+        jnp.concatenate([wa_ref[0], wbl_ref[0], wbh_ref[0]], 0), m_own_ref[...], NT
+    ) + dot(jnp.concatenate([wc_ref[0], wdl_ref[0], wdh_ref[0]], 0), m_oth_ref[...], NT)
+    raw_ref[:, pl.ds(own, TOK_DEV)] = both[:HEAD_DIM]
+    raw_ref[:, pl.ds(oth, TOK_DEV)] = both[HEAD_DIM:]
     g = (raw_ref[...] * inv_ref[0, :1]).astype(BF16)
     g_ref[0] = g
     attn = jnp.concatenate(
-        [attn_ref[h * HEAD_DIM : (h + 1) * HEAD_DIM, :] for h in range(GROUP)], 1
+        [attn_ref[0, h * HEAD_DIM : (h + 1) * HEAD_DIM, :] for h in range(GROUP)], 1
     )
     delta = row_sum(g.astype(F32) * attn.astype(F32))
     delta_ref[0] = jnp.broadcast_to(delta, delta_ref.shape[1:])
-    dq, dk, dv = terms(
-        h2_ref[:TOK_DEV], h2_ref[TOK_DEV:], two_heads(q_ref), p_ref[0], pf_ref[0], g, delta
-    )
-    dq_ref[0] = dq
-    d2_ref[:TOK_DEV] = (dk * (SCALE * act_scale)).astype(BF16)
-    d2_ref[TOK_DEV:] = (dv * act_scale).astype(BF16)
+    dscore = score_terms(h2_ref[TOK_DEV:], g, delta, pf_ref[0])
+    ds_ref[0] = dscore
+    d2_ref[:TOK_DEV] = (dot(dscore, two_heads(q_ref), NN) * (SCALE * act_scale)).astype(BF16)
+    d2_ref[TOK_DEV:] = (dot(p_ref[0], g, NT) * act_scale).astype(BF16)
 
 
 def near_grad_kernel(
-    scale_ref, q_ref, k0_ref, v0_ref, h1_ref, p_ref, pf_ref, g_ref, delta_ref, far_ref,
+    scale_ref, q_ref, k0_ref, v0_ref, h1_ref, h2_ref, p_ref, pf_ref, g_ref, delta_ref, ds_ref,
     dq_ref, d0_ref, d1_ref, sq_ref,
 ):
     act_scale = scale_ref[0]
     q = two_heads(q_ref)
     g = g_ref[0]
     delta = delta_ref[0, :1]
-    dq = far_ref[0]
+    dq = dot(h2_ref[...], ds_ref[0], TN)
     for k, v, at, out in (
         (h1_ref[:TOK_DEV], h1_ref[TOK_DEV:], 0, d1_ref),
         (k0_ref[...], v0_ref[...], TOK_DEV, d0_ref),
     ):
-        piece, dk, dv = terms(
-            k, v, q, p_ref[0, at : at + TOK_DEV], pf_ref[0, at : at + TOK_DEV], g, delta
-        )
-        dq = dq + piece
-        out[:TOK_DEV] = (dk * (SCALE * act_scale)).astype(out.dtype)
-        out[TOK_DEV:] = (dv * act_scale).astype(out.dtype)
+        dscore = score_terms(v, g, delta, pf_ref[0, at : at + TOK_DEV])
+        dq = dq + dot(k, dscore, TN)
+        out[:TOK_DEV] = (dot(dscore, q, NN) * (SCALE * act_scale)).astype(out.dtype)
+        out[TOK_DEV:] = (dot(p_ref[0, at : at + TOK_DEV], g, NT) * act_scale).astype(out.dtype)
     dq = dq * (SCALE * act_scale)
     sq_ref[...] = jnp.broadcast_to(jnp.sum(dq * dq), sq_ref.shape)
     for h in range(GROUP):
@@ -187,8 +195,7 @@
             (m3_ref[:TOK_DEV], m3_ref[TOK_DEV:]),
         )
     ):
-        place = (at_ref[1] + 4 - back) % 4
-        both = dot(a_own_ref[place], own, NN) + dot(a_oth_ref[place], oth, NN)
+        both = dot(a_own_ref[back], own, NN) + dot(a_oth_ref[back], oth, NN)
         acc = both if acc is None else acc + both
     acc = acc.reshape(2, 8, 2, 16, HALF)
     for low in range(2):
@@ -202,7 +209,7 @@
 HEAD_COLS = pl.BlockSpec((TOK_DEV, GROUP * D), lambda h, *_: (0, h))
 KV_COLS = pl.BlockSpec((TOK_DEV, D), lambda h, *_: (0, h))
 BOTH_COLS = pl.BlockSpec((2 * TOK_DEV, D), lambda h, *_: (0, h))
-ATTN_ROWS = pl.BlockSpec((GROUP * D, TOK_DEV), lambda h, *_: (h, 0))
+ATTN_ROWS = pl.BlockSpec((1, GROUP * D, TOK_DEV), lambda h, at, *_: ((h + 4 - at[1]) % 4, 0, 0))
 
 
 def of_head(rows, columns=SCORES):
@@ -251,7 +258,7 @@
         [HEAD_COLS, BOTH_COLS, of_head(D), of_head(8)],
         [of_head(TOK_DEV), of_head(TOK_DEV), ATTN_ROWS, of_head(8)],
         [per_head(TOK_DEV, BF16), per_head(TOK_DEV, BF16),
-         jax.ShapeDtypeStruct((WIDTH, TOK_DEV), BF16), per_head(8, F32)],
+         jax.ShapeDtypeStruct((KV_HEADS, GROUP * D, TOK_DEV), BF16), per_head(8, F32)],
         2, 7,
     )(where, q, h2, acc, tot)
 
@@ -263,22 +270,22 @@
         far_grad_kernel, 2,
         [HEAD_COLS, BOTH_COLS, of_head(TOK_DEV), of_head(TOK_DEV), of_head(8), ATTN_ROWS, full,
          full, rel(D), rel(D)] + [rel(D // 2)] * 4,
-        [BOTH_COLS, of_head(D), of_head(8), of_head(D)],
-        [flat(2 * TOK_DEV, BF16), per_head(D, BF16), per_head(8, F32), per_head(D, F32)],
-        4 + 7, 16, [pltpu.VMEM((D, SCORES), F32)],
+        [BOTH_COLS, of_head(D), of_head(8), of_head(TOK_DEV)],
+        [flat(2 * TOK_DEV, BF16), per_head(D, BF16), per_head(8, F32), per_head(TOK_DEV, BF16)],
+        3 + 7, 15, [pltpu.VMEM((D, SCORES), F32)],
     )(where, scale, q, h2, p, pf, inv, attn, m_own, m_oth, *weights)
 
 
-def near_backward(scale, q, k, v, h1, p, pf, g, delta, far):
+def near_backward(scale, q, k, v, h1, h2, p, pf, g, delta, dscore):
     return call(
         near_grad_kernel, 1,
-        [HEAD_COLS, KV_COLS, KV_COLS, BOTH_COLS, of_head(2 * TOK_DEV), of_head(2 * TOK_DEV),
-         of_head(D), of_head(8), of_head(D)],
+        [HEAD_COLS, KV_COLS, KV_COLS, BOTH_COLS, KV_COLS, of_head(2 * TOK_DEV),
+         of_head(2 * TOK_DEV), of_head(D), of_head(8), of_head(TOK_DEV)],
         [HEAD_COLS, BOTH_COLS, BOTH_COLS, pl.BlockSpec((8, 128), lambda h, *_: (h, 0))],
         [jax.ShapeDtypeStruct((TOK_DEV, WIDTH), BF16), flat(2 * TOK_DEV, F32),
          flat(2 * TOK_DEV, BF16), jax.ShapeDtypeStruct((8 * KV_HEADS, 128), F32)],
-        8, 14,
-    )(scale, q, k, v, h1, p, pf, g, delta, far)
+        9, 13,
+    )(scale, q, k, v, h1, h2, p, pf, g, delta, dscore)
 
 
 def weight_product(where, a_own, a_oth, m0, m1, m3, m2a, m2b):
@@ -335,24 +342,26 @@
     mid = HEAD_DIM // 2
     w_far = [ring(w_up[:mid], "seq_0", 1), ring(w_down[mid:], "seq_0", -1)]
     wa = jnp.stack([w_z, w_up, jnp.concatenate(w_far, 0), w_down])
-    wbl = ring_x(wa[:, :mid], 1)
-    wbh = ring_x(wa[:, mid:], -1)
+    wbl = across_x(wa[:, :mid], 1)
+    wbh = across_x(wa[:, mid:], -1)
     wc = swap(wa, "dp_1")
     wdl = swap(wbl, "dp_1")
     wdh = swap(wbh, "dp_1")
 
     p, pf, acc, tot = near_forward(where, q_rows, k_rows, v_rows, h1)
     p2, pf2, attn, inv = far_forward(where, q_rows, h2, acc, tot)
-    a_own = lax.all_to_all(attn, "seq_0", 0, 0, tiled=True)
+    a_own = jnp.stack([
+        attn[0], ring(attn[1], "seq_0", 1), ring(attn[2], "seq_0", 2), ring(attn[3], "seq_0", -1)
+    ])
     a_oth = swap(a_own, "dp_1")
 
-    d2, g, delta, far = far_backward(
+    d2, g, delta, dscore = far_backward(
         where, act_scale, q_rows, h2, p2, pf2, inv, attn, m_own, m_oth,
         (wa, wc, wbl, wbh, wdl, wdh),
     )
     r1 = shifted(d2, -1)
     dq, d0, d1, dq_sq = near_backward(
-        act_scale, q_rows, k_rows, v_rows, h1, p, pf, g, delta, far
+        act_scale, q_rows, k_rows, v_rows, h1, h2, p, pf, g, delta, dscore
     )
     r2 = shifted((d1.astype(F32) + r1.astype(F32)).astype(BF16), -1)
     dkv = d0 + r2.astype(F32)
@@ -360,7 +369,7 @@
     dkv = dkv.astype(BF16)
 
     part = weight_product(
-        where, a_own.reshape(4, 512, TOK_DEV), a_oth.reshape(4, 512, TOK_DEV), m0, m1, m3, m2a, m2b
+        where, a_own, a_oth, m0, m1, m3, m2a, m2b
     )
     part = (
         part[0].astype(F32)

time: 260 us -> 276 us (1.062)
  waiting for transfers between devices: 91 us -> 126 us
  starting transfers between devices: 91.6 us -> 73.5 us
    ppermute x8 -> x11, waiting for transfers between devices: 33.4 us -> 73.2 us  [ring(): lax.ppermute(value, axis, [(s, (s + steps) % count) for s in range(count)])]
    all_to_all x3, waiting for transfers between devices: 22.6 us -> 38.5 us  [for_each(): lax.all_to_all(jnp.broadcast_to(value[None], (size, *value.shape)), axis,...]
    all_to_all x1 -> x0, waiting for transfers between devices: 12.1 us -> none  [all_steps(): a_own = lax.all_to_all(attn, 'seq_0', 0, 0, tiled=True)]
    all_to_all x3, starting transfers between devices: 30.4 us -> 21.2 us  [for_each(): lax.all_to_all(jnp.broadcast_to(value[None], (size, *value.shape)), axis,...]
    all_to_all x1 -> x0, starting transfers between devices: 8.77 us -> none  [all_steps(): a_own = lax.all_to_all(attn, 'seq_0', 0, 0, tiled=True)]
    all_to_all x1, starting transfers between devices: 10.8 us -> 3.53 us  [all_steps(): pieces = lax.all_to_all(part, 'seq_2', 0, 0, tiled=True)]
    ppermute x9, starting transfers between devices: 13.5 us -> 20 us  [swap(): return lax.ppermute(value, axis, [(0, 1), (1, 0)])]
    ppermute x4, waiting for transfers between devices: 13.6 us -> 9.02 us  [shifted(): lax.ppermute(value, SEQ, [(source, source + steps) for source in range(in...]
  transfers between devices with their start and end apart: 31 -> 33, of which waited for: 11 -> 12; matrix products, arithmetic and copies ran while one was open for 10% -> 10% of each run, Pallas kernels for 15% -> 14%
where the time goes in v1:
time: 276 us; the launch traced here: 275 us
  waiting for transfers between devices  126 us (46%)
  starting transfers between devices  73.5 us (27%)
  Pallas kernels  37.1 us (13%)
  other arithmetic  16.6 us (6%)
  local copies, waits for them, and re-layouts  15.1 us (5%)
  between operations  6.02 us (2%)
    ppermute x11, waiting for transfers between devices, ring(): lax.ppermute(value, axis, [(s, (s + steps) % count) for s in range(count)])  73.2 us
    all_to_all x3, waiting for transfers between devices, for_each(): lax.all_to_all(jnp.broadcast_to(value[None], (size, *value.shape)), axis,...  38.5 us
    all_to_all x3, starting transfers between devices, for_each(): lax.all_to_all(jnp.broadcast_to(value[None], (size, *value.shape)), axis,...  21.2 us
    ppermute x9, starting transfers between devices, swap(): return lax.ppermute(value, axis, [(0, 1), (1, 0)])  20 us
    ppermute x11, starting transfers between devices, ring(): lax.ppermute(value, axis, [(s, (s + steps) % count) for s in range(count)])  14.3 us
    pallas_call x1, Pallas kernels, far_backward(): call(far_grad_kernel, 2, [HEAD_COLS, BOTH_COLS, of_head(TOK_DEV), of_head...  10.4 us
    ppermute x4, starting transfers between devices, shifted(): lax.ppermute(value, SEQ, [(source, source + steps) for source in range(in...  9.28 us
    ppermute x4, waiting for transfers between devices, shifted(): lax.ppermute(value, SEQ, [(source, source + steps) for source in range(in...  9.02 us
  transfers between devices with their start and end apart: 33, of which 12 were waited for; matrix products, arithmetic and copies ran while one was open for 10% of the time, Pallas kernels for 14%

profile of v1, /device:TPU:1, one launch (start us, length us, event | category | flops | bytes accessed | tf_op | source)
XLA Modules:
  0.0 274.8 jit_solution(10893162942669751413)
XLA Ops:
  0.6 1.3 pad_maximum_fusion.1
  2.0 5.4 %collective-permute-start.2 = (bf16[512,1024]{1,0:T(8,128)(2,1)S(1)}, bf16[512,1024]{1,0:T(8,128)(2,1)}, u32[]{:S(2)}, u32[]{:S(2)}) collective-permute-start(bf16[512,1024]{1,0:T(8,128)(2,1)S(1)} %pad_maximum_fusion.1), channel_id=1, source_target_pairs={{0,4},{4,8},{8,12},{12,16},{16,20},{20,24},{24,28},{28,32},{32,36}... | collective-permute-start | bytes 3145736 | tf_op jit(solution)/shard_map/ppermute | solution.py:33
  7.3 0.8 broadcast_in_dim.30
  8.1 6.3 %all-to-all-start = ((bf16[8,32,896]{2,1,0:T(8,128)(2,1)}), bf16[8,32,896]{2,1,0:T(8,128)(2,1)S(1)}, u32[]{:S(2)}, u32[]{:S(2)}) async-start(bf16[8,32,896]{2,1,0:T(8,128)(2,1)} %broadcast_in_dim.30), calls=%async_computation | async-start | bytes 917504 | tf_op jit(solution)/shard_map/all_to_all | solution.py:66
  15.1 26.3 %all-to-all-done = bf16[8,32,896]{2,1,0:T(8,128)(2,1)S(1)} async-done(((bf16[8,32,896]{2,1,0:T(8,128)(2,1)}), bf16[8,32,896]{2,1,0:T(8,128)(2,1)S(1)}, u32[]{:S(2)}, u32[]{:S(2)}) %all-to-all-start) | async-done | bytes 458784 | tf_op jit(solution)/shard_map/all_to_all | solution.py:66
  41.5 2.7 collective-permute-start.6
  44.2 1.3 collective-permute-start.3
  45.6 1.3 bitcast_select_fusion
  46.9 4.6 %collective-permute-done.6 = bf16[256,896]{1,0:T(8,128)(2,1)S(1)} collective-permute-done((bf16[256,896]{1,0:T(8,128)(2,1)S(1)}, bf16[256,896]{1,0:T(8,128)(2,1)S(1)}, u32[]{:S(2)}, u32[]{:S(2)}) %collective-permute-start.6) | collective-permute-done | bytes 458784 | tf_op jit(solution)/shard_map/ppermute | solution.py:38
  51.5 0.8 slice.85
  52.3 3.4 %collective-permute-start.7 = (bf16[128,896]{1,0:T(8,128)(2,1)}, bf16[128,896]{1,0:T(8,128)(2,1)S(1)}, u32[]{:S(2)}, u32[]{:S(2)}) collective-permute-start(bf16[128,896]{1,0:T(8,128)(2,1)} %slice.85), channel_id=1, source_target_pairs={{0,192},{64,0},{128,64},{192,128},{1,193},{65,1},{129,65},{193,129... | collective-permute-start | bytes 688136 | tf_op jit(solution)/shard_map/ppermute | solution.py:38
  55.7 18.3 %collective-permute-done.4 = bf16[256,896]{1,0:T(8,128)(2,1)} collective-permute-done((bf16[256,896]{1,0:T(8,128)(2,1)S(1)}, bf16[256,896]{1,0:T(8,128)(2,1)}, u32[]{:S(2)}, u32[]{:S(2)}) %collective-permute-start.4) | collective-permute-done | bytes 458784 | tf_op jit(solution)/shard_map/ppermute | solution.py:38
  74.0 1.6 slice.84
  75.6 2.3 collective-permute-start.5
  77.9 0.9 constant_dynamic-slice_fusion.1
  78.8 3.7 %collective-permute-start.19 = (bf16[256,896]{1,0:T(8,128)(2,1)}, bf16[256,896]{1,0:T(8,128)(2,1)}, u32[]{:S(2)}, u32[]{:S(2)}) collective-permute-start(bf16[256,896]{1,0:T(8,128)(2,1)} %get-tuple-element.52.m_oth_ref), channel_id=1, source_target_pairs={{0,1},{1,0},{2,3},{3,2},{4,5},{5,4},{6,7},{7,6},{8,9},{9,8},{10,11... | collective-permute-start | bytes 1376264 | tf_op jit(solution)/shard_map/ppermute | solution.py:61
  83.1 6.8 %shard_map.101 = (bf16[4,512,512]{2,1,0:T(8,128)(2,1)}, bf16[4,512,512]{2,1,0:T(8,128)(2,1)}, f32[4,256,512]{2,1,0:T(8,128)}, f32[4,8,512]{2,1,0:T(8,128)}) custom-call(s32[4]{0:T(128)} %pad_add_fusion.at_ref, bf16[256,2048]{1,0:T(8,128)(2,1)} %bitcast.53, bf16[256,1024]{1,0:T(8,128)(2,1)} %bitcast.58, bf16[256,1024]{1,0:T(8,128)(2,1)} %bitcast.61, ...), custom_call_target="tpu_custom_call" | custom-call | flops 1073741824 | bytes 9437184 | tf_op jit(solution)/shard_map/pallas_call | solution.py:245
  90.0 1.6 pad_maximum_fusion.wa_ref
  91.7 1.8 fusion.4
  93.5 2.7 collective-permute-start.10
  96.2 1.0 copy-done.2
  97.2 5.9 %shard_map.102 = (bf16[4,256,512]{2,1,0:T(8,128)(2,1)}, bf16[4,256,512]{2,1,0:T(8,128)(2,1)}, bf16[4,512,256]{2,1,0:T(8,128)(2,1)}, f32[4,8,512]{2,1,0:T(8,128)}) custom-call(s32[4]{0:T(128)} %pad_add_fusion.at_ref, bf16[256,2048]{1,0:T(8,128)(2,1)} %bitcast.54, bf16[512,1024]{1,0:T(8,128)(2,1)} %copy-done.2, f32[4,256,512]{2,1,0:T(8,128)} %get-tuple-element.23.acc_ref, ...), custom_call_target="tpu_custom_call" | custom-call | flops 536870912 | bytes 7340032 | tf_op jit(solution)/shard_map/pallas_call | solution.py:256
  103.1 2.0 fusion.5
  105.4 1.9 collective-permute-start
  107.3 1.1 pad_maximum_fusion.3.m0_ref
  108.4 1.2 collective-permute-start.20
  109.6 2.8 %collective-permute-done.17 = bf16[512,256]{1,0:T(8,128)(2,1)S(1)} collective-permute-done((bf16[512,256]{1,0:T(8,128)(2,1)S(1)}, bf16[512,256]{1,0:T(8,128)(2,1)S(1)}, u32[]{:S(2)}, u32[]{:S(2)}) %collective-permute-start.17) | collective-permute-done | bytes 262176 | tf_op jit(solution)/shard_map/ppermute | solution.py:38
  112.3 1.6 collective-permute-start.16
  114.0 23.3 %collective-permute-done.16 = bf16[512,256]{1,0:T(8,128)(2,1)S(1)} collective-permute-done((bf16[512,256]{1,0:T(8,128)(2,1)S(1)}, bf16[512,256]{1,0:T(8,128)(2,1)S(1)}, u32[]{:S(2)}, u32[]{:S(2)}) %collective-permute-start.16) | collective-permute-done | bytes 262176 | tf_op jit(solution)/shard_map/ppermute | solution.py:38
  137.3 8.2 %collective-permute-done.15 = bf16[512,256]{1,0:T(8,128)(2,1)S(1)} collective-permute-done((bf16[512,256]{1,0:T(8,128)(2,1)S(1)}, bf16[512,256]{1,0:T(8,128)(2,1)S(1)}, u32[]{:S(2)}, u32[]{:S(2)}) %collective-permute-start.15) | collective-permute-done | bytes 262176 | tf_op jit(solution)/shard_map/ppermute | solution.py:38
  145.5 1.7 collective-permute-start.11
  147.3 1.2 pad_maximum_fusion.2.a_own_ref
  149.6 16.0 %collective-permute-done.21.m3_ref = bf16[512,896]{1,0:T(8,128)(2,1)S(1)} collective-permute-done((bf16[512,896]{1,0:T(8,128)(2,1)S(1)}, bf16[512,896]{1,0:T(8,128)(2,1)S(1)}, u32[]{:S(2)}, u32[]{:S(2)}) %collective-permute-start.21) | collective-permute-done | bytes 917536 | tf_op jit(solution)/shard_map/ppermute | solution.py:38
  165.7 2.3 collective-permute-start.1
  167.9 0.9 slice.91
  168.8 0.8 collective-permute-done.1
  169.6 2.7 collective-permute-start.23
  172.9 10.4 %shard_map.103 = (bf16[512,1024]{1,0:T(8,128)(2,1)}, bf16[4,256,512]{2,1,0:T(8,128)(2,1)}, f32[4,8,512]{2,1,0:T(8,128)}, bf16[4,256,512]{2,1,0:T(8,128)(2,1)}) custom-call(s32[4]{0:T(128)} %pad_add_fusion.at_ref, f32[1]{0:T(128)S(6)} %div.6.scale_ref, bf16[256,2048]{1,0:T(8,128)(2,1)} %bitcast.55, bf16[512,1024]{1,0:T(8,128)(2,1)} %copy-done.2, ...), custom_call_target="tpu_custom_call" | custom-call | flops 2684354560 | bytes 15728640 | tf_op jit(solution)/shard_map/pallas_call | solution.py:269
  183.2 1.3 collective-permute-start.13
  184.6 0.7 copy-done.13
  185.3 5.9 %weight_product.1 = bf16[4,128,896]{2,1,0:T(8,128)(2,1)} custom-call(s32[4]{0:T(128)} %pad_add_fusion.at_ref, bf16[4,512,256]{2,1,0:T(8,128)(2,1)} %copy-done.7, bf16[4,512,256]{2,1,0:T(8,128)(2,1)} %collective-permute-done.18.a_oth_ref, bf16[512,896]{1,0:T(8,128)(2,1)} %copy-done.9, bf16[512,896]{1,0:T(8,128)(2,1)} %copy-done.11, ...), custom_call_target="tpu_custom_call" | custom-call | flops 1879048192 | bytes 7340032 | tf_op jit(solution)/shard_map/weight_product/pallas_call | solution.py:293
  191.3 1.2 slice_bitcast_fusion.7
  192.9 1.5 collective-permute-start.25
  195.0 8.1 %shard_map.104 = (bf16[256,2048]{1,0:T(8,128)(2,1)}, f32[512,1024]{1,0:T(8,128)}, bf16[512,1024]{1,0:T(8,128)(2,1)}, f32[32,128]{1,0:T(8,128)}) custom-call(f32[1]{0:T(128)S(6)} %div.6.scale_ref, bf16[256,2048]{1,0:T(8,128)(2,1)} %bitcast.56, bf16[256,1024]{1,0:T(8,128)(2,1)} %bitcast.59, bf16[256,1024]{1,0:T(8,128)(2,1)} %bitcast.62, ...), custom_call_target="tpu_custom_call" | custom-call | flops 2415919104 | bytes 13631488 | tf_op jit(solution)/shard_map/pallas_call | solution.py:280
  203.1 1.7 fusion.3
  204.9 3.5 %all-to-all-start.1 = ((bf16[8,16,896]{2,1,0:T(8,128)(2,1)}), bf16[8,16,896]{2,1,0:T(8,128)(2,1)S(1)}, u32[]{:S(2)}, u32[]{:S(2)}) async-start(bf16[8,16,896]{2,1,0:T(8,128)(2,1)} %bitcast.67), calls=%async_computation.1 | async-start | bytes 458752 | tf_op jit(solution)/shard_map/all_to_all | solution.py:380
  208.4 2.6 add_convert_fusion
  211.1 1.3 collective-permute-start.14
  212.4 5.0 %all-to-all-done.1 = bf16[8,16,896]{2,1,0:T(8,128)(2,1)S(1)} async-done(((bf16[8,16,896]{2,1,0:T(8,128)(2,1)}), bf16[8,16,896]{2,1,0:T(8,128)(2,1)S(1)}, u32[]{:S(2)}, u32[]{:S(2)}) %all-to-all-start.1) | async-done | bytes 229408 | tf_op jit(solution)/shard_map/all_to_all | solution.py:380
  217.4 0.6 multiply_reduce_fusion.1
  218.0 7.0 %collective-permute-start.27 = (f32[16,896]{1,0:T(8,128)S(1)}, f32[16,896]{1,0:T(8,128)S(1)}, u32[]{:S(2)}, u32[]{:S(2)}) collective-permute-start(f32[16,896]{1,0:T(8,128)S(1)} %get-tuple-element.38), channel_id=1, source_target_pairs={{0,1},{1,0},{2,3},{3,2},{4,5},{5,4},{6,7},{7,6},{8,9},{9,8},{10,11... | collective-permute-start | bytes 172040 | tf_op jit(solution)/shard_map/ppermute | solution.py:61
  225.0 1.3 slice_reduce_fusion
  226.3 2.7 collective-permute-start.28
  229.1 9.0 %collective-permute-done.14 = bf16[512,1024]{1,0:T(8,128)(2,1)S(1)} collective-permute-done((bf16[512,1024]{1,0:T(8,128)(2,1)}, bf16[512,1024]{1,0:T(8,128)(2,1)S(1)}, u32[]{:S(2)}, u32[]{:S(2)}) %collective-permute-start.14) | collective-permute-done | bytes 1048608 | tf_op jit(solution)/shard_map/ppermute | solution.py:33
  238.1 1.0 copy-done.6
  239.1 2.4 multiply_reduce_fusion
  243.4 0.6 broadcast_in_dim_broadcast_in_dim_broadcast_in_dim.6
  244.0 7.9 %all-to-all-start.2 = ((f32[8,8,128]{2,1,0:T(8,128)}), f32[8,8,128]{2,1,0:T(8,128)S(1)}, u32[]{:S(2)}, u32[]{:S(2)}) async-start(f32[8,8,128]{2,1,0:T(8,128)} %broadcast_in_dim_broadcast_in_dim_broadcast_in_dim.6), calls=%async_computation.2 | async-start | bytes 65536 | tf_op jit(solution)/shard_map/all_to_all | solution.py:66
  251.9 0.7 maximum_select_fusion
  252.6 4.0 %all-to-all-done.2 = f32[8,8,128]{2,1,0:T(8,128)S(1)} async-done(((f32[8,8,128]{2,1,0:T(8,128)}), f32[8,8,128]{2,1,0:T(8,128)S(1)}, u32[]{:S(2)}, u32[]{:S(2)}) %all-to-all-start.2) | async-done | bytes 32800 | tf_op jit(solution)/shard_map/all_to_all | solution.py:66
  256.6 0.7 broadcast_in_dim_broadcast_in_dim_broadcast_in_dim.7
  257.3 7.1 %all-to-all-start.3 = ((f32[32,8,128]{2,1,0:T(8,128)}), f32[32,8,128]{2,1,0:T(8,128)S(1)}, u32[]{:S(2)}, u32[]{:S(2)}) async-start(f32[32,8,128]{2,1,0:T(8,128)} %broadcast_in_dim_broadcast_in_dim_broadcast_in_dim.7), calls=%async_computation.3 | async-start | bytes 262144 | tf_op jit(solution)/shard_map/all_to_all | solution.py:66
  264.4 1.0 slice_bitcast_fusion
  265.4 8.1 %all-to-all-done.3 = f32[32,8,128]{2,1,0:T(8,128)S(1)} async-done(((f32[32,8,128]{2,1,0:T(8,128)}), f32[32,8,128]{2,1,0:T(8,128)S(1)}, u32[]{:S(2)}, u32[]{:S(2)}) %all-to-all-start.3) | async-done | bytes 131104 | tf_op jit(solution)/shard_map/all_to_all | solution.py:66
  (68 shorter events, 3.0 us)
Async XLA Ops:
  0.6 6.7 %copy-start = (bf16[32,1792]{1,0:T(8,128)(2,1)S(1)}, bf16[32,1792]{1,0:T(8,128)(2,1)}, u32[]{:S(2)}) copy-start(bf16[32,1792]{1,0:T(8,128)(2,1)} %param.10) | copy-start | bytes 344068
  2.0 42.3 %collective-permute-start.2 = (bf16[512,1024]{1,0:T(8,128)(2,1)S(1)}, bf16[512,1024]{1,0:T(8,128)(2,1)}, u32[]{:S(2)}, u32[]{:S(2)}) collective-permute-start(bf16[512,1024]{1,0:T(8,128)(2,1)S(1)} %pad_maximum_fusion.1), channel_id=1, source_target_pairs={{0,4},{4,8},{8,12},{12,16},{16,20},{20,24},{24,28},{28,32},{32,36}... | collective-permute-start | bytes 3145736 | tf_op jit(solution)/shard_map/ppermute | solution.py:33
  8.1 33.3 %all-to-all-start = ((bf16[8,32,896]{2,1,0:T(8,128)(2,1)}), bf16[8,32,896]{2,1,0:T(8,128)(2,1)S(1)}, u32[]{:S(2)}, u32[]{:S(2)}) async-start(bf16[8,32,896]{2,1,0:T(8,128)(2,1)} %broadcast_in_dim.30), calls=%async_computation | async-start | bytes 917504 | tf_op jit(solution)/shard_map/all_to_all | solution.py:66
  41.5 37.4 %copy-start.5 = (bf16[8,32,896]{2,1,0:T(8,128)(2,1)}, bf16[8,32,896]{2,1,0:T(8,128)(2,1)S(1)}, u32[]{:S(2)}) copy-start(bf16[8,32,896]{2,1,0:T(8,128)(2,1)S(1)} %all-to-all-done) | copy-start | bytes 1376260
  41.5 10.0 %collective-permute-start.6 = (bf16[256,896]{1,0:T(8,128)(2,1)S(1)}, bf16[256,896]{1,0:T(8,128)(2,1)S(1)}, u32[]{:S(2)}, u32[]{:S(2)}) collective-permute-start(bf16[256,896]{1,0:T(8,128)(2,1)S(1)} %bitcast.63), channel_id=1, source_target_pairs={{0,192},{64,0},{128,64},{192,128},{1,193},{65,1},{129,65},{193,129... | collective-permute-start | bytes 1376264 | tf_op jit(solution)/shard_map/ppermute | solution.py:38
  44.2 29.8 %collective-permute-start.4 = (bf16[256,896]{1,0:T(8,128)(2,1)S(1)}, bf16[256,896]{1,0:T(8,128)(2,1)}, u32[]{:S(2)}, u32[]{:S(2)}) collective-permute-start(bf16[256,896]{1,0:T(8,128)(2,1)S(1)} %bitcast.64), channel_id=1, source_target_pairs={{0,64},{64,128},{128,192},{192,0},{1,65},{65,129},{129,193},{193,1... | collective-permute-start | bytes 1376264 | tf_op jit(solution)/shard_map/ppermute | solution.py:38
  44.2 52.0 %collective-permute-start.3 = (bf16[512,1024]{1,0:T(8,128)(2,1)}, bf16[512,1024]{1,0:T(8,128)(2,1)S(1)}, u32[]{:S(2)}, u32[]{:S(2)}) collective-permute-start(bf16[512,1024]{1,0:T(8,128)(2,1)} %collective-permute-done.2.h1_ref), channel_id=1, source_target_pairs={{0,4},{4,8},{8,12},{12,16},{16,20},{20,24},{24,28},{28,32},{32,36}... | collective-permute-start | bytes 3145736 | tf_op jit(solution)/shard_map/ppermute | solution.py:33
  51.5 24.1 %copy-start.8 = (bf16[256,896]{1,0:T(8,128)(2,1)}, bf16[256,896]{1,0:T(8,128)(2,1)S(1)}, u32[]{:S(2)}) copy-start(bf16[256,896]{1,0:T(8,128)(2,1)S(1)} %collective-permute-done.6) | copy-start | bytes 1376260
  52.3 37.7 %collective-permute-start.7 = (bf16[128,896]{1,0:T(8,128)(2,1)}, bf16[128,896]{1,0:T(8,128)(2,1)S(1)}, u32[]{:S(2)}, u32[]{:S(2)}) collective-permute-start(bf16[128,896]{1,0:T(8,128)(2,1)} %slice.85), channel_id=1, source_target_pairs={{0,192},{64,0},{128,64},{192,128},{1,193},{65,1},{129,65},{193,129... | collective-permute-start | bytes 688136 | tf_op jit(solution)/shard_map/ppermute | solution.py:38
  75.6 14.3 %collective-permute-start.5 = (bf16[128,896]{1,0:T(8,128)(2,1)}, bf16[128,896]{1,0:T(8,128)(2,1)S(1)}, u32[]{:S(2)}, u32[]{:S(2)}) collective-permute-start(bf16[128,896]{1,0:T(8,128)(2,1)} %slice.84), channel_id=1, source_target_pairs={{0,64},{64,128},{128,192},{192,0},{1,65},{65,129},{129,193},{193,1... | collective-permute-start | bytes 688136 | tf_op jit(solution)/shard_map/ppermute | solution.py:38
  78.8 28.4 %copy-start.3 = (bf16[256,896]{1,0:T(8,128)(2,1)}, bf16[256,896]{1,0:T(8,128)(2,1)S(1)}, u32[]{:S(2)}) copy-start(bf16[256,896]{1,0:T(8,128)(2,1)S(1)} %get-tuple-element.53.m_own_ref) | copy-start | bytes 1376260
  78.8 26.5 %collective-permute-start.19 = (bf16[256,896]{1,0:T(8,128)(2,1)}, bf16[256,896]{1,0:T(8,128)(2,1)}, u32[]{:S(2)}, u32[]{:S(2)}) collective-permute-start(bf16[256,896]{1,0:T(8,128)(2,1)} %get-tuple-element.52.m_oth_ref), channel_id=1, source_target_pairs={{0,1},{1,0},{2,3},{3,2},{4,5},{5,4},{6,7},{7,6},{8,9},{9,8},{10,11... | collective-permute-start | bytes 1376264 | tf_op jit(solution)/shard_map/ppermute | solution.py:61
  91.6 11.5 %copy-start.1 = (bf16[4,256,896]{2,1,0:T(8,128)(2,1)}, bf16[4,256,896]{2,1,0:T(8,128)(2,1)S(1)}, u32[]{:S(2)}) copy-start(bf16[4,256,896]{2,1,0:T(8,128)(2,1)S(1)} %pad_maximum_fusion.wa_ref) | copy-start | bytes 5505028
  91.6 78.0 %collective-permute-start.8 = (bf16[4,256,896]{2,1,0:T(8,128)(2,1)S(1)}, bf16[4,256,896]{2,1,0:T(8,128)(2,1)}, u32[]{:S(2)}, u32[]{:S(2)}) collective-permute-start(bf16[4,256,896]{2,1,0:T(8,128)(2,1)S(1)} %pad_maximum_fusion.wa_ref), channel_id=1, source_target_pairs={{0,1},{1,0},{2,3},{3,2},{4,5},{5,4},{6,7},{7,6},{8,9},{9,8},{10,11... | collective-permute-start | bytes 5505032 | tf_op jit(solution)/shard_map/ppermute | solution.py:61
  93.5 52.0 %collective-permute-start.9 = (bf16[4,128,896]{2,1,0:T(8,128)(2,1)}, bf16[4,128,896]{2,1,0:T(8,128)(2,1)}, u32[]{:S(2)}, u32[]{:S(2)}) collective-permute-start(bf16[4,128,896]{2,1,0:T(8,128)(2,1)} %get-tuple-element.42), channel_id=1, source_target_pairs={{0,34},{2,32},{4,36},{6,38},{8,40},{10,42},{12,44},{14,46},{16,48}... | collective-permute-start | bytes 2752520 | tf_op jit(solution)/shard_map/ppermute | solution.py:57
  93.5 53.7 %collective-permute-start.10 = (bf16[4,128,896]{2,1,0:T(8,128)(2,1)}, bf16[4,128,896]{2,1,0:T(8,128)(2,1)}, u32[]{:S(2)}, u32[]{:S(2)}) collective-permute-start(bf16[4,128,896]{2,1,0:T(8,128)(2,1)} %get-tuple-element.41), channel_id=1, source_target_pairs={{0,34},{2,32},{4,38},{6,36},{8,42},{10,40},{12,46},{14,44},{16,50}... | collective-permute-start | bytes 2752520 | tf_op jit(solution)/shard_map/ppermute | solution.py:57
  96.2 1.0 copy-start.2
  105.0 7.3 %collective-permute-start.17 = (bf16[512,256]{1,0:T(8,128)(2,1)S(1)}, bf16[512,256]{1,0:T(8,128)(2,1)S(1)}, u32[]{:S(2)}, u32[]{:S(2)}) collective-permute-start(bf16[512,256]{1,0:T(8,128)(2,1)S(1)} %get-tuple-element.44), channel_id=1, source_target_pairs={{0,192},{64,0},{128,64},{192,128},{1,193},{65,1},{129,65},{193,129... | collective-permute-start | bytes 786440 | tf_op jit(solution)/shard_map/ppermute | solution.py:38
  105.4 3.0 %collective-permute-start = (f32[1]{0:T(128)}, f32[1]{0:T(128)}, u32[]{:S(2)}, u32[]{:S(2)}) collective-permute-start(f32[1]{0:T(128)} %bitcast.1), channel_id=1, source_target_pairs={{0,1},{1,0},{2,3},{3,2},{4,5},{5,4},{6,7},{7,6},{8,9},{9,8},{10,11... | collective-permute-start | bytes 20 | tf_op jit(solution)/shard_map/ppermute | solution.py:61
  108.4 61.2 %copy-start.9 = (bf16[512,896]{1,0:T(8,128)(2,1)}, bf16[512,896]{1,0:T(8,128)(2,1)S(1)}, u32[]{:S(2)}) copy-start(bf16[512,896]{1,0:T(8,128)(2,1)S(1)} %pad_maximum_fusion.3.m0_ref) | copy-start | bytes 2752516
  108.4 40.1 %collective-permute-start.20 = (bf16[512,896]{1,0:T(8,128)(2,1)S(1)}, bf16[512,896]{1,0:T(8,128)(2,1)S(1)}, u32[]{:S(2)}, u32[]{:S(2)}) collective-permute-start(bf16[512,896]{1,0:T(8,128)(2,1)S(1)} %pad_maximum_fusion.3.m0_ref), channel_id=1, source_target_pairs={{0,64},{64,128},{128,192},{192,0},{1,65},{65,129},{129,193},{193,1... | collective-permute-start | bytes 2752520 | tf_op jit(solution)/shard_map/ppermute | solution.py:38
  112.3 35.0 %copy-start.10 = (bf16[512,256]{1,0:T(8,128)(2,1)}, bf16[512,256]{1,0:T(8,128)(2,1)S(1)}, u32[]{:S(2)}) copy-start(bf16[512,256]{1,0:T(8,128)(2,1)S(1)} %collective-permute-done.17) | copy-start | bytes 786436
  112.3 24.9 %collective-permute-start.16 = (bf16[512,256]{1,0:T(8,128)(2,1)S(1)}, bf16[512,256]{1,0:T(8,128)(2,1)S(1)}, u32[]{:S(2)}, u32[]{:S(2)}) collective-permute-start(bf16[512,256]{1,0:T(8,128)(2,1)S(1)} %get-tuple-element.45), channel_id=1, source_target_pairs={{0,128},{64,192},{128,0},{192,64},{1,129},{65,193},{129,1},{193,65... | collective-permute-start | bytes 786440 | tf_op jit(solution)/shard_map/ppermute | solution.py:38
  137.3 8.2 %collective-permute-start.15 = (bf16[512,256]{1,0:T(8,128)(2,1)S(1)}, bf16[512,256]{1,0:T(8,128)(2,1)S(1)}, u32[]{:S(2)}, u32[]{:S(2)}) collective-permute-start(bf16[512,256]{1,0:T(8,128)(2,1)S(1)} %get-tuple-element.46), channel_id=1, source_target_pairs={{0,64},{64,128},{128,192},{192,0},{1,65},{65,129},{129,193},{193,1... | collective-permute-start | bytes 786440 | tf_op jit(solution)/shard_map/ppermute | solution.py:38
  145.5 20.2 %collective-permute-start.21 = (bf16[512,896]{1,0:T(8,128)(2,1)S(1)}, bf16[512,896]{1,0:T(8,128)(2,1)S(1)}, u32[]{:S(2)}, u32[]{:S(2)}) collective-permute-start(bf16[512,896]{1,0:T(8,128)(2,1)S(1)} %pad_maximum_fusion.3.m0_ref), channel_id=1, source_target_pairs={{0,192},{64,0},{128,64},{192,128},{1,193},{65,1},{129,65},{193,129... | collective-permute-start | bytes 2752520 | tf_op jit(solution)/shard_map/ppermute | solution.py:38
  145.5 27.4 %collective-permute-start.11 = (bf16[4,128,896]{2,1,0:T(8,128)(2,1)}, bf16[4,128,896]{2,1,0:T(8,128)(2,1)}, u32[]{:S(2)}, u32[]{:S(2)}) collective-permute-start(bf16[4,128,896]{2,1,0:T(8,128)(2,1)} %collective-permute-done.9.wbl_ref), channel_id=1, source_target_pairs={{0,1},{1,0},{2,3},{3,2},{4,5},{5,4},{6,7},{7,6},{8,9},{9,8},{10,11... | collective-permute-start | bytes 2752520 | tf_op jit(solution)/shard_map/ppermute | solution.py:61
  147.2 25.7 %collective-permute-start.12 = (bf16[4,128,896]{2,1,0:T(8,128)(2,1)}, bf16[4,128,896]{2,1,0:T(8,128)(2,1)}, u32[]{:S(2)}, u32[]{:S(2)}) collective-permute-start(bf16[4,128,896]{2,1,0:T(8,128)(2,1)} %collective-permute-done.10.wbh_ref), channel_id=1, source_target_pairs={{0,1},{1,0},{2,3},{3,2},{4,5},{5,4},{6,7},{7,6},{8,9},{9,8},{10,11... | collective-permute-start | bytes 2752520 | tf_op jit(solution)/shard_map/ppermute | solution.py:61
  148.5 34.8 %copy-start.7 = (bf16[4,512,256]{2,1,0:T(8,128)(2,1)}, bf16[4,512,256]{2,1,0:T(8,128)(2,1)S(1)}, u32[]{:S(2)}) copy-start(bf16[4,512,256]{2,1,0:T(8,128)(2,1)S(1)} %pad_maximum_fusion.2.a_own_ref) | copy-start | bytes 3145732
  148.5 23.7 %copy-start.11 = (bf16[512,896]{1,0:T(8,128)(2,1)}, bf16[512,896]{1,0:T(8,128)(2,1)S(1)}, u32[]{:S(2)}) copy-start(bf16[512,896]{1,0:T(8,128)(2,1)S(1)} %collective-permute-done.20.m1_ref) | copy-start | bytes 2752516
  148.5 36.1 %collective-permute-start.18 = (bf16[4,512,256]{2,1,0:T(8,128)(2,1)S(1)}, bf16[4,512,256]{2,1,0:T(8,128)(2,1)}, u32[]{:S(2)}, u32[]{:S(2)}) collective-permute-start(bf16[4,512,256]{2,1,0:T(8,128)(2,1)S(1)} %pad_maximum_fusion.2.a_own_ref), channel_id=1, source_target_pairs={{0,1},{1,0},{2,3},{3,2},{4,5},{5,4},{6,7},{7,6},{8,9},{9,8},{10,11... | collective-permute-start | bytes 3145736 | tf_op jit(solution)/shard_map/ppermute | solution.py:61
  165.7 7.1 %copy-start.12 = (bf16[512,896]{1,0:T(8,128)(2,1)}, bf16[512,896]{1,0:T(8,128)(2,1)S(1)}, u32[]{:S(2)}) copy-start(bf16[512,896]{1,0:T(8,128)(2,1)S(1)} %collective-permute-done.21.m3_ref) | copy-start | bytes 2752516
  165.7 3.9 %collective-permute-start.1 = (f32[1]{0:T(128)}, f32[1]{0:T(128)}, u32[]{:S(2)}, u32[]{:S(2)}) collective-permute-start(f32[1]{0:T(128)} %add.53), channel_id=1, source_target_pairs={{0,2},{2,0},{1,3},{3,1},{4,6},{6,4},{5,7},{7,5},{8,10},{10,8},{9,1... | collective-permute-start | bytes 20 | tf_op jit(solution)/shard_map/ppermute | solution.py:61
  169.5 15.0 %collective-permute-start.22 = (bf16[256,896]{1,0:T(8,128)(2,1)S(1)}, bf16[256,896]{1,0:T(8,128)(2,1)}, u32[]{:S(2)}, u32[]{:S(2)}) collective-permute-start(bf16[256,896]{1,0:T(8,128)(2,1)S(1)} %slice.90), channel_id=1, source_target_pairs={{0,64},{64,128},{128,192},{192,0},{1,65},{65,129},{129,193},{193,1... | collective-permute-start | bytes 1376264 | tf_op jit(solution)/shard_map/ppermute | solution.py:38
  169.6 15.0 %collective-permute-start.23 = (bf16[256,896]{1,0:T(8,128)(2,1)}, bf16[256,896]{1,0:T(8,128)(2,1)S(1)}, u32[]{:S(2)}, u32[]{:S(2)}) collective-permute-start(bf16[256,896]{1,0:T(8,128)(2,1)} %slice.91), channel_id=1, source_target_pairs={{0,192},{64,0},{128,64},{192,128},{1,193},{65,1},{129,65},{193,129... | collective-permute-start | bytes 1376264 | tf_op jit(solution)/shard_map/ppermute | solution.py:38
  183.2 25.2 %collective-permute-start.13 = (bf16[512,1024]{1,0:T(8,128)(2,1)}, bf16[512,1024]{1,0:T(8,128)(2,1)S(1)}, u32[]{:S(2)}, u32[]{:S(2)}) collective-permute-start(bf16[512,1024]{1,0:T(8,128)(2,1)} %get-tuple-element.35), channel_id=1, source_target_pairs={{4,0},{8,4},{12,8},{16,12},{20,16},{24,20},{28,24},{32,28},{36,32}... | collective-permute-start | bytes 3145736 | tf_op jit(solution)/shard_map/ppermute | solution.py:33
  184.6 0.8 copy-start.13
  192.5 10.6 %collective-permute-start.26 = (bf16[128,896]{1,0:T(8,128)(2,1)S(1)}, bf16[128,896]{1,0:T(8,128)(2,1)S(1)}, u32[]{:S(2)}, u32[]{:S(2)}) collective-permute-start(bf16[128,896]{1,0:T(8,128)(2,1)S(1)} %get-tuple-element.50), channel_id=1, source_target_pairs={{0,34},{32,0},{2,32},{34,2},{1,35},{33,1},{3,33},{35,3},{4,38},{36... | collective-permute-start | bytes 688136 | tf_op jit(solution)/shard_map/ppermute | solution.py:43
  192.9 10.2 %collective-permute-start.25 = (bf16[128,896]{1,0:T(8,128)(2,1)S(1)}, bf16[128,896]{1,0:T(8,128)(2,1)S(1)}, u32[]{:S(2)}, u32[]{:S(2)}) collective-permute-start(bf16[128,896]{1,0:T(8,128)(2,1)S(1)} %get-tuple-element.51), channel_id=1, source_target_pairs={{0,2},{32,34},{2,0},{34,32},{1,3},{33,35},{3,1},{35,33},{4,6},{36,... | collective-permute-start | bytes 688136 | tf_op jit(solution)/shard_map/ppermute | solution.py:43
  194.5 8.7 %collective-permute-start.24 = (bf16[128,896]{1,0:T(8,128)(2,1)S(1)}, bf16[128,896]{1,0:T(8,128)(2,1)S(1)}, u32[]{:S(2)}, u32[]{:S(2)}) collective-permute-start(bf16[128,896]{1,0:T(8,128)(2,1)S(1)} %get-tuple-element.49), channel_id=1, source_target_pairs={{0,32},{32,2},{2,34},{34,0},{1,33},{33,3},{3,35},{35,1},{4,36},{36... | collective-permute-start | bytes 688136 | tf_op jit(solution)/shard_map/ppermute | solution.py:43
  204.9 34.2 %copy-start.4 = (f32[512,1024]{1,0:T(8,128)S(1)}, f32[512,1024]{1,0:T(8,128)}, u32[]{:S(2)}) copy-start(f32[512,1024]{1,0:T(8,128)} %get-tuple-element.33) | copy-start | bytes 6291460
  204.9 12.5 %all-to-all-start.1 = ((bf16[8,16,896]{2,1,0:T(8,128)(2,1)}), bf16[8,16,896]{2,1,0:T(8,128)(2,1)S(1)}, u32[]{:S(2)}, u32[]{:S(2)}) async-start(bf16[8,16,896]{2,1,0:T(8,128)(2,1)} %bitcast.67), calls=%async_computation.1 | async-start | bytes 458752 | tf_op jit(solution)/shard_map/all_to_all | solution.py:380
  211.1 27.0 %collective-permute-start.14 = (bf16[512,1024]{1,0:T(8,128)(2,1)}, bf16[512,1024]{1,0:T(8,128)(2,1)S(1)}, u32[]{:S(2)}, u32[]{:S(2)}) collective-permute-start(bf16[512,1024]{1,0:T(8,128)(2,1)} %add_convert_fusion), channel_id=1, source_target_pairs={{4,0},{8,4},{12,8},{16,12},{20,16},{24,20},{28,24},{32,28},{36,32}... | collective-permute-start | bytes 3145736 | tf_op jit(solution)/shard_map/ppermute | solution.py:33
  218.0 8.3 %collective-permute-start.27 = (f32[16,896]{1,0:T(8,128)S(1)}, f32[16,896]{1,0:T(8,128)S(1)}, u32[]{:S(2)}, u32[]{:S(2)}) collective-permute-start(f32[16,896]{1,0:T(8,128)S(1)} %get-tuple-element.38), channel_id=1, source_target_pairs={{0,1},{1,0},{2,3},{3,2},{4,5},{5,4},{6,7},{7,6},{8,9},{9,8},{10,11... | collective-permute-start | bytes 172040 | tf_op jit(solution)/shard_map/ppermute | solution.py:61
  226.3 25.6 %collective-permute-start.28 = (f32[16,1792]{1,0:T(8,128)S(1)}, f32[16,1792]{1,0:T(8,128)S(1)}, u32[]{:S(2)}, u32[]{:S(2)}) collective-permute-start(f32[16,1792]{1,0:T(8,128)S(1)} %maximum_select_fusion.1), channel_id=1, source_target_pairs={{0,2},{2,0},{1,3},{3,1},{4,6},{6,4},{5,7},{7,5},{8,10},{10,8},{9,1... | collective-permute-start | bytes 344072 | tf_op jit(solution)/shard_map/ppermute | solution.py:61
  238.1 1.0 copy-start.6
  244.0 12.6 %all-to-all-start.2 = ((f32[8,8,128]{2,1,0:T(8,128)}), f32[8,8,128]{2,1,0:T(8,128)S(1)}, u32[]{:S(2)}, u32[]{:S(2)}) async-start(f32[8,8,128]{2,1,0:T(8,128)} %broadcast_in_dim_broadcast_in_dim_broadcast_in_dim.6), calls=%async_computation.2 | async-start | bytes 65536 | tf_op jit(solution)/shard_map/all_to_all | solution.py:66
  257.3 16.2 %all-to-all-start.3 = ((f32[32,8,128]{2,1,0:T(8,128)}), f32[32,8,128]{2,1,0:T(8,128)S(1)}, u32[]{:S(2)}, u32[]{:S(2)}) async-start(f32[32,8,128]{2,1,0:T(8,128)} %broadcast_in_dim_broadcast_in_dim_broadcast_in_dim.7), calls=%async_computation.3 | async-start | bytes 262144 | tf_op jit(solution)/shard_map/all_to_all | solution.py:66

commit v2 on v1

--- a/solution.py
+++ b/solution.py
@@ -350,15 +350,18 @@
 
     p, pf, acc, tot = near_forward(where, q_rows, k_rows, v_rows, h1)
     p2, pf2, attn, inv = far_forward(where, q_rows, h2, acc, tot)
-    a_own = jnp.stack([
+    attn_parts = (
         attn[0], ring(attn[1], "seq_0", 1), ring(attn[2], "seq_0", 2), ring(attn[3], "seq_0", -1)
-    ])
-    a_oth = swap(a_own, "dp_1")
+    )
 
     d2, g, delta, dscore = far_backward(
         where, act_scale, q_rows, h2, p2, pf2, inv, attn, m_own, m_oth,
         (wa, wc, wbl, wbh, wdl, wdh),
     )
+    attn_parts, _ = lax.optimization_barrier((attn_parts, delta))
+    a_own = jnp.stack(attn_parts)
+    a_oth = swap(a_own, "dp_1")
+
     r1 = shifted(d2, -1)
     dq, d0, d1, dq_sq = near_backward(
         act_scale, q_rows, k_rows, v_rows, h1, h2, p, pf, g, delta, dscore

time: 276 us -> 267 us (0.967)
  waiting for transfers between devices: 126 us -> 67.2 us
  starting transfers between devices: 73.5 us -> 100 us
  blocking collectives: 0 us -> 23.6 us
    ppermute x11, waiting for transfers between devices: 73.2 us -> 32 us  [ring(): lax.ppermute(value, axis, [(s, (s + steps) % count) for s in range(count)])]
    ppermute x9, starting transfers between devices: 20 us -> 52.5 us  [swap(): return lax.ppermute(value, axis, [(0, 1), (1, 0)])]
    all_to_all x3 -> x2, waiting for transfers between devices: 38.5 us -> 12.1 us  [for_each(): lax.all_to_all(jnp.broadcast_to(value[None], (size, *value.shape)), axis,...]
    all_to_all x0 -> x1, blocking collectives: none -> 23.6 us  [for_each(): lax.all_to_all(jnp.broadcast_to(value[None], (size, *value.shape)), axis,...]
    all_to_all x3 -> x2, starting transfers between devices: 21.2 us -> 16.4 us  [for_each(): lax.all_to_all(jnp.broadcast_to(value[None], (size, *value.shape)), axis,...]
    ppermute x4, waiting for transfers between devices: 9.02 us -> 12.8 us  [shifted(): lax.ppermute(value, SEQ, [(source, source + steps) for source in range(in...]
    ppermute x4, starting transfers between devices: 9.28 us -> 6.2 us  [shifted(): lax.ppermute(value, SEQ, [(source, source + steps) for source in range(in...]
    ppermute x3, waiting for transfers between devices: 0.01 us -> 2.85 us  [ring_x(): lax.ppermute(value, X_AXES, [(at(s), at((s + steps) % 4)) for s in range(...]
  transfers between devices with their start and end apart: 33 -> 32, of which waited for: 12 -> 12; matrix products, arithmetic and copies ran while one was open for 10% -> 10% of each run, Pallas kernels for 14% -> 14%
where the time goes in v2:
time: 267 us; the launch traced here: 266 us
  starting transfers between devices  100 us (37%)
  waiting for transfers between devices  67.2 us (25%)
  Pallas kernels  37.1 us (14%)
  blocking collectives  23.6 us (9%)
  local copies, waits for them, and re-layouts  16.8 us (6%)
  other arithmetic  14.9 us (6%)
  between operations  6.03 us (2%)
    ppermute x9, starting transfers between devices, swap(): return lax.ppermute(value, axis, [(0, 1), (1, 0)])  52.5 us
    ppermute x11, waiting for transfers between devices, ring(): lax.ppermute(value, axis, [(s, (s + steps) % count) for s in range(count)])  32 us
    all_to_all x1, blocking collectives, for_each(): lax.all_to_all(jnp.broadcast_to(value[None], (size, *value.shape)), axis,...  23.6 us
    ppermute x11, starting transfers between devices, ring(): lax.ppermute(value, axis, [(s, (s + steps) % count) for s in range(count)])  16.6 us
    all_to_all x2, starting transfers between devices, for_each(): lax.all_to_all(jnp.broadcast_to(value[None], (size, *value.shape)), axis,...  16.4 us
    ppermute x4, waiting for transfers between devices, shifted(): lax.ppermute(value, SEQ, [(source, source + steps) for source in range(in...  12.8 us
    all_to_all x2, waiting for transfers between devices, for_each(): lax.all_to_all(jnp.broadcast_to(value[None], (size, *value.shape)), axis,...  12.1 us
    pallas_call x1, Pallas kernels, far_backward(): call(far_grad_kernel, 2, [HEAD_COLS, BOTH_COLS, of_head(TOK_DEV), of_head...  10.3 us
  transfers between devices with their start and end apart: 32, of which 12 were waited for; matrix products, arithmetic and copies ran while one was open for 10% of the time, Pallas kernels for 14%

profile of v2, /device:TPU:1, one launch (start us, length us, event | category | flops | bytes accessed | tf_op | source)
XLA Modules:
  0.0 265.9 jit_solution(9370284898678742102)
XLA Ops:
  0.7 0.9 copy-done
  1.6 23.6 %all_to_all.24 = bf16[8,32,896]{2,1,0:T(8,128)(2,1)S(1)} all-to-all(bf16[8,32,896]{2,1,0:T(8,128)(2,1)S(1)} %broadcast_in_dim.30), channel_id=1, replica_groups=mesh['seq_0'=4,'seq_1'=2,'seq_2'=8,'dp_0'=2,'dp_1'=2] {'seq_2'}, dimensions={0} | all-to-all | bytes 917504 | tf_op jit(solution)/shard_map/all_to_all | solution.py:66
  25.2 2.7 %collective-permute-start.6 = (bf16[256,896]{1,0:T(8,128)(2,1)S(1)}, bf16[256,896]{1,0:T(8,128)(2,1)S(1)}, u32[]{:S(2)}, u32[]{:S(2)}) collective-permute-start(bf16[256,896]{1,0:T(8,128)(2,1)S(1)} %bitcast.66), channel_id=1, source_target_pairs={{0,192},{64,0},{128,64},{192,128},{1,193},{65,1},{129,65},{193,129... | collective-permute-start | bytes 1376264 | tf_op jit(solution)/shard_map/ppermute | solution.py:38
  27.9 7.6 %collective-permute-done.6 = bf16[256,896]{1,0:T(8,128)(2,1)S(1)} collective-permute-done((bf16[256,896]{1,0:T(8,128)(2,1)S(1)}, bf16[256,896]{1,0:T(8,128)(2,1)S(1)}, u32[]{:S(2)}, u32[]{:S(2)}) %collective-permute-start.6) | collective-permute-done | bytes 458784 | tf_op jit(solution)/shard_map/ppermute | solution.py:38
  35.6 3.5 %collective-permute-start.7 = (bf16[128,896]{1,0:T(8,128)(2,1)S(1)}, bf16[128,896]{1,0:T(8,128)(2,1)S(1)}, u32[]{:S(2)}, u32[]{:S(2)}) collective-permute-start(bf16[128,896]{1,0:T(8,128)(2,1)S(1)} %slice.85), channel_id=1, source_target_pairs={{0,192},{64,0},{128,64},{192,128},{1,193},{65,1},{129,65},{193,129... | collective-permute-start | bytes 688136 | tf_op jit(solution)/shard_map/ppermute | solution.py:38
  39.3 2.3 collective-permute-start.2
  42.0 3.2 %collective-permute-done.5 = bf16[128,896]{1,0:T(8,128)(2,1)S(1)} collective-permute-done((bf16[128,896]{1,0:T(8,128)(2,1)S(1)}, bf16[128,896]{1,0:T(8,128)(2,1)S(1)}, u32[]{:S(2)}, u32[]{:S(2)}) %collective-permute-start.5) | collective-permute-done | bytes 229408 | tf_op jit(solution)/shard_map/ppermute | solution.py:38
  45.6 1.6 fusion.4
  47.2 2.5 collective-permute-start.9
  49.9 23.9 %collective-permute-start.8 = (bf16[4,256,896]{2,1,0:T(8,128)(2,1)S(1)}, bf16[4,256,896]{2,1,0:T(8,128)(2,1)}, u32[]{:S(2)}, u32[]{:S(2)}) collective-permute-start(bf16[4,256,896]{2,1,0:T(8,128)(2,1)S(1)} %pad_maximum_fusion.wa_ref), channel_id=1, source_target_pairs={{0,1},{1,0},{2,3},{3,2},{4,5},{5,4},{6,7},{7,6},{8,9},{9,8},{10,11... | collective-permute-start | bytes 5505032 | tf_op jit(solution)/shard_map/ppermute | solution.py:61
  73.8 1.3 collective-permute-start.3
  75.8 1.5 collective-permute-start
  77.3 8.1 %collective-permute-start.11 = (bf16[4,128,896]{2,1,0:T(8,128)(2,1)}, bf16[4,128,896]{2,1,0:T(8,128)(2,1)}, u32[]{:S(2)}, u32[]{:S(2)}) collective-permute-start(bf16[4,128,896]{2,1,0:T(8,128)(2,1)} %collective-permute-done.9.wbl_ref), channel_id=1, source_target_pairs={{0,1},{1,0},{2,3},{3,2},{4,5},{5,4},{6,7},{7,6},{8,9},{9,8},{10,11... | collective-permute-start | bytes 2752520 | tf_op jit(solution)/shard_map/ppermute | solution.py:61
  85.5 9.8 %collective-permute-start.12 = (bf16[4,128,896]{2,1,0:T(8,128)(2,1)}, bf16[4,128,896]{2,1,0:T(8,128)(2,1)}, u32[]{:S(2)}, u32[]{:S(2)}) collective-permute-start(bf16[4,128,896]{2,1,0:T(8,128)(2,1)} %collective-permute-done.10.wbh_ref), channel_id=1, source_target_pairs={{0,1},{1,0},{2,3},{3,2},{4,5},{5,4},{6,7},{7,6},{8,9},{9,8},{10,11... | collective-permute-start | bytes 2752520 | tf_op jit(solution)/shard_map/ppermute | solution.py:61
  95.3 2.2 bitcast_select_fusion
  97.5 2.0 constant_dynamic-slice_fusion.1
  100.1 2.3 collective-permute-start.1
  102.4 1.8 collective-permute-done.1
  104.2 1.0 collective-permute-start.19
  106.4 6.8 %shard_map.101 = (bf16[4,512,512]{2,1,0:T(8,128)(2,1)}, bf16[4,512,512]{2,1,0:T(8,128)(2,1)}, f32[4,256,512]{2,1,0:T(8,128)}, f32[4,8,512]{2,1,0:T(8,128)}) custom-call(s32[4]{0:T(128)} %pad_add_fusion.at_ref, bf16[256,2048]{1,0:T(8,128)(2,1)} %bitcast.56, bf16[256,1024]{1,0:T(8,128)(2,1)} %bitcast.60, bf16[256,1024]{1,0:T(8,128)(2,1)} %bitcast.63, ...), custom_call_target="tpu_custom_call" | custom-call | flops 1073741824 | bytes 9437184 | tf_op jit(solution)/shard_map/pallas_call | solution.py:245
  113.3 1.1 copy-done.2
  114.3 5.9 %shard_map.102 = (bf16[4,256,512]{2,1,0:T(8,128)(2,1)}, bf16[4,256,512]{2,1,0:T(8,128)(2,1)}, bf16[4,512,256]{2,1,0:T(8,128)(2,1)}, f32[4,8,512]{2,1,0:T(8,128)}) custom-call(s32[4]{0:T(128)} %pad_add_fusion.at_ref, bf16[256,2048]{1,0:T(8,128)(2,1)} %bitcast.57, bf16[512,1024]{1,0:T(8,128)(2,1)} %copy-done.2, f32[4,256,512]{2,1,0:T(8,128)} %get-tuple-element.27.acc_ref, ...), custom_call_target="tpu_custom_call" | custom-call | flops 536870912 | bytes 7340032 | tf_op jit(solution)/shard_map/pallas_call | solution.py:256
  120.2 2.0 slice_bitcast_fusion.2
  122.1 2.2 collective-permute-start.15
  124.4 2.5 collective-permute-start.17
  126.9 1.1 pad_maximum_fusion.3.m0_ref
  128.1 2.7 collective-permute-start.21
  130.7 10.3 %shard_map.103 = (bf16[512,1024]{1,0:T(8,128)(2,1)}, bf16[4,256,512]{2,1,0:T(8,128)(2,1)}, f32[4,8,512]{2,1,0:T(8,128)}, bf16[4,256,512]{2,1,0:T(8,128)(2,1)}) custom-call(s32[4]{0:T(128)} %pad_add_fusion.at_ref, f32[1]{0:T(128)S(6)} %div.6.scale_ref, bf16[256,2048]{1,0:T(8,128)(2,1)} %bitcast.58, bf16[512,1024]{1,0:T(8,128)(2,1)} %copy-done.2, ...), custom_call_target="tpu_custom_call" | custom-call | flops 2684354560 | bytes 15728640 | tf_op jit(solution)/shard_map/pallas_call | solution.py:269
  141.1 0.7 copy-done.10
  141.8 1.2 pad_maximum_fusion.2.a_own_ref
  143.0 1.2 collective-permute-start.18
  144.2 12.6 %collective-permute-done.20.m1_ref = bf16[512,896]{1,0:T(8,128)(2,1)} collective-permute-done((bf16[512,896]{1,0:T(8,128)(2,1)S(1)}, bf16[512,896]{1,0:T(8,128)(2,1)}, u32[]{:S(2)}, u32[]{:S(2)}) %collective-permute-start.20) | collective-permute-done | bytes 917536 | tf_op jit(solution)/shard_map/ppermute | solution.py:38
  156.8 1.1 slice.90
  157.9 1.1 collective-permute-start.22
  159.0 1.1 slice.91
  160.1 1.7 collective-permute-start.23
  161.8 1.3 collective-permute-start.13
  163.0 7.3 %collective-permute-done.22.m2a_ref = bf16[256,896]{1,0:T(8,128)(2,1)S(1)} collective-permute-done((bf16[256,896]{1,0:T(8,128)(2,1)S(1)}, bf16[256,896]{1,0:T(8,128)(2,1)S(1)}, u32[]{:S(2)}, u32[]{:S(2)}) %collective-permute-start.22) | collective-permute-done | bytes 458784 | tf_op jit(solution)/shard_map/ppermute | solution.py:38
  170.4 0.7 collective-permute-done.23.m2b_ref
  171.1 0.8 copy-done.13
  171.9 1.0 copy-done.11
  172.9 5.9 %weight_product.1 = bf16[4,128,896]{2,1,0:T(8,128)(2,1)} custom-call(s32[4]{0:T(128)} %pad_add_fusion.at_ref, bf16[4,512,256]{2,1,0:T(8,128)(2,1)} %copy-done.8, bf16[4,512,256]{2,1,0:T(8,128)(2,1)} %copy-done.11, bf16[512,896]{1,0:T(8,128)(2,1)} %copy-done.9, bf16[512,896]{1,0:T(8,128)(2,1)} %collective-permute-done.20.m1_ref, ...), custom_call_target="tpu_custom_call" | custom-call | flops 1879048192 | bytes 7340032 | tf_op jit(solution)/shard_map/weight_product/pallas_call | solution.py:293
  178.9 1.2 slice_bitcast_fusion.8
  180.2 1.6 collective-permute-start.25
  181.8 0.8 collective-permute-start.24
  182.6 8.1 %shard_map.104 = (bf16[256,2048]{1,0:T(8,128)(2,1)}, f32[512,1024]{1,0:T(8,128)}, bf16[512,1024]{1,0:T(8,128)(2,1)}, f32[32,128]{1,0:T(8,128)}) custom-call(f32[1]{0:T(128)S(6)} %div.6.scale_ref, bf16[256,2048]{1,0:T(8,128)(2,1)} %bitcast.59, bf16[256,1024]{1,0:T(8,128)(2,1)} %bitcast.61, bf16[256,1024]{1,0:T(8,128)(2,1)} %bitcast.64, ...), custom_call_target="tpu_custom_call" | custom-call | flops 2415919104 | bytes 13631488 | tf_op jit(solution)/shard_map/pallas_call | solution.py:280
  190.7 2.8 %collective-permute-done.24 = bf16[128,896]{1,0:T(8,128)(2,1)S(1)} collective-permute-done((bf16[128,896]{1,0:T(8,128)(2,1)S(1)}, bf16[128,896]{1,0:T(8,128)(2,1)S(1)}, u32[]{:S(2)}, u32[]{:S(2)}) %collective-permute-start.24) | collective-permute-done | bytes 229408 | tf_op jit(solution)/shard_map/ppermute | solution.py:43
  193.6 1.7 fusion.3
  195.3 3.5 %all-to-all-start.1 = ((bf16[8,16,896]{2,1,0:T(8,128)(2,1)}), bf16[8,16,896]{2,1,0:T(8,128)(2,1)S(1)}, u32[]{:S(2)}, u32[]{:S(2)}) async-start(bf16[8,16,896]{2,1,0:T(8,128)(2,1)} %bitcast.72), calls=%async_computation.1 | async-start | bytes 458752 | tf_op jit(solution)/shard_map/all_to_all | solution.py:383
  198.9 2.6 add_convert_fusion
  201.5 1.3 collective-permute-start.14
  202.8 5.6 %all-to-all-done.1 = bf16[8,16,896]{2,1,0:T(8,128)(2,1)S(1)} async-done(((bf16[8,16,896]{2,1,0:T(8,128)(2,1)}), bf16[8,16,896]{2,1,0:T(8,128)(2,1)S(1)}, u32[]{:S(2)}, u32[]{:S(2)}) %all-to-all-start.1) | async-done | bytes 229408 | tf_op jit(solution)/shard_map/all_to_all | solution.py:383
  209.1 2.5 collective-permute-start.27
  211.6 1.3 slice_reduce_fusion
  212.9 2.1 collective-permute-start.28
  215.0 12.8 %collective-permute-done.14 = bf16[512,1024]{1,0:T(8,128)(2,1)S(1)} collective-permute-done((bf16[512,1024]{1,0:T(8,128)(2,1)}, bf16[512,1024]{1,0:T(8,128)(2,1)S(1)}, u32[]{:S(2)}, u32[]{:S(2)}) %collective-permute-start.14) | collective-permute-done | bytes 1048608 | tf_op jit(solution)/shard_map/ppermute | solution.py:33
  227.8 1.0 copy-done.7
  228.8 2.4 multiply_reduce_fusion
  233.7 9.2 %all-to-all-start.2 = ((f32[8,8,128]{2,1,0:T(8,128)}), f32[8,8,128]{2,1,0:T(8,128)S(1)}, u32[]{:S(2)}, u32[]{:S(2)}) async-start(f32[8,8,128]{2,1,0:T(8,128)} %broadcast_in_dim_broadcast_in_dim_broadcast_in_dim.6), calls=%async_computation.2 | async-start | bytes 65536 | tf_op jit(solution)/shard_map/all_to_all | solution.py:66
  242.9 0.7 maximum_select_fusion
  243.6 4.0 %all-to-all-done.2 = f32[8,8,128]{2,1,0:T(8,128)S(1)} async-done(((f32[8,8,128]{2,1,0:T(8,128)}), f32[8,8,128]{2,1,0:T(8,128)S(1)}, u32[]{:S(2)}, u32[]{:S(2)}) %all-to-all-start.2) | async-done | bytes 32800 | tf_op jit(solution)/shard_map/all_to_all | solution.py:66
  248.4 7.2 %all-to-all-start.3 = ((f32[32,8,128]{2,1,0:T(8,128)}), f32[32,8,128]{2,1,0:T(8,128)S(1)}, u32[]{:S(2)}, u32[]{:S(2)}) async-start(f32[32,8,128]{2,1,0:T(8,128)} %broadcast_in_dim_broadcast_in_dim_broadcast_in_dim.7), calls=%async_computation.3 | async-start | bytes 262144 | tf_op jit(solution)/shard_map/all_to_all | solution.py:66
  255.5 1.0 slice_bitcast_fusion
  256.6 8.1 %all-to-all-done.3 = f32[32,8,128]{2,1,0:T(8,128)S(1)} async-done(((f32[32,8,128]{2,1,0:T(8,128)}), f32[32,8,128]{2,1,0:T(8,128)S(1)}, u32[]{:S(2)}, u32[]{:S(2)}) %all-to-all-start.3) | async-done | bytes 131104 | tf_op jit(solution)/shard_map/all_to_all | solution.py:66
  (67 shorter events, 4.1 us)
Async XLA Ops:
  0.6 0.9 copy-start
  0.6 38.6 %copy-start.5 = (bf16[1,256,1024]{2,1,0:T(8,128)(2,1)S(1)}, bf16[1,256,1024]{2,1,0:T(8,128)(2,1)}, u32[]{:S(2)}) copy-start(bf16[1,256,1024]{2,1,0:T(8,128)(2,1)} %param.7) | copy-start | bytes 1572868
  0.7 38.5 %copy-start.6 = (bf16[1,256,1024]{2,1,0:T(8,128)(2,1)S(1)}, bf16[1,256,1024]{2,1,0:T(8,128)(2,1)}, u32[]{:S(2)}) copy-start(bf16[1,256,1024]{2,1,0:T(8,128)(2,1)} %param.8) | copy-start | bytes 1572868
  25.2 10.4 %collective-permute-start.6 = (bf16[256,896]{1,0:T(8,128)(2,1)S(1)}, bf16[256,896]{1,0:T(8,128)(2,1)S(1)}, u32[]{:S(2)}, u32[]{:S(2)}) collective-permute-start(bf16[256,896]{1,0:T(8,128)(2,1)S(1)} %bitcast.66), channel_id=1, source_target_pairs={{0,192},{64,0},{128,64},{192,128},{1,193},{65,1},{129,65},{193,129... | collective-permute-start | bytes 1376264 | tf_op jit(solution)/shard_map/ppermute | solution.py:38
  27.9 11.2 %collective-permute-start.4 = (bf16[256,896]{1,0:T(8,128)(2,1)S(1)}, bf16[256,896]{1,0:T(8,128)(2,1)S(1)}, u32[]{:S(2)}, u32[]{:S(2)}) collective-permute-start(bf16[256,896]{1,0:T(8,128)(2,1)S(1)} %bitcast.67), channel_id=1, source_target_pairs={{0,64},{64,128},{128,192},{192,0},{1,65},{65,129},{129,193},{193,1... | collective-permute-start | bytes 1376264 | tf_op jit(solution)/shard_map/ppermute | solution.py:38
  35.6 6.5 %collective-permute-start.7 = (bf16[128,896]{1,0:T(8,128)(2,1)S(1)}, bf16[128,896]{1,0:T(8,128)(2,1)S(1)}, u32[]{:S(2)}, u32[]{:S(2)}) collective-permute-start(bf16[128,896]{1,0:T(8,128)(2,1)S(1)} %slice.85), channel_id=1, source_target_pairs={{0,192},{64,0},{128,64},{192,128},{1,193},{65,1},{129,65},{193,129... | collective-permute-start | bytes 688136 | tf_op jit(solution)/shard_map/ppermute | solution.py:38
  39.1 6.2 %collective-permute-start.5 = (bf16[128,896]{1,0:T(8,128)(2,1)S(1)}, bf16[128,896]{1,0:T(8,128)(2,1)S(1)}, u32[]{:S(2)}, u32[]{:S(2)}) collective-permute-start(bf16[128,896]{1,0:T(8,128)(2,1)S(1)} %slice.84), channel_id=1, source_target_pairs={{0,64},{64,128},{128,192},{192,0},{1,65},{65,129},{129,193},{193,1... | collective-permute-start | bytes 688136 | tf_op jit(solution)/shard_map/ppermute | solution.py:38
  39.3 34.5 %collective-permute-start.2 = (bf16[512,1024]{1,0:T(8,128)(2,1)S(1)}, bf16[512,1024]{1,0:T(8,128)(2,1)}, u32[]{:S(2)}, u32[]{:S(2)}) collective-permute-start(bf16[512,1024]{1,0:T(8,128)(2,1)S(1)} %pad_maximum_fusion.1), channel_id=1, source_target_pairs={{0,4},{4,8},{8,12},{12,16},{16,20},{20,24},{24,28},{28,32},{32,36}... | collective-permute-start | bytes 3145736 | tf_op jit(solution)/shard_map/ppermute | solution.py:33
  45.6 51.9 %copy-start.1 = (bf16[4,256,896]{2,1,0:T(8,128)(2,1)}, bf16[4,256,896]{2,1,0:T(8,128)(2,1)S(1)}, u32[]{:S(2)}) copy-start(bf16[4,256,896]{2,1,0:T(8,128)(2,1)S(1)} %pad_maximum_fusion.wa_ref) | copy-start | bytes 5505028
  47.2 30.1 %collective-permute-start.9 = (bf16[4,128,896]{2,1,0:T(8,128)(2,1)}, bf16[4,128,896]{2,1,0:T(8,128)(2,1)}, u32[]{:S(2)}, u32[]{:S(2)}) collective-permute-start(bf16[4,128,896]{2,1,0:T(8,128)(2,1)} %get-tuple-element.50), channel_id=1, source_target_pairs={{0,34},{2,32},{4,36},{6,38},{8,40},{10,42},{12,44},{14,46},{16,48}... | collective-permute-start | bytes 2752520 | tf_op jit(solution)/shard_map/ppermute | solution.py:57
  49.7 35.8 %collective-permute-start.10 = (bf16[4,128,896]{2,1,0:T(8,128)(2,1)}, bf16[4,128,896]{2,1,0:T(8,128)(2,1)}, u32[]{:S(2)}, u32[]{:S(2)}) collective-permute-start(bf16[4,128,896]{2,1,0:T(8,128)(2,1)} %get-tuple-element.49), channel_id=1, source_target_pairs={{0,34},{2,32},{4,38},{6,36},{8,42},{10,40},{12,46},{14,44},{16,50}... | collective-permute-start | bytes 2752520 | tf_op jit(solution)/shard_map/ppermute | solution.py:57
  49.9 74.5 %collective-permute-start.8 = (bf16[4,256,896]{2,1,0:T(8,128)(2,1)S(1)}, bf16[4,256,896]{2,1,0:T(8,128)(2,1)}, u32[]{:S(2)}, u32[]{:S(2)}) collective-permute-start(bf16[4,256,896]{2,1,0:T(8,128)(2,1)S(1)} %pad_maximum_fusion.wa_ref), channel_id=1, source_target_pairs={{0,1},{1,0},{2,3},{3,2},{4,5},{5,4},{6,7},{7,6},{8,9},{9,8},{10,11... | collective-permute-start | bytes 5505032 | tf_op jit(solution)/shard_map/ppermute | solution.py:61
  73.8 39.5 %collective-permute-start.3 = (bf16[512,1024]{1,0:T(8,128)(2,1)}, bf16[512,1024]{1,0:T(8,128)(2,1)S(1)}, u32[]{:S(2)}, u32[]{:S(2)}) collective-permute-start(bf16[512,1024]{1,0:T(8,128)(2,1)} %collective-permute-done.2.h1_ref), channel_id=1, source_target_pairs={{0,4},{4,8},{8,12},{12,16},{16,20},{20,24},{24,28},{28,32},{32,36}... | collective-permute-start | bytes 3145736 | tf_op jit(solution)/shard_map/ppermute | solution.py:33
  75.8 23.7 %collective-permute-start = (f32[1]{0:T(128)}, f32[1]{0:T(128)}, u32[]{:S(2)}, u32[]{:S(2)}) collective-permute-start(f32[1]{0:T(128)} %bitcast.1), channel_id=1, source_target_pairs={{0,1},{1,0},{2,3},{3,2},{4,5},{5,4},{6,7},{7,6},{8,9},{9,8},{10,11... | collective-permute-start | bytes 20 | tf_op jit(solution)/shard_map/ppermute | solution.py:61
  77.3 50.6 %collective-permute-start.11 = (bf16[4,128,896]{2,1,0:T(8,128)(2,1)}, bf16[4,128,896]{2,1,0:T(8,128)(2,1)}, u32[]{:S(2)}, u32[]{:S(2)}) collective-permute-start(bf16[4,128,896]{2,1,0:T(8,128)(2,1)} %collective-permute-done.9.wbl_ref), channel_id=1, source_target_pairs={{0,1},{1,0},{2,3},{3,2},{4,5},{5,4},{6,7},{7,6},{8,9},{9,8},{10,11... | collective-permute-start | bytes 2752520 | tf_op jit(solution)/shard_map/ppermute | solution.py:61
  85.5 42.6 %collective-permute-start.12 = (bf16[4,128,896]{2,1,0:T(8,128)(2,1)}, bf16[4,128,896]{2,1,0:T(8,128)(2,1)}, u32[]{:S(2)}, u32[]{:S(2)}) collective-permute-start(bf16[4,128,896]{2,1,0:T(8,128)(2,1)} %collective-permute-done.10.wbh_ref), channel_id=1, source_target_pairs={{0,1},{1,0},{2,3},{3,2},{4,5},{5,4},{6,7},{7,6},{8,9},{9,8},{10,11... | collective-permute-start | bytes 2752520 | tf_op jit(solution)/shard_map/ppermute | solution.py:61
  99.5 27.3 %copy-start.3 = (bf16[256,896]{1,0:T(8,128)(2,1)}, bf16[256,896]{1,0:T(8,128)(2,1)S(1)}, u32[]{:S(2)}) copy-start(bf16[256,896]{1,0:T(8,128)(2,1)S(1)} %get-tuple-element.61.m_own_ref) | copy-start | bytes 1376260
  100.1 4.1 %collective-permute-start.1 = (f32[1]{0:T(128)}, f32[1]{0:T(128)}, u32[]{:S(2)}, u32[]{:S(2)}) collective-permute-start(f32[1]{0:T(128)} %add.53), channel_id=1, source_target_pairs={{0,2},{2,0},{1,3},{3,1},{4,6},{6,4},{5,7},{7,5},{8,10},{10,8},{9,1... | collective-permute-start | bytes 20 | tf_op jit(solution)/shard_map/ppermute | solution.py:61
  104.2 20.2 %collective-permute-start.19 = (bf16[256,896]{1,0:T(8,128)(2,1)}, bf16[256,896]{1,0:T(8,128)(2,1)}, u32[]{:S(2)}, u32[]{:S(2)}) collective-permute-start(bf16[256,896]{1,0:T(8,128)(2,1)} %get-tuple-element.60.m_oth_ref), channel_id=1, source_target_pairs={{0,1},{1,0},{2,3},{3,2},{4,5},{5,4},{6,7},{7,6},{8,9},{9,8},{10,11... | collective-permute-start | bytes 1376264 | tf_op jit(solution)/shard_map/ppermute | solution.py:61
  113.3 1.1 copy-start.2
  122.1 18.9 %collective-permute-start.15 = (bf16[512,256]{1,0:T(8,128)(2,1)}, bf16[512,256]{1,0:T(8,128)(2,1)S(1)}, u32[]{:S(2)}, u32[]{:S(2)}) collective-permute-start(bf16[512,256]{1,0:T(8,128)(2,1)} %get-tuple-element.53), channel_id=1, source_target_pairs={{0,64},{64,128},{128,192},{192,0},{1,65},{65,129},{129,193},{193,1... | collective-permute-start | bytes 786440 | tf_op jit(solution)/shard_map/ppermute | solution.py:38
  124.4 16.7 %collective-permute-start.16 = (bf16[512,256]{1,0:T(8,128)(2,1)S(1)}, bf16[512,256]{1,0:T(8,128)(2,1)}, u32[]{:S(2)}, u32[]{:S(2)}) collective-permute-start(bf16[512,256]{1,0:T(8,128)(2,1)S(1)} %get-tuple-element.52), channel_id=1, source_target_pairs={{0,128},{64,192},{128,0},{192,64},{1,129},{65,193},{129,1},{193,65... | collective-permute-start | bytes 786440 | tf_op jit(solution)/shard_map/ppermute | solution.py:38
  124.4 16.7 %collective-permute-start.17 = (bf16[512,256]{1,0:T(8,128)(2,1)S(1)}, bf16[512,256]{1,0:T(8,128)(2,1)S(1)}, u32[]{:S(2)}, u32[]{:S(2)}) collective-permute-start(bf16[512,256]{1,0:T(8,128)(2,1)S(1)} %get-tuple-element.51), channel_id=1, source_target_pairs={{0,192},{64,0},{128,64},{192,128},{1,193},{65,1},{129,65},{193,129... | collective-permute-start | bytes 786440 | tf_op jit(solution)/shard_map/ppermute | solution.py:38
  127.9 13.1 %copy-start.9 = (bf16[512,896]{1,0:T(8,128)(2,1)}, bf16[512,896]{1,0:T(8,128)(2,1)S(1)}, u32[]{:S(2)}) copy-start(bf16[512,896]{1,0:T(8,128)(2,1)S(1)} %pad_maximum_fusion.3.m0_ref) | copy-start | bytes 2752516
  128.0 28.8 %collective-permute-start.20 = (bf16[512,896]{1,0:T(8,128)(2,1)S(1)}, bf16[512,896]{1,0:T(8,128)(2,1)}, u32[]{:S(2)}, u32[]{:S(2)}) collective-permute-start(bf16[512,896]{1,0:T(8,128)(2,1)S(1)} %pad_maximum_fusion.3.m0_ref), channel_id=1, source_target_pairs={{0,64},{64,128},{128,192},{192,0},{1,65},{65,129},{129,193},{193,1... | collective-permute-start | bytes 2752520 | tf_op jit(solution)/shard_map/ppermute | solution.py:38
  128.1 30.9 %collective-permute-start.21 = (bf16[512,896]{1,0:T(8,128)(2,1)S(1)}, bf16[512,896]{1,0:T(8,128)(2,1)}, u32[]{:S(2)}, u32[]{:S(2)}) collective-permute-start(bf16[512,896]{1,0:T(8,128)(2,1)S(1)} %pad_maximum_fusion.3.m0_ref), channel_id=1, source_target_pairs={{0,192},{64,0},{128,64},{192,128},{1,193},{65,1},{129,65},{193,129... | collective-permute-start | bytes 2752520 | tf_op jit(solution)/shard_map/ppermute | solution.py:38
  141.1 0.7 copy-start.10
  143.0 28.9 %copy-start.8 = (bf16[4,512,256]{2,1,0:T(8,128)(2,1)}, bf16[4,512,256]{2,1,0:T(8,128)(2,1)S(1)}, u32[]{:S(2)}) copy-start(bf16[4,512,256]{2,1,0:T(8,128)(2,1)S(1)} %pad_maximum_fusion.2.a_own_ref) | copy-start | bytes 3145732
  143.0 28.9 %collective-permute-start.18 = (bf16[4,512,256]{2,1,0:T(8,128)(2,1)S(1)}, bf16[4,512,256]{2,1,0:T(8,128)(2,1)S(1)}, u32[]{:S(2)}, u32[]{:S(2)}) collective-permute-start(bf16[4,512,256]{2,1,0:T(8,128)(2,1)S(1)} %pad_maximum_fusion.2.a_own_ref), channel_id=1, source_target_pairs={{0,1},{1,0},{2,3},{3,2},{4,5},{5,4},{6,7},{7,6},{8,9},{9,8},{10,11... | collective-permute-start | bytes 3145736 | tf_op jit(solution)/shard_map/ppermute | solution.py:61
  157.9 12.5 %collective-permute-start.22 = (bf16[256,896]{1,0:T(8,128)(2,1)S(1)}, bf16[256,896]{1,0:T(8,128)(2,1)S(1)}, u32[]{:S(2)}, u32[]{:S(2)}) collective-permute-start(bf16[256,896]{1,0:T(8,128)(2,1)S(1)} %slice.90), channel_id=1, source_target_pairs={{0,64},{64,128},{128,192},{192,0},{1,65},{65,129},{129,193},{193,1... | collective-permute-start | bytes 1376264 | tf_op jit(solution)/shard_map/ppermute | solution.py:38
  160.1 11.0 %collective-permute-start.23 = (bf16[256,896]{1,0:T(8,128)(2,1)S(1)}, bf16[256,896]{1,0:T(8,128)(2,1)S(1)}, u32[]{:S(2)}, u32[]{:S(2)}) collective-permute-start(bf16[256,896]{1,0:T(8,128)(2,1)S(1)} %slice.91), channel_id=1, source_target_pairs={{0,192},{64,0},{128,64},{192,128},{1,193},{65,1},{129,65},{193,129... | collective-permute-start | bytes 1376264 | tf_op jit(solution)/shard_map/ppermute | solution.py:38
  161.8 37.1 %collective-permute-start.13 = (bf16[512,1024]{1,0:T(8,128)(2,1)}, bf16[512,1024]{1,0:T(8,128)(2,1)S(1)}, u32[]{:S(2)}, u32[]{:S(2)}) collective-permute-start(bf16[512,1024]{1,0:T(8,128)(2,1)} %get-tuple-element.39), channel_id=1, source_target_pairs={{4,0},{8,4},{12,8},{16,12},{20,16},{24,20},{28,24},{32,28},{36,32}... | collective-permute-start | bytes 3145736 | tf_op jit(solution)/shard_map/ppermute | solution.py:33
  170.4 0.8 copy-start.12
  171.1 0.8 copy-start.13
  171.9 1.0 copy-start.11
  180.1 10.6 %collective-permute-start.26 = (bf16[128,896]{1,0:T(8,128)(2,1)S(1)}, bf16[128,896]{1,0:T(8,128)(2,1)S(1)}, u32[]{:S(2)}, u32[]{:S(2)}) collective-permute-start(bf16[128,896]{1,0:T(8,128)(2,1)S(1)} %get-tuple-element.58), channel_id=1, source_target_pairs={{0,34},{32,0},{2,32},{34,2},{1,35},{33,1},{3,33},{35,3},{4,38},{36... | collective-permute-start | bytes 688136 | tf_op jit(solution)/shard_map/ppermute | solution.py:43
  180.2 10.6 %collective-permute-start.25 = (bf16[128,896]{1,0:T(8,128)(2,1)S(1)}, bf16[128,896]{1,0:T(8,128)(2,1)S(1)}, u32[]{:S(2)}, u32[]{:S(2)}) collective-permute-start(bf16[128,896]{1,0:T(8,128)(2,1)S(1)} %get-tuple-element.59), channel_id=1, source_target_pairs={{0,2},{32,34},{2,0},{34,32},{1,3},{33,35},{3,1},{35,33},{4,6},{36,... | collective-permute-start | bytes 688136 | tf_op jit(solution)/shard_map/ppermute | solution.py:43
  181.8 11.8 %collective-permute-start.24 = (bf16[128,896]{1,0:T(8,128)(2,1)S(1)}, bf16[128,896]{1,0:T(8,128)(2,1)S(1)}, u32[]{:S(2)}, u32[]{:S(2)}) collective-permute-start(bf16[128,896]{1,0:T(8,128)(2,1)S(1)} %get-tuple-element.57), channel_id=1, source_target_pairs={{0,32},{32,2},{2,34},{34,0},{1,33},{33,3},{3,35},{35,1},{4,36},{36... | collective-permute-start | bytes 688136 | tf_op jit(solution)/shard_map/ppermute | solution.py:43
  195.3 33.5 %copy-start.4 = (f32[512,1024]{1,0:T(8,128)S(1)}, f32[512,1024]{1,0:T(8,128)}, u32[]{:S(2)}) copy-start(f32[512,1024]{1,0:T(8,128)} %get-tuple-element.37) | copy-start | bytes 6291460
  195.3 13.1 %all-to-all-start.1 = ((bf16[8,16,896]{2,1,0:T(8,128)(2,1)}), bf16[8,16,896]{2,1,0:T(8,128)(2,1)S(1)}, u32[]{:S(2)}, u32[]{:S(2)}) async-start(bf16[8,16,896]{2,1,0:T(8,128)(2,1)} %bitcast.72), calls=%async_computation.1 | async-start | bytes 458752 | tf_op jit(solution)/shard_map/all_to_all | solution.py:383
  201.5 26.3 %collective-permute-start.14 = (bf16[512,1024]{1,0:T(8,128)(2,1)}, bf16[512,1024]{1,0:T(8,128)(2,1)S(1)}, u32[]{:S(2)}, u32[]{:S(2)}) collective-permute-start(bf16[512,1024]{1,0:T(8,128)(2,1)} %add_convert_fusion), channel_id=1, source_target_pairs={{4,0},{8,4},{12,8},{16,12},{20,16},{24,20},{28,24},{32,28},{36,32}... | collective-permute-start | bytes 3145736 | tf_op jit(solution)/shard_map/ppermute | solution.py:33
  209.1 3.8 %collective-permute-start.27 = (f32[16,896]{1,0:T(8,128)S(1)}, f32[16,896]{1,0:T(8,128)S(1)}, u32[]{:S(2)}, u32[]{:S(2)}) collective-permute-start(f32[16,896]{1,0:T(8,128)S(1)} %get-tuple-element.46), channel_id=1, source_target_pairs={{0,1},{1,0},{2,3},{3,2},{4,5},{5,4},{6,7},{7,6},{8,9},{9,8},{10,11... | collective-permute-start | bytes 172040 | tf_op jit(solution)/shard_map/ppermute | solution.py:61
  212.9 30.0 %collective-permute-start.28 = (f32[16,1792]{1,0:T(8,128)S(1)}, f32[16,1792]{1,0:T(8,128)S(1)}, u32[]{:S(2)}, u32[]{:S(2)}) collective-permute-start(f32[16,1792]{1,0:T(8,128)S(1)} %maximum_select_fusion.1), channel_id=1, source_target_pairs={{0,2},{2,0},{1,3},{3,1},{4,6},{6,4},{5,7},{7,5},{8,10},{10,8},{9,1... | collective-permute-start | bytes 344072 | tf_op jit(solution)/shard_map/ppermute | solution.py:61
  227.8 1.0 copy-start.7
  233.7 13.9 %all-to-all-start.2 = ((f32[8,8,128]{2,1,0:T(8,128)}), f32[8,8,128]{2,1,0:T(8,128)S(1)}, u32[]{:S(2)}, u32[]{:S(2)}) async-start(f32[8,8,128]{2,1,0:T(8,128)} %broadcast_in_dim_broadcast_in_dim_broadcast_in_dim.6), calls=%async_computation.2 | async-start | bytes 65536 | tf_op jit(solution)/shard_map/all_to_all | solution.py:66
  248.4 16.3 %all-to-all-start.3 = ((f32[32,8,128]{2,1,0:T(8,128)}), f32[32,8,128]{2,1,0:T(8,128)S(1)}, u32[]{:S(2)}, u32[]{:S(2)}) async-start(f32[32,8,128]{2,1,0:T(8,128)} %broadcast_in_dim_broadcast_in_dim_broadcast_in_dim.7), calls=%async_computation.3 | async-start | bytes 262144 | tf_op jit(solution)/shard_map/all_to_all | solution.py:66

commit v3 on v2

--- a/solution.py
+++ b/solution.py
@@ -185,17 +185,12 @@
         ].T.astype(BF16)
 
 
-def weight_kernel(at_ref, a_own_ref, a_oth_ref, m0_ref, m1_ref, m3_ref, m2a_ref, m2b_ref, out_ref):
+def weight_kernel(at_ref, a_own_ref, a_oth_ref, m0_ref, m1_ref, m2_ref, m3_ref, out_ref):
     acc = None
-    for back, (own, oth) in enumerate(
-        (
-            (m0_ref[:TOK_DEV], m0_ref[TOK_DEV:]),
-            (m1_ref[:TOK_DEV], m1_ref[TOK_DEV:]),
-            (m2a_ref[...], m2b_ref[...]),
-            (m3_ref[:TOK_DEV], m3_ref[TOK_DEV:]),
+    for back, m_ref in enumerate((m0_ref, m1_ref, m2_ref, m3_ref)):
+        both = dot(a_own_ref[back], m_ref[:TOK_DEV], NN) + dot(
+            a_oth_ref[back], m_ref[TOK_DEV:], NN
         )
-    ):
-        both = dot(a_own_ref[back], own, NN) + dot(a_oth_ref[back], oth, NN)
         acc = both if acc is None else acc + both
     acc = acc.reshape(2, 8, 2, 16, HALF)
     for low in range(2):
@@ -288,18 +283,18 @@
     )(scale, q, k, v, h1, h2, p, pf, g, delta, dscore)
 
 
-def weight_product(where, a_own, a_oth, m0, m1, m3, m2a, m2b):
+def weight_product(where, a_own, a_oth, m0, m1, m2, m3):
     vmem = pl.BlockSpec(memory_space=pltpu.VMEM)
     return pl.pallas_call(
         weight_kernel,
-        in_specs=[pl.BlockSpec(memory_space=pltpu.SMEM)] + [vmem] * 7,
+        in_specs=[pl.BlockSpec(memory_space=pltpu.SMEM)] + [vmem] * 6,
         out_specs=vmem,
         out_shape=jax.ShapeDtypeStruct((4, 128, HALF), BF16),
         cost_estimate=pl.CostEstimate(
             flops=2 * 512 * HALF * 2048, transcendentals=0, bytes_accessed=7 << 20
         ),
         name="weight_product",
-    )(where, a_own, a_oth, m0, m1, m3, m2a, m2b)
+    )(where, a_own, a_oth, m0, m1, m2, m3)
 
 
 def all_steps(queries, keys, values, out_grad, out_weight, seq_len):
@@ -333,8 +328,7 @@
     m0 = jnp.concatenate([m_own, swap(m_oth, "dp_1")], 0)
     m1 = ring(m0, "seq_0", 1)
     m3 = ring(m0, "seq_0", -1)
-    m2a = ring(m1[:TOK_DEV], "seq_0", 1)
-    m2b = ring(m3[TOK_DEV:], "seq_0", -1)
+    m2 = ring(m3, "seq_0", -1)
 
     w_z = for_each(half_of(out_weight, core), "seq_2").reshape(HEAD_DIM, HALF)
     w_up = ring(w_z, "seq_0", 1)
@@ -368,11 +362,12 @@
     )
     r2 = shifted((d1.astype(F32) + r1.astype(F32)).astype(BF16), -1)
     dkv = d0 + r2.astype(F32)
-    square = jnp.sum(dkv * dkv) + jnp.sum(dq_sq.reshape(KV_HEADS, 8, 128)[:, 0, 0])
+    square = jnp.sum(dkv * dkv)
+    square = square + jnp.sum(dq_sq.reshape(KV_HEADS, 8, 128)[:, 0, 0])
     dkv = dkv.astype(BF16)
 
     part = weight_product(
-        where, a_own, a_oth, m0, m1, m3, m2a, m2b
+        where, a_own, a_oth, m0, m1, m2, m3
     )
     part = (
         part[0].astype(F32)

time: 267 us -> 271 us (1.015)
  waiting for transfers between devices: 67.2 us -> 114 us
  starting transfers between devices: 100 us -> 60 us
  local copies, waits for them, and re-layouts: 16.8 us -> 13.1 us
    ppermute x9, starting transfers between devices: 52.5 us -> 16.8 us  [swap(): return lax.ppermute(value, axis, [(0, 1), (1, 0)])]
    ppermute x2, waiting for transfers between devices: 0.01 us -> 30.4 us  [across_x(): return lax.ppermute(value, ('seq_1', 'seq_2', 'dp_0'), pairs)]
    ppermute x11 -> x10, waiting for transfers between devices: 32 us -> 47 us  [ring(): lax.ppermute(value, axis, [(s, (s + steps) % count) for s in range(count)])]
    all_to_all x2, starting transfers between devices: 16.4 us -> 12.1 us  [for_each(): lax.all_to_all(jnp.broadcast_to(value[None], (size, *value.shape)), axis,...]
    unnamed x28 -> x20, local copies, waits for them, and re-layouts: 5.5 us -> 4.7 us
    ppermute x11 -> x10, starting transfers between devices: 16.6 us -> 15.9 us  [ring(): lax.ppermute(value, axis, [(s, (s + steps) % count) for s in range(count)])]
  transfers between devices with their start and end apart: 32 -> 31, of which waited for: 12 -> 12; matrix products, arithmetic and copies ran while one was open for 10% -> 9% of each run, Pallas kernels for 14% -> 14%
where the time goes in v3:
time: 271 us; the launch traced here: 270 us
  waiting for transfers between devices  114 us (42%)
  starting transfers between devices  60 us (22%)
  Pallas kernels  37.1 us (14%)
  blocking collectives  23.6 us (9%)
  other arithmetic  16.1 us (6%)
  local copies, waits for them, and re-layouts  13.1 us (5%)
  between operations  6.06 us (2%)
    ppermute x10, waiting for transfers between devices, ring(): lax.ppermute(value, axis, [(s, (s + steps) % count) for s in range(count)])  47 us
    ppermute x2, waiting for transfers between devices, across_x(): return lax.ppermute(value, ('seq_1', 'seq_2', 'dp_0'), pairs)  30.4 us
    all_to_all x1, blocking collectives, for_each(): lax.all_to_all(jnp.broadcast_to(value[None], (size, *value.shape)), axis,...  23.6 us
    ppermute x9, starting transfers between devices, swap(): return lax.ppermute(value, axis, [(0, 1), (1, 0)])  16.8 us
    ppermute x10, starting transfers between devices, ring(): lax.ppermute(value, axis, [(s, (s + steps) % count) for s in range(count)])  15.9 us
    ppermute x4, waiting for transfers between devices, shifted(): lax.ppermute(value, SEQ, [(source, source + steps) for source in range(in...  14 us
    all_to_all x2, waiting for transfers between devices, for_each(): lax.all_to_all(jnp.broadcast_to(value[None], (size, *value.shape)), axis,...  12.1 us
    all_to_all x2, starting transfers between devices, for_each(): lax.all_to_all(jnp.broadcast_to(value[None], (size, *value.shape)), axis,...  12.1 us
  transfers between devices with their start and end apart: 31, of which 12 were waited for; matrix products, arithmetic and copies ran while one was open for 9% of the time, Pallas kernels for 14%

profile of v3, /device:TPU:1, one launch (start us, length us, event | category | flops | bytes accessed | tf_op | source)
XLA Modules:
  0.0 269.8 jit_solution(2622816038512390281)
XLA Ops:
  0.7 0.9 copy-done
  1.6 23.6 %all_to_all.24 = bf16[8,32,896]{2,1,0:T(8,128)(2,1)S(1)} all-to-all(bf16[8,32,896]{2,1,0:T(8,128)(2,1)S(1)} %broadcast_in_dim.30), channel_id=1, replica_groups=mesh['seq_0'=4,'seq_1'=2,'seq_2'=8,'dp_0'=2,'dp_1'=2] {'seq_2'}, dimensions={0} | all-to-all | bytes 917504 | tf_op jit(solution)/shard_map/all_to_all | solution.py:66
  25.2 2.7 %collective-permute-start.6 = (bf16[256,896]{1,0:T(8,128)(2,1)S(1)}, bf16[256,896]{1,0:T(8,128)(2,1)S(1)}, u32[]{:S(2)}, u32[]{:S(2)}) collective-permute-start(bf16[256,896]{1,0:T(8,128)(2,1)S(1)} %bitcast.66), channel_id=1, source_target_pairs={{0,192},{64,0},{128,64},{192,128},{1,193},{65,1},{129,65},{193,129... | collective-permute-start | bytes 1376264 | tf_op jit(solution)/shard_map/ppermute | solution.py:38
  27.9 1.3 pad_maximum_fusion.1
  29.2 2.5 collective-permute-start.2
  31.7 3.8 %collective-permute-done.6 = bf16[256,896]{1,0:T(8,128)(2,1)S(1)} collective-permute-done((bf16[256,896]{1,0:T(8,128)(2,1)S(1)}, bf16[256,896]{1,0:T(8,128)(2,1)S(1)}, u32[]{:S(2)}, u32[]{:S(2)}) %collective-permute-start.6) | collective-permute-done | bytes 458784 | tf_op jit(solution)/shard_map/ppermute | solution.py:38
  35.6 3.5 %collective-permute-start.7 = (bf16[128,896]{1,0:T(8,128)(2,1)S(1)}, bf16[128,896]{1,0:T(8,128)(2,1)S(1)}, u32[]{:S(2)}, u32[]{:S(2)}) collective-permute-start(bf16[128,896]{1,0:T(8,128)(2,1)S(1)} %slice.77), channel_id=1, source_target_pairs={{0,192},{64,0},{128,64},{192,128},{1,193},{65,1},{129,65},{193,129... | collective-permute-start | bytes 688136 | tf_op jit(solution)/shard_map/ppermute | solution.py:38
  39.1 19.0 %collective-permute-done.4 = bf16[256,896]{1,0:T(8,128)(2,1)S(1)} collective-permute-done((bf16[256,896]{1,0:T(8,128)(2,1)S(1)}, bf16[256,896]{1,0:T(8,128)(2,1)S(1)}, u32[]{:S(2)}, u32[]{:S(2)}) %collective-permute-start.4) | collective-permute-done | bytes 458784 | tf_op jit(solution)/shard_map/ppermute | solution.py:38
  58.1 2.3 collective-permute-start.5
  60.3 3.9 %collective-permute-done.5 = bf16[128,896]{1,0:T(8,128)(2,1)S(1)} collective-permute-done((bf16[128,896]{1,0:T(8,128)(2,1)S(1)}, bf16[128,896]{1,0:T(8,128)(2,1)S(1)}, u32[]{:S(2)}, u32[]{:S(2)}) %collective-permute-start.5) | collective-permute-done | bytes 229408 | tf_op jit(solution)/shard_map/ppermute | solution.py:38
  64.6 5.4 %collective-permute-start.8 = (bf16[4,256,896]{2,1,0:T(8,128)(2,1)S(1)}, bf16[4,256,896]{2,1,0:T(8,128)(2,1)}, u32[]{:S(2)}, u32[]{:S(2)}) collective-permute-start(bf16[4,256,896]{2,1,0:T(8,128)(2,1)S(1)} %pad_maximum_fusion.wa_ref), channel_id=1, source_target_pairs={{0,1},{1,0},{2,3},{3,2},{4,5},{5,4},{6,7},{7,6},{8,9},{9,8},{10,11... | collective-permute-start | bytes 5505032 | tf_op jit(solution)/shard_map/ppermute | solution.py:61
  69.9 1.4 fusion.4
  71.4 2.7 collective-permute-start.10
  74.7 1.8 collective-permute-start
  76.5 1.3 collective-permute-start.3
  77.9 2.2 bitcast_select_fusion
  80.1 2.0 constant_dynamic-slice_fusion.1
  82.1 12.5 %collective-permute-done.9.wbl_ref = bf16[4,128,896]{2,1,0:T(8,128)(2,1)} collective-permute-done((bf16[4,128,896]{2,1,0:T(8,128)(2,1)}, bf16[4,128,896]{2,1,0:T(8,128)(2,1)}, u32[]{:S(2)}, u32[]{:S(2)}) %collective-permute-start.9) | collective-permute-done | bytes 917536 | tf_op jit(solution)/shard_map/ppermute | solution.py:57
  94.6 1.7 collective-permute-start.11
  96.3 17.9 %collective-permute-done.10.wbh_ref = bf16[4,128,896]{2,1,0:T(8,128)(2,1)} collective-permute-done((bf16[4,128,896]{2,1,0:T(8,128)(2,1)}, bf16[4,128,896]{2,1,0:T(8,128)(2,1)}, u32[]{:S(2)}, u32[]{:S(2)}) %collective-permute-start.10) | collective-permute-done | bytes 917536 | tf_op jit(solution)/shard_map/ppermute | solution.py:57
  114.3 1.1 collective-permute-start.12
  116.5 2.1 pad_maximum_fusion.3.m0_ref
  118.6 1.7 collective-permute-start.21
  120.3 6.8 %shard_map.101 = (bf16[4,512,512]{2,1,0:T(8,128)(2,1)}, bf16[4,512,512]{2,1,0:T(8,128)(2,1)}, f32[4,256,512]{2,1,0:T(8,128)}, f32[4,8,512]{2,1,0:T(8,128)}) custom-call(s32[4]{0:T(128)} %pad_add_fusion.at_ref, bf16[256,2048]{1,0:T(8,128)(2,1)} %bitcast.56, bf16[256,1024]{1,0:T(8,128)(2,1)} %bitcast.61, bf16[256,1024]{1,0:T(8,128)(2,1)} %bitcast.64, ...), custom_call_target="tpu_custom_call" | custom-call | flops 1073741824 | bytes 9437184 | tf_op jit(solution)/shard_map/pallas_call | solution.py:240
  127.2 2.3 collective-permute-start.1
  129.5 5.9 %shard_map.102 = (bf16[4,256,512]{2,1,0:T(8,128)(2,1)}, bf16[4,256,512]{2,1,0:T(8,128)(2,1)}, bf16[4,512,256]{2,1,0:T(8,128)(2,1)}, f32[4,8,512]{2,1,0:T(8,128)}) custom-call(s32[4]{0:T(128)} %pad_add_fusion.at_ref, bf16[256,2048]{1,0:T(8,128)(2,1)} %bitcast.57, bf16[512,1024]{1,0:T(8,128)(2,1)} %copy-done.2, f32[4,256,512]{2,1,0:T(8,128)} %get-tuple-element.27.acc_ref, ...), custom_call_target="tpu_custom_call" | custom-call | flops 536870912 | bytes 7340032 | tf_op jit(solution)/shard_map/pallas_call | solution.py:251
  135.4 1.3 slice_bitcast_fusion.2
  136.8 1.1 collective-permute-start.16
  137.9 1.6 collective-permute-start.17
  140.3 10.3 %shard_map.103 = (bf16[512,1024]{1,0:T(8,128)(2,1)}, bf16[4,256,512]{2,1,0:T(8,128)(2,1)}, f32[4,8,512]{2,1,0:T(8,128)}, bf16[4,256,512]{2,1,0:T(8,128)(2,1)}) custom-call(s32[4]{0:T(128)} %pad_add_fusion.at_ref, f32[1]{0:T(128)S(6)} %div.6.scale_ref, bf16[256,2048]{1,0:T(8,128)(2,1)} %bitcast.58, bf16[512,1024]{1,0:T(8,128)(2,1)} %copy-done.2, ...), custom_call_target="tpu_custom_call" | custom-call | flops 2684354560 | bytes 15728640 | tf_op jit(solution)/shard_map/pallas_call | solution.py:264
  150.6 0.9 collective-permute-done.17
  151.6 1.5 collective-permute-start.18
  153.2 0.7 collective-permute-start.20
  153.9 2.1 collective-permute-start.22
  156.0 1.3 collective-permute-start.13
  157.3 19.4 %collective-permute-done.20.m1_ref = bf16[512,896]{1,0:T(8,128)(2,1)S(1)} collective-permute-done((bf16[512,896]{1,0:T(8,128)(2,1)}, bf16[512,896]{1,0:T(8,128)(2,1)S(1)}, u32[]{:S(2)}, u32[]{:S(2)}) %collective-permute-start.20) | collective-permute-done | bytes 917536 | tf_op jit(solution)/shard_map/ppermute | solution.py:38
  176.7 0.9 copy-done.8
  177.6 0.9 copy-done.9
  178.6 1.0 copy-done.7
  179.5 5.9 %weight_product.1 = bf16[4,128,896]{2,1,0:T(8,128)(2,1)} custom-call(s32[4]{0:T(128)} %pad_add_fusion.at_ref, bf16[4,512,256]{2,1,0:T(8,128)(2,1)} %copy-done.6, bf16[4,512,256]{2,1,0:T(8,128)(2,1)} %copy-done.7, bf16[512,896]{1,0:T(8,128)(2,1)} %pad_maximum_fusion.3.m0_ref, bf16[512,896]{1,0:T(8,128)(2,1)} %copy-done.8, bf16[512,896]{1,0:T(8,128)(2,1)} %copy-done.9, ...), custom_call_target="tpu_custom_call" | custom-call | flops 1879048192 | bytes 7340032 | tf_op jit(solution)/shard_map/weight_product/pallas_call | solution.py:288
  185.5 1.2 slice_bitcast_fusion.8
  187.1 1.4 collective-permute-start.24
  188.5 0.8 collective-permute-start.23
  189.2 8.1 %shard_map.104 = (bf16[256,2048]{1,0:T(8,128)(2,1)}, f32[512,1024]{1,0:T(8,128)}, bf16[512,1024]{1,0:T(8,128)(2,1)}, f32[32,128]{1,0:T(8,128)}) custom-call(f32[1]{0:T(128)S(6)} %div.6.scale_ref, bf16[256,2048]{1,0:T(8,128)(2,1)} %bitcast.59, bf16[256,1024]{1,0:T(8,128)(2,1)} %bitcast.62, bf16[256,1024]{1,0:T(8,128)(2,1)} %bitcast.65, ...), custom_call_target="tpu_custom_call" | custom-call | flops 2415919104 | bytes 13631488 | tf_op jit(solution)/shard_map/pallas_call | solution.py:275
  197.4 3.6 %collective-permute-done.23 = bf16[128,896]{1,0:T(8,128)(2,1)S(1)} collective-permute-done((bf16[128,896]{1,0:T(8,128)(2,1)S(1)}, bf16[128,896]{1,0:T(8,128)(2,1)S(1)}, u32[]{:S(2)}, u32[]{:S(2)}) %collective-permute-start.23) | collective-permute-done | bytes 229408 | tf_op jit(solution)/shard_map/ppermute | solution.py:43
  201.0 1.7 fusion.3
  202.7 3.5 %all-to-all-start.1 = ((bf16[8,16,896]{2,1,0:T(8,128)(2,1)}), bf16[8,16,896]{2,1,0:T(8,128)(2,1)S(1)}, u32[]{:S(2)}, u32[]{:S(2)}) async-start(bf16[8,16,896]{2,1,0:T(8,128)(2,1)} %bitcast.72), calls=%async_computation.1 | async-start | bytes 458752 | tf_op jit(solution)/shard_map/all_to_all | solution.py:378
  206.3 2.6 add_convert_fusion
  208.9 1.3 collective-permute-start.14
  210.2 6.6 %all-to-all-done.1 = bf16[8,16,896]{2,1,0:T(8,128)(2,1)S(1)} async-done(((bf16[8,16,896]{2,1,0:T(8,128)(2,1)}), bf16[8,16,896]{2,1,0:T(8,128)(2,1)S(1)}, u32[]{:S(2)}, u32[]{:S(2)}) %all-to-all-start.1) | async-done | bytes 229408 | tf_op jit(solution)/shard_map/all_to_all | solution.py:378
  217.5 1.5 collective-permute-start.26
  219.0 1.3 slice_reduce_fusion
  220.3 1.5 collective-permute-start.27
  221.8 14.0 %collective-permute-done.14 = bf16[512,1024]{1,0:T(8,128)(2,1)S(1)} collective-permute-done((bf16[512,1024]{1,0:T(8,128)(2,1)}, bf16[512,1024]{1,0:T(8,128)(2,1)S(1)}, u32[]{:S(2)}, u32[]{:S(2)}) %collective-permute-start.14) | collective-permute-done | bytes 1048608 | tf_op jit(solution)/shard_map/ppermute | solution.py:33
  235.8 1.0 copy-done.5
  236.8 2.4 multiply_reduce_fusion
  241.2 0.6 broadcast_in_dim_broadcast_in_dim_broadcast_in_dim.6
  241.8 4.3 %all-to-all-start.2 = ((f32[8,8,128]{2,1,0:T(8,128)}), f32[8,8,128]{2,1,0:T(8,128)S(1)}, u32[]{:S(2)}, u32[]{:S(2)}) async-start(f32[8,8,128]{2,1,0:T(8,128)} %broadcast_in_dim_broadcast_in_dim_broadcast_in_dim.6), calls=%async_computation.2 | async-start | bytes 65536 | tf_op jit(solution)/shard_map/all_to_all | solution.py:66
  246.1 0.7 maximum_select_fusion
  246.8 4.0 %all-to-all-done.2 = f32[8,8,128]{2,1,0:T(8,128)S(1)} async-done(((f32[8,8,128]{2,1,0:T(8,128)}), f32[8,8,128]{2,1,0:T(8,128)S(1)}, u32[]{:S(2)}, u32[]{:S(2)}) %all-to-all-start.2) | async-done | bytes 32800 | tf_op jit(solution)/shard_map/all_to_all | solution.py:66
  250.8 0.7 broadcast_in_dim_broadcast_in_dim_broadcast_in_dim.7
  251.5 7.8 %all-to-all-start.3 = ((f32[32,8,128]{2,1,0:T(8,128)}), f32[32,8,128]{2,1,0:T(8,128)S(1)}, u32[]{:S(2)}, u32[]{:S(2)}) async-start(f32[32,8,128]{2,1,0:T(8,128)} %broadcast_in_dim_broadcast_in_dim_broadcast_in_dim.7), calls=%async_computation.3 | async-start | bytes 262144 | tf_op jit(solution)/shard_map/all_to_all | solution.py:66
  259.4 1.0 slice_bitcast_fusion
  260.4 8.1 %all-to-all-done.3 = f32[32,8,128]{2,1,0:T(8,128)S(1)} async-done(((f32[32,8,128]{2,1,0:T(8,128)}), f32[32,8,128]{2,1,0:T(8,128)S(1)}, u32[]{:S(2)}, u32[]{:S(2)}) %all-to-all-start.3) | async-done | bytes 131104 | tf_op jit(solution)/shard_map/all_to_all | solution.py:66
  (55 shorter events, 2.4 us)
Async XLA Ops:
  0.6 0.9 copy-start
  25.2 10.4 %collective-permute-start.6 = (bf16[256,896]{1,0:T(8,128)(2,1)S(1)}, bf16[256,896]{1,0:T(8,128)(2,1)S(1)}, u32[]{:S(2)}, u32[]{:S(2)}) collective-permute-start(bf16[256,896]{1,0:T(8,128)(2,1)S(1)} %bitcast.66), channel_id=1, source_target_pairs={{0,192},{64,0},{128,64},{192,128},{1,193},{65,1},{129,65},{193,129... | collective-permute-start | bytes 1376264 | tf_op jit(solution)/shard_map/ppermute | solution.py:38
  27.9 30.1 %collective-permute-start.4 = (bf16[256,896]{1,0:T(8,128)(2,1)S(1)}, bf16[256,896]{1,0:T(8,128)(2,1)S(1)}, u32[]{:S(2)}, u32[]{:S(2)}) collective-permute-start(bf16[256,896]{1,0:T(8,128)(2,1)S(1)} %bitcast.67), channel_id=1, source_target_pairs={{0,64},{64,128},{128,192},{192,0},{1,65},{65,129},{129,193},{193,1... | collective-permute-start | bytes 1376264 | tf_op jit(solution)/shard_map/ppermute | solution.py:38
  29.2 47.3 %collective-permute-start.2 = (bf16[512,1024]{1,0:T(8,128)(2,1)S(1)}, bf16[512,1024]{1,0:T(8,128)(2,1)}, u32[]{:S(2)}, u32[]{:S(2)}) collective-permute-start(bf16[512,1024]{1,0:T(8,128)(2,1)S(1)} %pad_maximum_fusion.1), channel_id=1, source_target_pairs={{0,4},{4,8},{8,12},{12,16},{16,20},{20,24},{24,28},{28,32},{32,36}... | collective-permute-start | bytes 3145736 | tf_op jit(solution)/shard_map/ppermute | solution.py:33
  35.6 24.8 %collective-permute-start.7 = (bf16[128,896]{1,0:T(8,128)(2,1)S(1)}, bf16[128,896]{1,0:T(8,128)(2,1)S(1)}, u32[]{:S(2)}, u32[]{:S(2)}) collective-permute-start(bf16[128,896]{1,0:T(8,128)(2,1)S(1)} %slice.77), channel_id=1, source_target_pairs={{0,192},{64,0},{128,64},{192,128},{1,193},{65,1},{129,65},{193,129... | collective-permute-start | bytes 688136 | tf_op jit(solution)/shard_map/ppermute | solution.py:38
  58.1 6.2 %collective-permute-start.5 = (bf16[128,896]{1,0:T(8,128)(2,1)S(1)}, bf16[128,896]{1,0:T(8,128)(2,1)S(1)}, u32[]{:S(2)}, u32[]{:S(2)}) collective-permute-start(bf16[128,896]{1,0:T(8,128)(2,1)S(1)} %slice.76), channel_id=1, source_target_pairs={{0,64},{64,128},{128,192},{192,0},{1,65},{65,129},{129,193},{193,1... | collective-permute-start | bytes 688136 | tf_op jit(solution)/shard_map/ppermute | solution.py:38
  64.5 15.6 %copy-start.1 = (bf16[4,256,896]{2,1,0:T(8,128)(2,1)}, bf16[4,256,896]{2,1,0:T(8,128)(2,1)S(1)}, u32[]{:S(2)}) copy-start(bf16[4,256,896]{2,1,0:T(8,128)(2,1)S(1)} %pad_maximum_fusion.wa_ref) | copy-start | bytes 5505028
  64.6 72.2 %collective-permute-start.8 = (bf16[4,256,896]{2,1,0:T(8,128)(2,1)S(1)}, bf16[4,256,896]{2,1,0:T(8,128)(2,1)}, u32[]{:S(2)}, u32[]{:S(2)}) collective-permute-start(bf16[4,256,896]{2,1,0:T(8,128)(2,1)S(1)} %pad_maximum_fusion.wa_ref), channel_id=1, source_target_pairs={{0,1},{1,0},{2,3},{3,2},{4,5},{5,4},{6,7},{7,6},{8,9},{9,8},{10,11... | collective-permute-start | bytes 5505032 | tf_op jit(solution)/shard_map/ppermute | solution.py:61
  71.4 23.2 %collective-permute-start.9 = (bf16[4,128,896]{2,1,0:T(8,128)(2,1)}, bf16[4,128,896]{2,1,0:T(8,128)(2,1)}, u32[]{:S(2)}, u32[]{:S(2)}) collective-permute-start(bf16[4,128,896]{2,1,0:T(8,128)(2,1)} %get-tuple-element.50), channel_id=1, source_target_pairs={{0,34},{2,32},{4,36},{6,38},{8,40},{10,42},{12,44},{14,46},{16,48}... | collective-permute-start | bytes 2752520 | tf_op jit(solution)/shard_map/ppermute | solution.py:57
  71.4 42.9 %collective-permute-start.10 = (bf16[4,128,896]{2,1,0:T(8,128)(2,1)}, bf16[4,128,896]{2,1,0:T(8,128)(2,1)}, u32[]{:S(2)}, u32[]{:S(2)}) collective-permute-start(bf16[4,128,896]{2,1,0:T(8,128)(2,1)} %get-tuple-element.49), channel_id=1, source_target_pairs={{0,34},{2,32},{4,38},{6,36},{8,42},{10,40},{12,46},{14,44},{16,50}... | collective-permute-start | bytes 2752520 | tf_op jit(solution)/shard_map/ppermute | solution.py:57
  74.7 7.4 %collective-permute-start = (f32[1]{0:T(128)}, f32[1]{0:T(128)}, u32[]{:S(2)}, u32[]{:S(2)}) collective-permute-start(f32[1]{0:T(128)} %bitcast.1), channel_id=1, source_target_pairs={{0,1},{1,0},{2,3},{3,2},{4,5},{5,4},{6,7},{7,6},{8,9},{9,8},{10,11... | collective-permute-start | bytes 20 | tf_op jit(solution)/shard_map/ppermute | solution.py:61
  76.5 50.6 %collective-permute-start.3 = (bf16[512,1024]{1,0:T(8,128)(2,1)}, bf16[512,1024]{1,0:T(8,128)(2,1)S(1)}, u32[]{:S(2)}, u32[]{:S(2)}) collective-permute-start(bf16[512,1024]{1,0:T(8,128)(2,1)} %collective-permute-done.2.h1_ref), channel_id=1, source_target_pairs={{0,4},{4,8},{8,12},{12,16},{16,20},{20,24},{24,28},{28,32},{32,36}... | collective-permute-start | bytes 3145736 | tf_op jit(solution)/shard_map/ppermute | solution.py:33
  82.1 45.0 %copy-start.3 = (bf16[256,896]{1,0:T(8,128)(2,1)}, bf16[256,896]{1,0:T(8,128)(2,1)S(1)}, u32[]{:S(2)}) copy-start(bf16[256,896]{1,0:T(8,128)(2,1)S(1)} %get-tuple-element.61.m_own_ref) | copy-start | bytes 1376260
  82.1 34.4 %collective-permute-start.19 = (bf16[256,896]{1,0:T(8,128)(2,1)}, bf16[256,896]{1,0:T(8,128)(2,1)}, u32[]{:S(2)}, u32[]{:S(2)}) collective-permute-start(bf16[256,896]{1,0:T(8,128)(2,1)} %get-tuple-element.60.m_oth_ref), channel_id=1, source_target_pairs={{0,1},{1,0},{2,3},{3,2},{4,5},{5,4},{6,7},{7,6},{8,9},{9,8},{10,11... | collective-permute-start | bytes 1376264 | tf_op jit(solution)/shard_map/ppermute | solution.py:61
  94.6 43.3 %collective-permute-start.11 = (bf16[4,128,896]{2,1,0:T(8,128)(2,1)}, bf16[4,128,896]{2,1,0:T(8,128)(2,1)}, u32[]{:S(2)}, u32[]{:S(2)}) collective-permute-start(bf16[4,128,896]{2,1,0:T(8,128)(2,1)} %collective-permute-done.9.wbl_ref), channel_id=1, source_target_pairs={{0,1},{1,0},{2,3},{3,2},{4,5},{5,4},{6,7},{7,6},{8,9},{9,8},{10,11... | collective-permute-start | bytes 2752520 | tf_op jit(solution)/shard_map/ppermute | solution.py:61
  114.3 26.0 %collective-permute-start.12 = (bf16[4,128,896]{2,1,0:T(8,128)(2,1)}, bf16[4,128,896]{2,1,0:T(8,128)(2,1)}, u32[]{:S(2)}, u32[]{:S(2)}) collective-permute-start(bf16[4,128,896]{2,1,0:T(8,128)(2,1)} %collective-permute-done.10.wbh_ref), channel_id=1, source_target_pairs={{0,1},{1,0},{2,3},{3,2},{4,5},{5,4},{6,7},{7,6},{8,9},{9,8},{10,11... | collective-permute-start | bytes 2752520 | tf_op jit(solution)/shard_map/ppermute | solution.py:61
  118.6 35.3 %collective-permute-start.21 = (bf16[512,896]{1,0:T(8,128)(2,1)}, bf16[512,896]{1,0:T(8,128)(2,1)}, u32[]{:S(2)}, u32[]{:S(2)}) collective-permute-start(bf16[512,896]{1,0:T(8,128)(2,1)} %pad_maximum_fusion.3.m0_ref), channel_id=1, source_target_pairs={{0,192},{64,0},{128,64},{192,128},{1,193},{65,1},{129,65},{193,129... | collective-permute-start | bytes 2752520 | tf_op jit(solution)/shard_map/ppermute | solution.py:38
  127.2 2.4 copy-start.2
  127.2 9.5 %collective-permute-start.1 = (f32[1]{0:T(128)}, f32[1]{0:T(128)}, u32[]{:S(2)}, u32[]{:S(2)}) collective-permute-start(f32[1]{0:T(128)} %add.53), channel_id=1, source_target_pairs={{0,2},{2,0},{1,3},{3,1},{4,6},{6,4},{5,7},{7,5},{8,10},{10,8},{9,1... | collective-permute-start | bytes 20 | tf_op jit(solution)/shard_map/ppermute | solution.py:61
  136.7 13.9 %collective-permute-start.15 = (bf16[512,256]{1,0:T(8,128)(2,1)S(1)}, bf16[512,256]{1,0:T(8,128)(2,1)S(1)}, u32[]{:S(2)}, u32[]{:S(2)}) collective-permute-start(bf16[512,256]{1,0:T(8,128)(2,1)S(1)} %get-tuple-element.53), channel_id=1, source_target_pairs={{0,64},{64,128},{128,192},{192,0},{1,65},{65,129},{129,193},{193,1... | collective-permute-start | bytes 786440 | tf_op jit(solution)/shard_map/ppermute | solution.py:38
  136.8 13.8 %collective-permute-start.16 = (bf16[512,256]{1,0:T(8,128)(2,1)S(1)}, bf16[512,256]{1,0:T(8,128)(2,1)S(1)}, u32[]{:S(2)}, u32[]{:S(2)}) collective-permute-start(bf16[512,256]{1,0:T(8,128)(2,1)S(1)} %get-tuple-element.52), channel_id=1, source_target_pairs={{0,128},{64,192},{128,0},{192,64},{1,129},{65,193},{129,1},{193,65... | collective-permute-start | bytes 786440 | tf_op jit(solution)/shard_map/ppermute | solution.py:38
  137.9 13.6 %collective-permute-start.17 = (bf16[512,256]{1,0:T(8,128)(2,1)S(1)}, bf16[512,256]{1,0:T(8,128)(2,1)S(1)}, u32[]{:S(2)}, u32[]{:S(2)}) collective-permute-start(bf16[512,256]{1,0:T(8,128)(2,1)S(1)} %get-tuple-element.51), channel_id=1, source_target_pairs={{0,192},{64,0},{128,64},{192,128},{1,193},{65,1},{129,65},{193,129... | collective-permute-start | bytes 786440 | tf_op jit(solution)/shard_map/ppermute | solution.py:38
  151.6 27.0 %copy-start.6 = (bf16[4,512,256]{2,1,0:T(8,128)(2,1)}, bf16[4,512,256]{2,1,0:T(8,128)(2,1)S(1)}, u32[]{:S(2)}) copy-start(bf16[4,512,256]{2,1,0:T(8,128)(2,1)S(1)} %pad_maximum_fusion.2.a_own_ref) | copy-start | bytes 3145732
  151.6 26.9 %collective-permute-start.18 = (bf16[4,512,256]{2,1,0:T(8,128)(2,1)S(1)}, bf16[4,512,256]{2,1,0:T(8,128)(2,1)S(1)}, u32[]{:S(2)}, u32[]{:S(2)}) collective-permute-start(bf16[4,512,256]{2,1,0:T(8,128)(2,1)S(1)} %pad_maximum_fusion.2.a_own_ref), channel_id=1, source_target_pairs={{0,1},{1,0},{2,3},{3,2},{4,5},{5,4},{6,7},{7,6},{8,9},{9,8},{10,11... | collective-permute-start | bytes 3145736 | tf_op jit(solution)/shard_map/ppermute | solution.py:61
  153.2 23.6 %collective-permute-start.20 = (bf16[512,896]{1,0:T(8,128)(2,1)}, bf16[512,896]{1,0:T(8,128)(2,1)S(1)}, u32[]{:S(2)}, u32[]{:S(2)}) collective-permute-start(bf16[512,896]{1,0:T(8,128)(2,1)} %pad_maximum_fusion.3.m0_ref), channel_id=1, source_target_pairs={{0,64},{64,128},{128,192},{192,0},{1,65},{65,129},{129,193},{193,1... | collective-permute-start | bytes 2752520 | tf_op jit(solution)/shard_map/ppermute | solution.py:38
  153.9 23.7 %collective-permute-start.22 = (bf16[512,896]{1,0:T(8,128)(2,1)}, bf16[512,896]{1,0:T(8,128)(2,1)S(1)}, u32[]{:S(2)}, u32[]{:S(2)}) collective-permute-start(bf16[512,896]{1,0:T(8,128)(2,1)} %collective-permute-done.21.m3_ref), channel_id=1, source_target_pairs={{0,192},{64,0},{128,64},{192,128},{1,193},{65,1},{129,65},{193,129... | collective-permute-start | bytes 2752520 | tf_op jit(solution)/shard_map/ppermute | solution.py:38
  156.0 50.3 %collective-permute-start.13 = (bf16[512,1024]{1,0:T(8,128)(2,1)}, bf16[512,1024]{1,0:T(8,128)(2,1)S(1)}, u32[]{:S(2)}, u32[]{:S(2)}) collective-permute-start(bf16[512,1024]{1,0:T(8,128)(2,1)} %get-tuple-element.39), channel_id=1, source_target_pairs={{4,0},{8,4},{12,8},{16,12},{20,16},{24,20},{28,24},{32,28},{36,32}... | collective-permute-start | bytes 3145736 | tf_op jit(solution)/shard_map/ppermute | solution.py:33
  176.7 0.9 copy-start.8
  177.6 0.9 copy-start.9
  178.6 1.0 copy-start.7
  186.7 10.7 %collective-permute-start.25 = (bf16[128,896]{1,0:T(8,128)(2,1)S(1)}, bf16[128,896]{1,0:T(8,128)(2,1)S(1)}, u32[]{:S(2)}, u32[]{:S(2)}) collective-permute-start(bf16[128,896]{1,0:T(8,128)(2,1)S(1)} %get-tuple-element.58), channel_id=1, source_target_pairs={{0,34},{32,0},{2,32},{34,2},{1,35},{33,1},{3,33},{35,3},{4,38},{36... | collective-permute-start | bytes 688136 | tf_op jit(solution)/shard_map/ppermute | solution.py:43
  187.1 10.3 %collective-permute-start.24 = (bf16[128,896]{1,0:T(8,128)(2,1)S(1)}, bf16[128,896]{1,0:T(8,128)(2,1)S(1)}, u32[]{:S(2)}, u32[]{:S(2)}) collective-permute-start(bf16[128,896]{1,0:T(8,128)(2,1)S(1)} %get-tuple-element.59), channel_id=1, source_target_pairs={{0,2},{32,34},{2,0},{34,32},{1,3},{33,35},{3,1},{35,33},{4,6},{36,... | collective-permute-start | bytes 688136 | tf_op jit(solution)/shard_map/ppermute | solution.py:43
  188.5 12.5 %collective-permute-start.23 = (bf16[128,896]{1,0:T(8,128)(2,1)S(1)}, bf16[128,896]{1,0:T(8,128)(2,1)S(1)}, u32[]{:S(2)}, u32[]{:S(2)}) collective-permute-start(bf16[128,896]{1,0:T(8,128)(2,1)S(1)} %get-tuple-element.57), channel_id=1, source_target_pairs={{0,32},{32,2},{2,34},{34,0},{1,33},{33,3},{3,35},{35,1},{4,36},{36... | collective-permute-start | bytes 688136 | tf_op jit(solution)/shard_map/ppermute | solution.py:43
  202.7 34.1 %copy-start.4 = (f32[512,1024]{1,0:T(8,128)S(1)}, f32[512,1024]{1,0:T(8,128)}, u32[]{:S(2)}) copy-start(f32[512,1024]{1,0:T(8,128)} %get-tuple-element.37) | copy-start | bytes 6291460
  202.7 14.1 %all-to-all-start.1 = ((bf16[8,16,896]{2,1,0:T(8,128)(2,1)}), bf16[8,16,896]{2,1,0:T(8,128)(2,1)S(1)}, u32[]{:S(2)}, u32[]{:S(2)}) async-start(bf16[8,16,896]{2,1,0:T(8,128)(2,1)} %bitcast.72), calls=%async_computation.1 | async-start | bytes 458752 | tf_op jit(solution)/shard_map/all_to_all | solution.py:378
  208.9 26.9 %collective-permute-start.14 = (bf16[512,1024]{1,0:T(8,128)(2,1)}, bf16[512,1024]{1,0:T(8,128)(2,1)S(1)}, u32[]{:S(2)}, u32[]{:S(2)}) collective-permute-start(bf16[512,1024]{1,0:T(8,128)(2,1)} %add_convert_fusion), channel_id=1, source_target_pairs={{4,0},{8,4},{12,8},{16,12},{20,16},{24,20},{28,24},{32,28},{36,32}... | collective-permute-start | bytes 3145736 | tf_op jit(solution)/shard_map/ppermute | solution.py:33
  217.5 2.8 %collective-permute-start.26 = (f32[16,896]{1,0:T(8,128)S(1)}, f32[16,896]{1,0:T(8,128)S(1)}, u32[]{:S(2)}, u32[]{:S(2)}) collective-permute-start(f32[16,896]{1,0:T(8,128)S(1)} %get-tuple-element.46), channel_id=1, source_target_pairs={{0,1},{1,0},{2,3},{3,2},{4,5},{5,4},{6,7},{7,6},{8,9},{9,8},{10,11... | collective-permute-start | bytes 172040 | tf_op jit(solution)/shard_map/ppermute | solution.py:61
  220.3 25.7 %collective-permute-start.27 = (f32[16,1792]{1,0:T(8,128)S(1)}, f32[16,1792]{1,0:T(8,128)S(1)}, u32[]{:S(2)}, u32[]{:S(2)}) collective-permute-start(f32[16,1792]{1,0:T(8,128)S(1)} %maximum_select_fusion.1), channel_id=1, source_target_pairs={{0,2},{2,0},{1,3},{3,1},{4,6},{6,4},{5,7},{7,5},{8,10},{10,8},{9,1... | collective-permute-start | bytes 344072 | tf_op jit(solution)/shard_map/ppermute | solution.py:61
  235.8 1.0 copy-start.5
  241.8 9.0 %all-to-all-start.2 = ((f32[8,8,128]{2,1,0:T(8,128)}), f32[8,8,128]{2,1,0:T(8,128)S(1)}, u32[]{:S(2)}, u32[]{:S(2)}) async-start(f32[8,8,128]{2,1,0:T(8,128)} %broadcast_in_dim_broadcast_in_dim_broadcast_in_dim.6), calls=%async_computation.2 | async-start | bytes 65536 | tf_op jit(solution)/shard_map/all_to_all | solution.py:66
  251.5 17.0 %all-to-all-start.3 = ((f32[32,8,128]{2,1,0:T(8,128)}), f32[32,8,128]{2,1,0:T(8,128)S(1)}, u32[]{:S(2)}, u32[]{:S(2)}) async-start(f32[32,8,128]{2,1,0:T(8,128)} %broadcast_in_dim_broadcast_in_dim_broadcast_in_dim.7), calls=%async_computation.3 | async-start | bytes 262144 | tf_op jit(solution)/shard_map/all_to_all | solution.py:66

commit v4 on v3

--- a/solution.py
+++ b/solution.py
@@ -116,7 +116,10 @@
     tot_ref[0] = jnp.broadcast_to(total, tot_ref.shape[1:])
 
 
-def far_kernel(at_ref, q_ref, h2_ref, acc_ref, tot_ref, p_ref, pf_ref, attn_ref, inv_ref):
+def far_kernel(
+    at_ref, q_ref, h2_ref, acc_ref, tot_ref,
+    p_ref, pf_ref, attn_ref, inv_ref, out0_ref, out1_ref, out2_ref, out3_ref,
+):
     key, query = places()
     t, e = squashed(h2_ref[:TOK_DEV], two_heads(q_ref))
     e = jnp.where(key > query + jnp.where(at_ref[0] >= 2, 0, 4 * TOK_DEV), e, 0.0)
@@ -126,8 +129,14 @@
     inverse = 1.0 / (tot_ref[0, :1] + row_sum(e))
     inv_ref[0] = jnp.broadcast_to(inverse, inv_ref.shape[1:])
     out = ((acc_ref[0] + dot(h2_ref[TOK_DEV:], p, TN)) * inverse).astype(BF16)
-    for h in range(GROUP):
-        attn_ref[0, h * HEAD_DIM : (h + 1) * HEAD_DIM, :] = out[:, h * TOK_DEV : (h + 1) * TOK_DEV]
+    out = jnp.concatenate([out[:, h * TOK_DEV : (h + 1) * TOK_DEV] for h in range(GROUP)], 0)
+    attn_ref[0] = out
+    place = (pl.program_id(0) + 4 - at_ref[1]) % 4
+    for away, out_ref in enumerate((out0_ref, out1_ref, out2_ref, out3_ref)):
+
+        @pl.when(place == away)
+        def _():
+            out_ref[...] = out
 
 
 def score_terms(v, g, delta, pf):
@@ -204,7 +213,7 @@
 HEAD_COLS = pl.BlockSpec((TOK_DEV, GROUP * D), lambda h, *_: (0, h))
 KV_COLS = pl.BlockSpec((TOK_DEV, D), lambda h, *_: (0, h))
 BOTH_COLS = pl.BlockSpec((2 * TOK_DEV, D), lambda h, *_: (0, h))
-ATTN_ROWS = pl.BlockSpec((1, GROUP * D, TOK_DEV), lambda h, at, *_: ((h + 4 - at[1]) % 4, 0, 0))
+ATTN_ROWS = pl.BlockSpec((1, GROUP * D, TOK_DEV), lambda h, *_: (h, 0, 0))
 
 
 def of_head(rows, columns=SCORES):
@@ -251,9 +260,11 @@
     return call(
         far_kernel, 1,
         [HEAD_COLS, BOTH_COLS, of_head(D), of_head(8)],
-        [of_head(TOK_DEV), of_head(TOK_DEV), ATTN_ROWS, of_head(8)],
+        [of_head(TOK_DEV), of_head(TOK_DEV), ATTN_ROWS, of_head(8)]
+        + [pl.BlockSpec((GROUP * D, TOK_DEV), lambda h, *_: (0, 0))] * 4,
         [per_head(TOK_DEV, BF16), per_head(TOK_DEV, BF16),
-         jax.ShapeDtypeStruct((KV_HEADS, GROUP * D, TOK_DEV), BF16), per_head(8, F32)],
+         jax.ShapeDtypeStruct((KV_HEADS, GROUP * D, TOK_DEV), BF16), per_head(8, F32)]
+        + [jax.ShapeDtypeStruct((GROUP * D, TOK_DEV), BF16)] * 4,
         2, 7,
     )(where, q, h2, acc, tot)
 
@@ -343,9 +354,9 @@
     wdh = swap(wbh, "dp_1")
 
     p, pf, acc, tot = near_forward(where, q_rows, k_rows, v_rows, h1)
-    p2, pf2, attn, inv = far_forward(where, q_rows, h2, acc, tot)
+    p2, pf2, attn, inv, *away = far_forward(where, q_rows, h2, acc, tot)
     attn_parts = (
-        attn[0], ring(attn[1], "seq_0", 1), ring(attn[2], "seq_0", 2), ring(attn[3], "seq_0", -1)
+        away[0], ring(away[1], "seq_0", 1), ring(away[2], "seq_0", 2), ring(away[3], "seq_0", -1)
     )
 
     d2, g, delta, dscore = far_backward(
@@ -360,15 +371,16 @@
     dq, d0, d1, dq_sq = near_backward(
         act_scale, q_rows, k_rows, v_rows, h1, h2, p, pf, g, delta, dscore
     )
+    part = weight_product(
+        where, a_own, a_oth, m0, m1, m2, m3
+    )
+    r1, _ = lax.optimization_barrier((r1, part))
     r2 = shifted((d1.astype(F32) + r1.astype(F32)).astype(BF16), -1)
     dkv = d0 + r2.astype(F32)
     square = jnp.sum(dkv * dkv)
     square = square + jnp.sum(dq_sq.reshape(KV_HEADS, 8, 128)[:, 0, 0])
     dkv = dkv.astype(BF16)
 
-    part = weight_product(
-        where, a_own, a_oth, m0, m1, m2, m3
-    )
     part = (
         part[0].astype(F32)
         + ring_x(part[1], 1).astype(F32)

time: 271 us -> 274 us (1.011)
  starting transfers between devices: 60 us -> 78.4 us
  waiting for transfers between devices: 114 us -> 101 us
    ppermute x9, starting transfers between devices: 16.8 us -> 36.2 us  [swap(): return lax.ppermute(value, axis, [(0, 1), (1, 0)])]
    ppermute x10, waiting for transfers between devices: 47 us -> 30.6 us  [ring(): lax.ppermute(value, axis, [(s, (s + steps) % count) for s in range(count)])]
    ppermute x2, waiting for transfers between devices: 30.4 us -> 33.5 us  [across_x(): return lax.ppermute(value, ('seq_1', 'seq_2', 'dp_0'), pairs)]
  transfers between devices with their start and end apart: 31 -> 31, of which waited for: 12 -> 11; matrix products, arithmetic and copies ran while one was open for 9% -> 6% of each run, Pallas kernels for 14% -> 14%
where the time goes in v4:
time: 274 us; the launch traced here: 272 us
  waiting for transfers between devices  101 us (37%)
  starting transfers between devices  78.4 us (29%)
  Pallas kernels  38.2 us (14%)
  blocking collectives  23.6 us (9%)
  other arithmetic  14 us (5%)
  local copies, waits for them, and re-layouts  10.7 us (4%)
  between operations  6.2 us (2%)
    ppermute x9, starting transfers between devices, swap(): return lax.ppermute(value, axis, [(0, 1), (1, 0)])  36.2 us
    ppermute x2, waiting for transfers between devices, across_x(): return lax.ppermute(value, ('seq_1', 'seq_2', 'dp_0'), pairs)  33.5 us
    ppermute x10, waiting for transfers between devices, ring(): lax.ppermute(value, axis, [(s, (s + steps) % count) for s in range(count)])  30.6 us
    all_to_all x1, blocking collectives, for_each(): lax.all_to_all(jnp.broadcast_to(value[None], (size, *value.shape)), axis,...  23.6 us
    ppermute x10, starting transfers between devices, ring(): lax.ppermute(value, axis, [(s, (s + steps) % count) for s in range(count)])  15.1 us
    ppermute x4, waiting for transfers between devices, shifted(): lax.ppermute(value, SEQ, [(source, source + steps) for source in range(in...  14.4 us
    all_to_all x2, starting transfers between devices, for_each(): lax.all_to_all(jnp.broadcast_to(value[None], (size, *value.shape)), axis,...  12.3 us
    all_to_all x2, waiting for transfers between devices, for_each(): lax.all_to_all(jnp.broadcast_to(value[None], (size, *value.shape)), axis,...  12.1 us
  transfers between devices with their start and end apart: 31, of which 11 were waited for; matrix products, arithmetic and copies ran while one was open for 6% of the time, Pallas kernels for 14%

profile of v4, /device:TPU:1, one launch (start us, length us, event | category | flops | bytes accessed | tf_op | source)
XLA Modules:
  0.0 272.4 jit_solution(11315345426226806113)
XLA Ops:
  0.7 0.9 copy-done
  1.6 23.6 %all_to_all.24 = bf16[8,32,896]{2,1,0:T(8,128)(2,1)S(1)} all-to-all(bf16[8,32,896]{2,1,0:T(8,128)(2,1)S(1)} %broadcast_in_dim.30), channel_id=1, replica_groups=mesh['seq_0'=4,'seq_1'=2,'seq_2'=8,'dp_0'=2,'dp_1'=2] {'seq_2'}, dimensions={0} | all-to-all | bytes 917504 | tf_op jit(solution)/shard_map/all_to_all | solution.py:66
  25.2 2.7 %collective-permute-start.6 = (bf16[256,896]{1,0:T(8,128)(2,1)S(1)}, bf16[256,896]{1,0:T(8,128)(2,1)S(1)}, u32[]{:S(2)}, u32[]{:S(2)}) collective-permute-start(bf16[256,896]{1,0:T(8,128)(2,1)S(1)} %bitcast.58), channel_id=1, source_target_pairs={{0,192},{64,0},{128,64},{192,128},{1,193},{65,1},{129,65},{193,129... | collective-permute-start | bytes 1376264 | tf_op jit(solution)/shard_map/ppermute | solution.py:38
  27.9 7.6 %collective-permute-done.6 = bf16[256,896]{1,0:T(8,128)(2,1)S(1)} collective-permute-done((bf16[256,896]{1,0:T(8,128)(2,1)S(1)}, bf16[256,896]{1,0:T(8,128)(2,1)S(1)}, u32[]{:S(2)}, u32[]{:S(2)}) %collective-permute-start.6) | collective-permute-done | bytes 458784 | tf_op jit(solution)/shard_map/ppermute | solution.py:38
  35.6 3.5 %collective-permute-start.7 = (bf16[128,896]{1,0:T(8,128)(2,1)S(1)}, bf16[128,896]{1,0:T(8,128)(2,1)S(1)}, u32[]{:S(2)}, u32[]{:S(2)}) collective-permute-start(bf16[128,896]{1,0:T(8,128)(2,1)S(1)} %slice.61), channel_id=1, source_target_pairs={{0,192},{64,0},{128,64},{192,128},{1,193},{65,1},{129,65},{193,129... | collective-permute-start | bytes 688136 | tf_op jit(solution)/shard_map/ppermute | solution.py:38
  39.3 2.3 collective-permute-start.2
  41.6 0.5 collective-permute-done.7
  42.0 3.2 %collective-permute-done.5 = bf16[128,896]{1,0:T(8,128)(2,1)S(1)} collective-permute-done((bf16[128,896]{1,0:T(8,128)(2,1)S(1)}, bf16[128,896]{1,0:T(8,128)(2,1)S(1)}, u32[]{:S(2)}, u32[]{:S(2)}) %collective-permute-start.5) | collective-permute-done | bytes 229408 | tf_op jit(solution)/shard_map/ppermute | solution.py:38
  45.3 0.3 pad_maximum_fusion.wa_ref
  45.6 23.4 %collective-permute-start.8 = (bf16[4,256,896]{2,1,0:T(8,128)(2,1)S(1)}, bf16[4,256,896]{2,1,0:T(8,128)(2,1)}, u32[]{:S(2)}, u32[]{:S(2)}) collective-permute-start(bf16[4,256,896]{2,1,0:T(8,128)(2,1)S(1)} %pad_maximum_fusion.wa_ref), channel_id=1, source_target_pairs={{0,1},{1,0},{2,3},{3,2},{4,5},{5,4},{6,7},{7,6},{8,9},{9,8},{10,11... | collective-permute-start | bytes 5505032 | tf_op jit(solution)/shard_map/ppermute | solution.py:61
  69.0 1.4 fusion.4
  70.4 2.7 collective-permute-start.10
  73.8 1.3 bitcast_select_fusion
  75.1 1.4 collective-permute-start.3
  76.5 0.9 constant_dynamic-slice_fusion.1
  77.4 0.7 collective-permute-start.18
  78.1 15.6 %collective-permute-done.9.wbl_ref = bf16[4,128,896]{2,1,0:T(8,128)(2,1)} collective-permute-done((bf16[4,128,896]{2,1,0:T(8,128)(2,1)}, bf16[4,128,896]{2,1,0:T(8,128)(2,1)}, u32[]{:S(2)}, u32[]{:S(2)}) %collective-permute-start.9) | collective-permute-done | bytes 917536 | tf_op jit(solution)/shard_map/ppermute | solution.py:57
  93.6 1.7 collective-permute-start.11
  95.4 17.9 %collective-permute-done.10.wbh_ref = bf16[4,128,896]{2,1,0:T(8,128)(2,1)} collective-permute-done((bf16[4,128,896]{2,1,0:T(8,128)(2,1)}, bf16[4,128,896]{2,1,0:T(8,128)(2,1)}, u32[]{:S(2)}, u32[]{:S(2)}) %collective-permute-start.10) | collective-permute-done | bytes 917536 | tf_op jit(solution)/shard_map/ppermute | solution.py:57
  113.3 1.1 collective-permute-start.12
  114.4 2.4 collective-permute-start
  116.8 2.0 pad_maximum_fusion.3.m0_ref
  118.8 0.6 pad_add_fusion.at_ref
  120.1 6.8 %shard_map.101 = (bf16[4,512,512]{2,1,0:T(8,128)(2,1)}, bf16[4,512,512]{2,1,0:T(8,128)(2,1)}, f32[4,256,512]{2,1,0:T(8,128)}, f32[4,8,512]{2,1,0:T(8,128)}) custom-call(s32[4]{0:T(128)} %pad_add_fusion.at_ref, bf16[256,2048]{1,0:T(8,128)(2,1)} %bitcast.48, bf16[256,1024]{1,0:T(8,128)(2,1)} %bitcast.52, bf16[256,1024]{1,0:T(8,128)(2,1)} %bitcast.55, ...), custom_call_target="tpu_custom_call" | custom-call | flops 1073741824 | bytes 9437184 | tf_op jit(solution)/shard_map/pallas_call | solution.py:249
  127.0 2.3 collective-permute-start.1
  129.3 6.7 %shard_map.102 = (bf16[4,256,512]{2,1,0:T(8,128)(2,1)}, bf16[4,256,512]{2,1,0:T(8,128)(2,1)}, bf16[4,512,256]{2,1,0:T(8,128)(2,1)}, f32[4,8,512]{2,1,0:T(8,128)}...) custom-call(s32[4]{0:T(128)} %pad_add_fusion.at_ref, ...), custom_call_target="tpu_custom_call" | custom-call | flops 536870912 | bytes 7340032 | tf_op jit(solution)/shard_map/pallas_call | solution.py:260
  136.1 2.3 collective-permute-start.14
  138.4 2.1 collective-permute-start.15
  140.4 1.8 collective-permute-start.16
  142.9 10.5 %shard_map.103 = (bf16[512,1024]{1,0:T(8,128)(2,1)}, bf16[4,256,512]{2,1,0:T(8,128)(2,1)}, f32[4,8,512]{2,1,0:T(8,128)}, bf16[4,256,512]{2,1,0:T(8,128)(2,1)}) custom-call(s32[4]{0:T(128)} %pad_add_fusion.at_ref, f32[1]{0:T(128)S(6)} %div.6.scale_ref, bf16[256,2048]{1,0:T(8,128)(2,1)} %bitcast.50, bf16[512,1024]{1,0:T(8,128)(2,1)} %copy-done.2, ...), custom_call_target="tpu_custom_call" | custom-call | flops 2684354560 | bytes 15728640 | tf_op jit(solution)/shard_map/pallas_call | solution.py:275
  153.6 2.0 collective-permute-start.17
  155.7 2.7 collective-permute-start.21
  158.3 1.3 collective-permute-start.13
  159.6 19.3 %collective-permute-done.19.m1_ref = bf16[512,896]{1,0:T(8,128)(2,1)S(1)} collective-permute-done((bf16[512,896]{1,0:T(8,128)(2,1)}, bf16[512,896]{1,0:T(8,128)(2,1)S(1)}, u32[]{:S(2)}, u32[]{:S(2)}) %collective-permute-start.19) | collective-permute-done | bytes 917536 | tf_op jit(solution)/shard_map/ppermute | solution.py:38
  178.9 0.9 copy-done.11
  179.8 0.9 copy-done.12
  180.8 1.0 copy-done.10
  181.8 6.0 %weight_product.1 = bf16[4,128,896]{2,1,0:T(8,128)(2,1)} custom-call(s32[4]{0:T(128)} %pad_add_fusion.at_ref, bf16[4,512,256]{2,1,0:T(8,128)(2,1)} %copy-done.8, bf16[4,512,256]{2,1,0:T(8,128)(2,1)} %copy-done.10, bf16[512,896]{1,0:T(8,128)(2,1)} %pad_maximum_fusion.3.m0_ref, bf16[512,896]{1,0:T(8,128)(2,1)} %copy-done.11, bf16[512,896]{1,0:T(8,128)(2,1)} %copy-done.12, ...), custom_call_target="tpu_custom_call" | custom-call | flops 1879048192 | bytes 7340032 | tf_op jit(solution)/shard_map/weight_product/pallas_call | solution.py:299
  187.8 1.2 slice_bitcast_fusion.4
  189.0 0.7 collective-permute-start.25
  189.7 0.9 collective-permute-start.24
  190.6 0.8 collective-permute-start.23
  191.4 8.2 %shard_map.104 = (bf16[256,2048]{1,0:T(8,128)(2,1)}, f32[512,1024]{1,0:T(8,128)}, bf16[512,1024]{1,0:T(8,128)(2,1)}, f32[32,128]{1,0:T(8,128)}) custom-call(f32[1]{0:T(128)S(6)} %div.6.scale_ref, bf16[256,2048]{1,0:T(8,128)(2,1)} %bitcast.51, bf16[256,1024]{1,0:T(8,128)(2,1)} %bitcast.53, bf16[256,1024]{1,0:T(8,128)(2,1)} %bitcast.56, ...), custom_call_target="tpu_custom_call" | custom-call | flops 2415919104 | bytes 13631488 | tf_op jit(solution)/shard_map/pallas_call | solution.py:286
  199.6 4.1 %collective-permute-done.23 = bf16[128,896]{1,0:T(8,128)(2,1)S(1)} collective-permute-done((bf16[128,896]{1,0:T(8,128)(2,1)S(1)}, bf16[128,896]{1,0:T(8,128)(2,1)S(1)}, u32[]{:S(2)}, u32[]{:S(2)}) %collective-permute-start.23) | collective-permute-done | bytes 229408 | tf_op jit(solution)/shard_map/ppermute | solution.py:43
  203.6 1.7 fusion.3
  205.4 3.5 %all-to-all-start.1 = ((bf16[8,16,896]{2,1,0:T(8,128)(2,1)}), bf16[8,16,896]{2,1,0:T(8,128)(2,1)S(1)}, u32[]{:S(2)}, u32[]{:S(2)}) async-start(bf16[8,16,896]{2,1,0:T(8,128)(2,1)} %bitcast.63), calls=%async_computation.1 | async-start | bytes 458752 | tf_op jit(solution)/shard_map/all_to_all | solution.py:390
  208.9 2.7 add_convert_fusion
  211.6 1.3 collective-permute-start.22
  212.9 6.5 %all-to-all-done.1 = bf16[8,16,896]{2,1,0:T(8,128)(2,1)S(1)} async-done(((bf16[8,16,896]{2,1,0:T(8,128)(2,1)}), bf16[8,16,896]{2,1,0:T(8,128)(2,1)S(1)}, u32[]{:S(2)}, u32[]{:S(2)}) %all-to-all-start.1) | async-done | bytes 229408 | tf_op jit(solution)/shard_map/all_to_all | solution.py:390
  219.5 0.6 multiply_reduce_fusion.1
  220.1 1.5 collective-permute-start.26
  221.6 1.3 slice_reduce_fusion
  222.9 1.0 collective-permute-start.27
  224.0 14.4 %collective-permute-done.22 = bf16[512,1024]{1,0:T(8,128)(2,1)S(1)} collective-permute-done((bf16[512,1024]{1,0:T(8,128)(2,1)}, bf16[512,1024]{1,0:T(8,128)(2,1)S(1)}, u32[]{:S(2)}, u32[]{:S(2)}) %collective-permute-start.22) | collective-permute-done | bytes 1048608 | tf_op jit(solution)/shard_map/ppermute | solution.py:33
  238.4 1.0 copy-done.7
  239.3 2.4 multiply_reduce_fusion
  243.7 0.6 broadcast_in_dim_broadcast_in_dim_broadcast_in_dim.6
  244.3 4.4 %all-to-all-start.2 = ((f32[8,8,128]{2,1,0:T(8,128)}), f32[8,8,128]{2,1,0:T(8,128)S(1)}, u32[]{:S(2)}, u32[]{:S(2)}) async-start(f32[8,8,128]{2,1,0:T(8,128)} %broadcast_in_dim_broadcast_in_dim_broadcast_in_dim.6), calls=%async_computation.2 | async-start | bytes 65536 | tf_op jit(solution)/shard_map/all_to_all | solution.py:66
  248.7 0.7 maximum_select_fusion
  249.4 4.0 %all-to-all-done.2 = f32[8,8,128]{2,1,0:T(8,128)S(1)} async-done(((f32[8,8,128]{2,1,0:T(8,128)}), f32[8,8,128]{2,1,0:T(8,128)S(1)}, u32[]{:S(2)}, u32[]{:S(2)}) %all-to-all-start.2) | async-done | bytes 32800 | tf_op jit(solution)/shard_map/all_to_all | solution.py:66
  253.4 0.7 broadcast_in_dim_broadcast_in_dim_broadcast_in_dim.7
  254.1 7.9 %all-to-all-start.3 = ((f32[32,8,128]{2,1,0:T(8,128)}), f32[32,8,128]{2,1,0:T(8,128)S(1)}, u32[]{:S(2)}, u32[]{:S(2)}) async-start(f32[32,8,128]{2,1,0:T(8,128)} %broadcast_in_dim_broadcast_in_dim_broadcast_in_dim.7), calls=%async_computation.3 | async-start | bytes 262144 | tf_op jit(solution)/shard_map/all_to_all | solution.py:66
  262.0 1.0 slice_bitcast_fusion
  263.1 8.1 %all-to-all-done.3 = f32[32,8,128]{2,1,0:T(8,128)S(1)} async-done(((f32[32,8,128]{2,1,0:T(8,128)}), f32[32,8,128]{2,1,0:T(8,128)S(1)}, u32[]{:S(2)}, u32[]{:S(2)}) %all-to-all-start.3) | async-done | bytes 131104 | tf_op jit(solution)/shard_map/all_to_all | solution.py:66
  (60 shorter events, 0.6 us)
Async XLA Ops:
  0.6 0.9 copy-start
  0.6 38.6 %copy-start.5 = (bf16[1,256,1024]{2,1,0:T(8,128)(2,1)S(1)}, bf16[1,256,1024]{2,1,0:T(8,128)(2,1)}, u32[]{:S(2)}) copy-start(bf16[1,256,1024]{2,1,0:T(8,128)(2,1)} %param.7) | copy-start | bytes 1572868
  0.7 38.5 %copy-start.6 = (bf16[1,256,1024]{2,1,0:T(8,128)(2,1)S(1)}, bf16[1,256,1024]{2,1,0:T(8,128)(2,1)}, u32[]{:S(2)}) copy-start(bf16[1,256,1024]{2,1,0:T(8,128)(2,1)} %param.8) | copy-start | bytes 1572868
  25.2 10.4 %collective-permute-start.6 = (bf16[256,896]{1,0:T(8,128)(2,1)S(1)}, bf16[256,896]{1,0:T(8,128)(2,1)S(1)}, u32[]{:S(2)}, u32[]{:S(2)}) collective-permute-start(bf16[256,896]{1,0:T(8,128)(2,1)S(1)} %bitcast.58), channel_id=1, source_target_pairs={{0,192},{64,0},{128,64},{192,128},{1,193},{65,1},{129,65},{193,129... | collective-permute-start | bytes 1376264 | tf_op jit(solution)/shard_map/ppermute | solution.py:38
  27.9 11.2 %collective-permute-start.4 = (bf16[256,896]{1,0:T(8,128)(2,1)S(1)}, bf16[256,896]{1,0:T(8,128)(2,1)S(1)}, u32[]{:S(2)}, u32[]{:S(2)}) collective-permute-start(bf16[256,896]{1,0:T(8,128)(2,1)S(1)} %bitcast.59), channel_id=1, source_target_pairs={{0,64},{64,128},{128,192},{192,0},{1,65},{65,129},{129,193},{193,1... | collective-permute-start | bytes 1376264 | tf_op jit(solution)/shard_map/ppermute | solution.py:38
  35.6 6.5 %collective-permute-start.7 = (bf16[128,896]{1,0:T(8,128)(2,1)S(1)}, bf16[128,896]{1,0:T(8,128)(2,1)S(1)}, u32[]{:S(2)}, u32[]{:S(2)}) collective-permute-start(bf16[128,896]{1,0:T(8,128)(2,1)S(1)} %slice.61), channel_id=1, source_target_pairs={{0,192},{64,0},{128,64},{192,128},{1,193},{65,1},{129,65},{193,129... | collective-permute-start | bytes 688136 | tf_op jit(solution)/shard_map/ppermute | solution.py:38
  39.1 6.2 %collective-permute-start.5 = (bf16[128,896]{1,0:T(8,128)(2,1)S(1)}, bf16[128,896]{1,0:T(8,128)(2,1)S(1)}, u32[]{:S(2)}, u32[]{:S(2)}) collective-permute-start(bf16[128,896]{1,0:T(8,128)(2,1)S(1)} %slice.60), channel_id=1, source_target_pairs={{0,64},{64,128},{128,192},{192,0},{1,65},{65,129},{129,193},{193,1... | collective-permute-start | bytes 688136 | tf_op jit(solution)/shard_map/ppermute | solution.py:38
  39.3 35.8 %collective-permute-start.2 = (bf16[512,1024]{1,0:T(8,128)(2,1)S(1)}, bf16[512,1024]{1,0:T(8,128)(2,1)}, u32[]{:S(2)}, u32[]{:S(2)}) collective-permute-start(bf16[512,1024]{1,0:T(8,128)(2,1)S(1)} %pad_maximum_fusion.1), channel_id=1, source_target_pairs={{0,4},{4,8},{8,12},{12,16},{16,20},{20,24},{24,28},{28,32},{32,36}... | collective-permute-start | bytes 3145736 | tf_op jit(solution)/shard_map/ppermute | solution.py:33
  45.6 29.5 %copy-start.1 = (bf16[4,256,896]{2,1,0:T(8,128)(2,1)}, bf16[4,256,896]{2,1,0:T(8,128)(2,1)S(1)}, u32[]{:S(2)}) copy-start(bf16[4,256,896]{2,1,0:T(8,128)(2,1)S(1)} %pad_maximum_fusion.wa_ref) | copy-start | bytes 5505028
  45.6 92.8 %collective-permute-start.8 = (bf16[4,256,896]{2,1,0:T(8,128)(2,1)S(1)}, bf16[4,256,896]{2,1,0:T(8,128)(2,1)}, u32[]{:S(2)}, u32[]{:S(2)}) collective-permute-start(bf16[4,256,896]{2,1,0:T(8,128)(2,1)S(1)} %pad_maximum_fusion.wa_ref), channel_id=1, source_target_pairs={{0,1},{1,0},{2,3},{3,2},{4,5},{5,4},{6,7},{7,6},{8,9},{9,8},{10,11... | collective-permute-start | bytes 5505032 | tf_op jit(solution)/shard_map/ppermute | solution.py:61
  70.4 23.2 %collective-permute-start.9 = (bf16[4,128,896]{2,1,0:T(8,128)(2,1)}, bf16[4,128,896]{2,1,0:T(8,128)(2,1)}, u32[]{:S(2)}, u32[]{:S(2)}) collective-permute-start(bf16[4,128,896]{2,1,0:T(8,128)(2,1)} %get-tuple-element.60), channel_id=1, source_target_pairs={{0,34},{2,32},{4,36},{6,38},{8,40},{10,42},{12,44},{14,46},{16,48}... | collective-permute-start | bytes 2752520 | tf_op jit(solution)/shard_map/ppermute | solution.py:57
  70.4 42.9 %collective-permute-start.10 = (bf16[4,128,896]{2,1,0:T(8,128)(2,1)}, bf16[4,128,896]{2,1,0:T(8,128)(2,1)}, u32[]{:S(2)}, u32[]{:S(2)}) collective-permute-start(bf16[4,128,896]{2,1,0:T(8,128)(2,1)} %get-tuple-element.59), channel_id=1, source_target_pairs={{0,34},{2,32},{4,38},{6,36},{8,42},{10,40},{12,46},{14,44},{16,50}... | collective-permute-start | bytes 2752520 | tf_op jit(solution)/shard_map/ppermute | solution.py:57
  75.1 51.9 %collective-permute-start.3 = (bf16[512,1024]{1,0:T(8,128)(2,1)}, bf16[512,1024]{1,0:T(8,128)(2,1)S(1)}, u32[]{:S(2)}, u32[]{:S(2)}) collective-permute-start(bf16[512,1024]{1,0:T(8,128)(2,1)} %collective-permute-done.2.h1_ref), channel_id=1, source_target_pairs={{0,4},{4,8},{8,12},{12,16},{16,20},{20,24},{24,28},{28,32},{32,36}... | collective-permute-start | bytes 3145736 | tf_op jit(solution)/shard_map/ppermute | solution.py:33
  77.4 49.6 %copy-start.3 = (bf16[256,896]{1,0:T(8,128)(2,1)}, bf16[256,896]{1,0:T(8,128)(2,1)S(1)}, u32[]{:S(2)}) copy-start(bf16[256,896]{1,0:T(8,128)(2,1)S(1)} %get-tuple-element.67.m_own_ref) | copy-start | bytes 1376260
  77.4 37.0 %collective-permute-start.18 = (bf16[256,896]{1,0:T(8,128)(2,1)}, bf16[256,896]{1,0:T(8,128)(2,1)}, u32[]{:S(2)}, u32[]{:S(2)}) collective-permute-start(bf16[256,896]{1,0:T(8,128)(2,1)} %get-tuple-element.66.m_oth_ref), channel_id=1, source_target_pairs={{0,1},{1,0},{2,3},{3,2},{4,5},{5,4},{6,7},{7,6},{8,9},{9,8},{10,11... | collective-permute-start | bytes 1376264 | tf_op jit(solution)/shard_map/ppermute | solution.py:61
  93.6 46.8 %collective-permute-start.11 = (bf16[4,128,896]{2,1,0:T(8,128)(2,1)}, bf16[4,128,896]{2,1,0:T(8,128)(2,1)}, u32[]{:S(2)}, u32[]{:S(2)}) collective-permute-start(bf16[4,128,896]{2,1,0:T(8,128)(2,1)} %collective-permute-done.9.wbl_ref), channel_id=1, source_target_pairs={{0,1},{1,0},{2,3},{3,2},{4,5},{5,4},{6,7},{7,6},{8,9},{9,8},{10,11... | collective-permute-start | bytes 2752520 | tf_op jit(solution)/shard_map/ppermute | solution.py:61
  113.3 29.6 %collective-permute-start.12 = (bf16[4,128,896]{2,1,0:T(8,128)(2,1)}, bf16[4,128,896]{2,1,0:T(8,128)(2,1)}, u32[]{:S(2)}, u32[]{:S(2)}) collective-permute-start(bf16[4,128,896]{2,1,0:T(8,128)(2,1)} %collective-permute-done.10.wbh_ref), channel_id=1, source_target_pairs={{0,1},{1,0},{2,3},{3,2},{4,5},{5,4},{6,7},{7,6},{8,9},{9,8},{10,11... | collective-permute-start | bytes 2752520 | tf_op jit(solution)/shard_map/ppermute | solution.py:61
  114.4 4.5 %collective-permute-start = (f32[1]{0:T(128)}, f32[1]{0:T(128)}, u32[]{:S(2)}, u32[]{:S(2)}) collective-permute-start(f32[1]{0:T(128)} %bitcast.1), channel_id=1, source_target_pairs={{0,1},{1,0},{2,3},{3,2},{4,5},{5,4},{6,7},{7,6},{8,9},{9,8},{10,11... | collective-permute-start | bytes 20 | tf_op jit(solution)/shard_map/ppermute | solution.py:61
  118.8 36.8 %collective-permute-start.20 = (bf16[512,896]{1,0:T(8,128)(2,1)}, bf16[512,896]{1,0:T(8,128)(2,1)}, u32[]{:S(2)}, u32[]{:S(2)}) collective-permute-start(bf16[512,896]{1,0:T(8,128)(2,1)} %pad_maximum_fusion.3.m0_ref), channel_id=1, source_target_pairs={{0,192},{64,0},{128,64},{192,128},{1,193},{65,1},{129,65},{193,129... | collective-permute-start | bytes 2752520 | tf_op jit(solution)/shard_map/ppermute | solution.py:38
  127.0 2.4 copy-start.2
  127.0 9.1 %collective-permute-start.1 = (f32[1]{0:T(128)}, f32[1]{0:T(128)}, u32[]{:S(2)}, u32[]{:S(2)}) collective-permute-start(f32[1]{0:T(128)} %add.53), channel_id=1, source_target_pairs={{0,2},{2,0},{1,3},{3,1},{4,6},{6,4},{5,7},{7,5},{8,10},{10,8},{9,1... | collective-permute-start | bytes 20 | tf_op jit(solution)/shard_map/ppermute | solution.py:61
  136.1 17.3 %collective-permute-start.14 = (bf16[512,256]{1,0:T(8,128)(2,1)}, bf16[512,256]{1,0:T(8,128)(2,1)S(1)}, u32[]{:S(2)}, u32[]{:S(2)}) collective-permute-start(bf16[512,256]{1,0:T(8,128)(2,1)} %get-tuple-element.46), channel_id=1, source_target_pairs={{0,64},{64,128},{128,192},{192,0},{1,65},{65,129},{129,193},{193,1... | collective-permute-start | bytes 786440 | tf_op jit(solution)/shard_map/ppermute | solution.py:38
  138.4 15.1 %collective-permute-start.15 = (bf16[512,256]{1,0:T(8,128)(2,1)}, bf16[512,256]{1,0:T(8,128)(2,1)S(1)}, u32[]{:S(2)}, u32[]{:S(2)}) collective-permute-start(bf16[512,256]{1,0:T(8,128)(2,1)} %get-tuple-element.47), channel_id=1, source_target_pairs={{0,128},{64,192},{128,0},{192,64},{1,129},{65,193},{129,1},{193,65... | collective-permute-start | bytes 786440 | tf_op jit(solution)/shard_map/ppermute | solution.py:38
  140.4 13.0 %collective-permute-start.16 = (bf16[512,256]{1,0:T(8,128)(2,1)}, bf16[512,256]{1,0:T(8,128)(2,1)S(1)}, u32[]{:S(2)}, u32[]{:S(2)}) collective-permute-start(bf16[512,256]{1,0:T(8,128)(2,1)} %get-tuple-element.48), channel_id=1, source_target_pairs={{0,192},{64,0},{128,64},{192,128},{1,193},{65,1},{129,65},{193,129... | collective-permute-start | bytes 786440 | tf_op jit(solution)/shard_map/ppermute | solution.py:38
  142.9 10.5 %copy-start.9 = (bf16[512,256]{1,0:T(8,128)(2,1)S(1)}, bf16[512,256]{1,0:T(8,128)(2,1)}, u32[]{:S(2)}) copy-start(bf16[512,256]{1,0:T(8,128)(2,1)} %get-tuple-element.49) | copy-start | bytes 786436
  153.6 27.2 %copy-start.8 = (bf16[4,512,256]{2,1,0:T(8,128)(2,1)}, bf16[4,512,256]{2,1,0:T(8,128)(2,1)S(1)}, u32[]{:S(2)}) copy-start(bf16[4,512,256]{2,1,0:T(8,128)(2,1)S(1)} %pad_maximum_fusion.2.a_own_ref) | copy-start | bytes 3145732
  153.6 27.2 %collective-permute-start.17 = (bf16[4,512,256]{2,1,0:T(8,128)(2,1)S(1)}, bf16[4,512,256]{2,1,0:T(8,128)(2,1)S(1)}, u32[]{:S(2)}, u32[]{:S(2)}) collective-permute-start(bf16[4,512,256]{2,1,0:T(8,128)(2,1)S(1)} %pad_maximum_fusion.2.a_own_ref), channel_id=1, source_target_pairs={{0,1},{1,0},{2,3},{3,2},{4,5},{5,4},{6,7},{7,6},{8,9},{9,8},{10,11... | collective-permute-start | bytes 3145736 | tf_op jit(solution)/shard_map/ppermute | solution.py:61
  155.7 23.2 %collective-permute-start.19 = (bf16[512,896]{1,0:T(8,128)(2,1)}, bf16[512,896]{1,0:T(8,128)(2,1)S(1)}, u32[]{:S(2)}, u32[]{:S(2)}) collective-permute-start(bf16[512,896]{1,0:T(8,128)(2,1)} %pad_maximum_fusion.3.m0_ref), channel_id=1, source_target_pairs={{0,64},{64,128},{128,192},{192,0},{1,65},{65,129},{129,193},{193,1... | collective-permute-start | bytes 2752520 | tf_op jit(solution)/shard_map/ppermute | solution.py:38
  155.7 24.2 %collective-permute-start.21 = (bf16[512,896]{1,0:T(8,128)(2,1)}, bf16[512,896]{1,0:T(8,128)(2,1)S(1)}, u32[]{:S(2)}, u32[]{:S(2)}) collective-permute-start(bf16[512,896]{1,0:T(8,128)(2,1)} %collective-permute-done.20.m3_ref), channel_id=1, source_target_pairs={{0,192},{64,0},{128,64},{192,128},{1,193},{65,1},{129,65},{193,129... | collective-permute-start | bytes 2752520 | tf_op jit(solution)/shard_map/ppermute | solution.py:38
  158.3 41.2 %collective-permute-start.13 = (bf16[512,1024]{1,0:T(8,128)(2,1)}, bf16[512,1024]{1,0:T(8,128)(2,1)S(1)}, u32[]{:S(2)}, u32[]{:S(2)}) collective-permute-start(bf16[512,1024]{1,0:T(8,128)(2,1)} %get-tuple-element.44), channel_id=1, source_target_pairs={{4,0},{8,4},{12,8},{16,12},{20,16},{24,20},{28,24},{32,28},{36,32}... | collective-permute-start | bytes 3145736 | tf_op jit(solution)/shard_map/ppermute | solution.py:33
  178.9 0.9 copy-start.11
  179.8 0.9 copy-start.12
  180.8 1.0 copy-start.10
  189.0 10.6 %collective-permute-start.25 = (bf16[128,896]{1,0:T(8,128)(2,1)S(1)}, bf16[128,896]{1,0:T(8,128)(2,1)S(1)}, u32[]{:S(2)}, u32[]{:S(2)}) collective-permute-start(bf16[128,896]{1,0:T(8,128)(2,1)S(1)} %get-tuple-element.64), channel_id=1, source_target_pairs={{0,34},{32,0},{2,32},{34,2},{1,35},{33,1},{3,33},{35,3},{4,38},{36... | collective-permute-start | bytes 688136 | tf_op jit(solution)/shard_map/ppermute | solution.py:43
  189.7 9.9 %collective-permute-start.24 = (bf16[128,896]{1,0:T(8,128)(2,1)S(1)}, bf16[128,896]{1,0:T(8,128)(2,1)S(1)}, u32[]{:S(2)}, u32[]{:S(2)}) collective-permute-start(bf16[128,896]{1,0:T(8,128)(2,1)S(1)} %get-tuple-element.65), channel_id=1, source_target_pairs={{0,2},{32,34},{2,0},{34,32},{1,3},{33,35},{3,1},{35,33},{4,6},{36,... | collective-permute-start | bytes 688136 | tf_op jit(solution)/shard_map/ppermute | solution.py:43
  190.6 13.0 %collective-permute-start.23 = (bf16[128,896]{1,0:T(8,128)(2,1)S(1)}, bf16[128,896]{1,0:T(8,128)(2,1)S(1)}, u32[]{:S(2)}, u32[]{:S(2)}) collective-permute-start(bf16[128,896]{1,0:T(8,128)(2,1)S(1)} %get-tuple-element.63), channel_id=1, source_target_pairs={{0,32},{32,2},{2,34},{34,0},{1,33},{33,3},{3,35},{35,1},{4,36},{36... | collective-permute-start | bytes 688136 | tf_op jit(solution)/shard_map/ppermute | solution.py:43
  205.4 34.0 %copy-start.4 = (f32[512,1024]{1,0:T(8,128)S(1)}, f32[512,1024]{1,0:T(8,128)}, u32[]{:S(2)}) copy-start(f32[512,1024]{1,0:T(8,128)} %get-tuple-element.42) | copy-start | bytes 6291460
  205.4 14.1 %all-to-all-start.1 = ((bf16[8,16,896]{2,1,0:T(8,128)(2,1)}), bf16[8,16,896]{2,1,0:T(8,128)(2,1)S(1)}, u32[]{:S(2)}, u32[]{:S(2)}) async-start(bf16[8,16,896]{2,1,0:T(8,128)(2,1)} %bitcast.63), calls=%async_computation.1 | async-start | bytes 458752 | tf_op jit(solution)/shard_map/all_to_all | solution.py:390
  211.6 26.8 %collective-permute-start.22 = (bf16[512,1024]{1,0:T(8,128)(2,1)}, bf16[512,1024]{1,0:T(8,128)(2,1)S(1)}, u32[]{:S(2)}, u32[]{:S(2)}) collective-permute-start(bf16[512,1024]{1,0:T(8,128)(2,1)} %add_convert_fusion), channel_id=1, source_target_pairs={{4,0},{8,4},{12,8},{16,12},{20,16},{24,20},{28,24},{32,28},{36,32}... | collective-permute-start | bytes 3145736 | tf_op jit(solution)/shard_map/ppermute | solution.py:33
  220.1 2.8 %collective-permute-start.26 = (f32[16,896]{1,0:T(8,128)S(1)}, f32[16,896]{1,0:T(8,128)S(1)}, u32[]{:S(2)}, u32[]{:S(2)}) collective-permute-start(f32[16,896]{1,0:T(8,128)S(1)} %get-tuple-element.56), channel_id=1, source_target_pairs={{0,1},{1,0},{2,3},{3,2},{4,5},{5,4},{6,7},{7,6},{8,9},{9,8},{10,11... | collective-permute-start | bytes 172040 | tf_op jit(solution)/shard_map/ppermute | solution.py:61
  222.9 25.7 %collective-permute-start.27 = (f32[16,1792]{1,0:T(8,128)S(1)}, f32[16,1792]{1,0:T(8,128)S(1)}, u32[]{:S(2)}, u32[]{:S(2)}) collective-permute-start(f32[16,1792]{1,0:T(8,128)S(1)} %maximum_select_fusion.1), channel_id=1, source_target_pairs={{0,2},{2,0},{1,3},{3,1},{4,6},{6,4},{5,7},{7,5},{8,10},{10,8},{9,1... | collective-permute-start | bytes 344072 | tf_op jit(solution)/shard_map/ppermute | solution.py:61
  238.4 1.0 copy-start.7
  244.3 9.1 %all-to-all-start.2 = ((f32[8,8,128]{2,1,0:T(8,128)}), f32[8,8,128]{2,1,0:T(8,128)S(1)}, u32[]{:S(2)}, u32[]{:S(2)}) async-start(f32[8,8,128]{2,1,0:T(8,128)} %broadcast_in_dim_broadcast_in_dim_broadcast_in_dim.6), calls=%async_computation.2 | async-start | bytes 65536 | tf_op jit(solution)/shard_map/all_to_all | solution.py:66
  254.1 17.1 %all-to-all-start.3 = ((f32[32,8,128]{2,1,0:T(8,128)}), f32[32,8,128]{2,1,0:T(8,128)S(1)}, u32[]{:S(2)}, u32[]{:S(2)}) async-start(f32[32,8,128]{2,1,0:T(8,128)} %broadcast_in_dim_broadcast_in_dim_broadcast_in_dim.7), calls=%async_computation.3 | async-start | bytes 262144 | tf_op jit(solution)/shard_map/all_to_all | solution.py:66

commit v5 on v4

--- a/solution.py
+++ b/solution.py
@@ -43,18 +43,12 @@
     return lax.ppermute(value, X_AXES, [(at(s), at((s + steps) % 4)) for s in range(4)])
 
 
-def across_x(value, steps):
-    pairs = []
+def next_row(value):
     depth = lax.axis_size("seq_2")
-    for low in range(2):
-        for z in range(depth):
-            for high in range(2):
-                step = steps if z else (1 if low else -1)
-                to = (2 * high + low + step) % 4
-                pairs.append(
-                    ((low * depth + z) * 2 + high, ((to % 2) * depth + z) * 2 + to // 2)
-                )
-    return lax.ppermute(value, ("seq_1", "seq_2", "dp_0"), pairs)
+    count = lax.axis_size(SEQ)
+    return lax.ppermute(
+        value, SEQ, [(s, s + depth) for s in range(depth - 1, count - depth, depth)]
+    )
 
 
 def swap(value, axis):
@@ -97,10 +91,12 @@
     return jnp.sum(e, axis=0, keepdims=True)
 
 
-def near_kernel(at_ref, q_ref, k0_ref, v0_ref, h1_ref, p_ref, pf_ref, acc_ref, tot_ref):
+def near_kernel(
+    at_ref, q_ref, k0_ref, v0_ref, k1_ref, v1_ref, p_ref, pf_ref, acc_ref, tot_ref
+):
     q = two_heads(q_ref)
     key, query = places()
-    t, e = squashed(h1_ref[:TOK_DEV], q)
+    t, e = squashed(k1_ref[...], q)
     e = e * jnp.where(at_ref[0] >= 1, 1.0, 0.0)
     p1 = e.astype(BF16)
     p_ref[0, :TOK_DEV] = p1
@@ -112,23 +108,23 @@
     p_ref[0, TOK_DEV:] = p0
     pf_ref[0, TOK_DEV:] = (e * (1.0 - t * t)).astype(BF16)
     total = total + row_sum(e)
-    acc_ref[0] = dot(h1_ref[TOK_DEV:], p1, TN) + dot(v0_ref[...], p0, TN)
+    acc_ref[0] = dot(v1_ref[...], p1, TN) + dot(v0_ref[...], p0, TN)
     tot_ref[0] = jnp.broadcast_to(total, tot_ref.shape[1:])
 
 
 def far_kernel(
-    at_ref, q_ref, h2_ref, acc_ref, tot_ref,
+    at_ref, q_ref, k2_ref, v2_ref, acc_ref, tot_ref,
     p_ref, pf_ref, attn_ref, inv_ref, out0_ref, out1_ref, out2_ref, out3_ref,
 ):
     key, query = places()
-    t, e = squashed(h2_ref[:TOK_DEV], two_heads(q_ref))
+    t, e = squashed(k2_ref[...], two_heads(q_ref))
     e = jnp.where(key > query + jnp.where(at_ref[0] >= 2, 0, 4 * TOK_DEV), e, 0.0)
     p = e.astype(BF16)
     p_ref[0] = p
     pf_ref[0] = (e * (1.0 - t * t)).astype(BF16)
     inverse = 1.0 / (tot_ref[0, :1] + row_sum(e))
     inv_ref[0] = jnp.broadcast_to(inverse, inv_ref.shape[1:])
-    out = ((acc_ref[0] + dot(h2_ref[TOK_DEV:], p, TN)) * inverse).astype(BF16)
+    out = ((acc_ref[0] + dot(v2_ref[...], p, TN)) * inverse).astype(BF16)
     out = jnp.concatenate([out[:, h * TOK_DEV : (h + 1) * TOK_DEV] for h in range(GROUP)], 0)
     attn_ref[0] = out
     place = (pl.program_id(0) + 4 - at_ref[1]) % 4
@@ -144,7 +140,7 @@
 
 
 def far_grad_kernel(
-    at_ref, scale_ref, q_ref, h2_ref, p_ref, pf_ref, inv_ref, attn_ref, m_own_ref, m_oth_ref,
+    at_ref, scale_ref, q_ref, v2_ref, p_ref, pf_ref, inv_ref, attn_ref, m_own_ref, m_oth_ref,
     wa_ref, wc_ref, wbl_ref, wbh_ref, wdl_ref, wdh_ref,
     d2_ref, g_ref, delta_ref, ds_ref, raw_ref,
 ):
@@ -163,23 +159,23 @@
     )
     delta = row_sum(g.astype(F32) * attn.astype(F32))
     delta_ref[0] = jnp.broadcast_to(delta, delta_ref.shape[1:])
-    dscore = score_terms(h2_ref[TOK_DEV:], g, delta, pf_ref[0])
+    dscore = score_terms(v2_ref[...], g, delta, pf_ref[0])
     ds_ref[0] = dscore
     d2_ref[:TOK_DEV] = (dot(dscore, two_heads(q_ref), NN) * (SCALE * act_scale)).astype(BF16)
     d2_ref[TOK_DEV:] = (dot(p_ref[0], g, NT) * act_scale).astype(BF16)
 
 
 def near_grad_kernel(
-    scale_ref, q_ref, k0_ref, v0_ref, h1_ref, h2_ref, p_ref, pf_ref, g_ref, delta_ref, ds_ref,
+    scale_ref, q_ref, k0_ref, v0_ref, k1_ref, v1_ref, k2_ref, p_ref, pf_ref, g_ref, delta_ref, ds_ref,
     dq_ref, d0_ref, d1_ref, sq_ref,
 ):
     act_scale = scale_ref[0]
     q = two_heads(q_ref)
     g = g_ref[0]
     delta = delta_ref[0, :1]
-    dq = dot(h2_ref[...], ds_ref[0], TN)
+    dq = dot(k2_ref[...], ds_ref[0], TN)
     for k, v, at, out in (
-        (h1_ref[:TOK_DEV], h1_ref[TOK_DEV:], 0, d1_ref),
+        (k1_ref[...], v1_ref[...], 0, d1_ref),
         (k0_ref[...], v0_ref[...], TOK_DEV, d0_ref),
     ):
         dscore = score_terms(v, g, delta, pf_ref[0, at : at + TOK_DEV])
@@ -245,53 +241,53 @@
     )
 
 
-def near_forward(where, q, k, v, h1):
+def near_forward(where, q, k, v, k1, v1):
     return call(
         near_kernel, 1,
-        [HEAD_COLS, KV_COLS, KV_COLS, BOTH_COLS],
+        [HEAD_COLS] + [KV_COLS] * 4,
         [of_head(2 * TOK_DEV), of_head(2 * TOK_DEV), of_head(D), of_head(8)],
         [per_head(2 * TOK_DEV, BF16), per_head(2 * TOK_DEV, BF16), per_head(D, F32),
          per_head(8, F32)],
         4, 9,
-    )(where, q, k, v, h1)
-
-
-def far_forward(where, q, h2, acc, tot):
+    )(where, q, k, v, k1, v1)
+
+
+def far_forward(where, q, k2, v2, acc, tot):
     return call(
         far_kernel, 1,
-        [HEAD_COLS, BOTH_COLS, of_head(D), of_head(8)],
+        [HEAD_COLS, KV_COLS, KV_COLS, of_head(D), of_head(8)],
         [of_head(TOK_DEV), of_head(TOK_DEV), ATTN_ROWS, of_head(8)]
         + [pl.BlockSpec((GROUP * D, TOK_DEV), lambda h, *_: (0, 0))] * 4,
         [per_head(TOK_DEV, BF16), per_head(TOK_DEV, BF16),
          jax.ShapeDtypeStruct((KV_HEADS, GROUP * D, TOK_DEV), BF16), per_head(8, F32)]
         + [jax.ShapeDtypeStruct((GROUP * D, TOK_DEV), BF16)] * 4,
         2, 7,
-    )(where, q, h2, acc, tot)
-
-
-def far_backward(where, scale, q, h2, p, pf, inv, attn, m_own, m_oth, weights):
+    )(where, q, k2, v2, acc, tot)
+
+
+def far_backward(where, scale, q, v2, p, pf, inv, attn, m_own, m_oth, weights):
     full = pl.BlockSpec((TOK_DEV, HALF), lambda h, *_: (0, 0))
     rel = lambda rows: pl.BlockSpec((1, rows, HALF), lambda h, at, *_: ((at[1] + 4 - h) % 4, 0, 0))
     return call(
         far_grad_kernel, 2,
-        [HEAD_COLS, BOTH_COLS, of_head(TOK_DEV), of_head(TOK_DEV), of_head(8), ATTN_ROWS, full,
+        [HEAD_COLS, KV_COLS, of_head(TOK_DEV), of_head(TOK_DEV), of_head(8), ATTN_ROWS, full,
          full, rel(D), rel(D)] + [rel(D // 2)] * 4,
         [BOTH_COLS, of_head(D), of_head(8), of_head(TOK_DEV)],
         [flat(2 * TOK_DEV, BF16), per_head(D, BF16), per_head(8, F32), per_head(TOK_DEV, BF16)],
         3 + 7, 15, [pltpu.VMEM((D, SCORES), F32)],
-    )(where, scale, q, h2, p, pf, inv, attn, m_own, m_oth, *weights)
-
-
-def near_backward(scale, q, k, v, h1, h2, p, pf, g, delta, dscore):
+    )(where, scale, q, v2, p, pf, inv, attn, m_own, m_oth, *weights)
+
+
+def near_backward(scale, q, k, v, k1, v1, k2, p, pf, g, delta, dscore):
     return call(
         near_grad_kernel, 1,
-        [HEAD_COLS, KV_COLS, KV_COLS, BOTH_COLS, KV_COLS, of_head(2 * TOK_DEV),
-         of_head(2 * TOK_DEV), of_head(D), of_head(8), of_head(TOK_DEV)],
+        [HEAD_COLS] + [KV_COLS] * 5
+        + [of_head(2 * TOK_DEV), of_head(2 * TOK_DEV), of_head(D), of_head(8), of_head(TOK_DEV)],
         [HEAD_COLS, BOTH_COLS, BOTH_COLS, pl.BlockSpec((8, 128), lambda h, *_: (h, 0))],
         [jax.ShapeDtypeStruct((TOK_DEV, WIDTH), BF16), flat(2 * TOK_DEV, F32),
          flat(2 * TOK_DEV, BF16), jax.ShapeDtypeStruct((8 * KV_HEADS, 128), F32)],
         9, 13,
-    )(scale, q, k, v, h1, h2, p, pf, g, delta, dscore)
+    )(scale, q, k, v, k1, v1, k2, p, pf, g, delta, dscore)
 
 
 def weight_product(where, a_own, a_oth, m0, m1, m2, m3):
@@ -320,9 +316,13 @@
     start = index * TOK_DEV
     where = jnp.stack([index, lax.axis_index("seq_0"), x_lo, 2 * x_hi + x_lo]).astype(jnp.int32)
 
-    kv = jnp.concatenate([k_rows, v_rows], 0)
-    h1 = shifted(kv, 1)
-    h2 = shifted(h1, 1)
+    at_end = lax.axis_index("seq_2") == lax.axis_size("seq_2") - 1
+    h1k = shifted(k_rows, 1)
+    h1v = jnp.where(at_end, next_row(v_rows), v_rows)
+    h1v = ring(h1v, "seq_2", 1)
+    h2k = shifted(h1k, 1)
+    h2v = jnp.where(at_end, next_row(h1v), h1v)
+    h2v = ring(h2v, "seq_2", 1)
 
     slots = TOK_DEV * lax.axis_size(SEQ) * lax.axis_size(DP)
     count = jnp.clip(length, 0, TOK_DEV * lax.axis_size(SEQ)).astype(F32).reshape(1)
@@ -347,20 +347,20 @@
     mid = HEAD_DIM // 2
     w_far = [ring(w_up[:mid], "seq_0", 1), ring(w_down[mid:], "seq_0", -1)]
     wa = jnp.stack([w_z, w_up, jnp.concatenate(w_far, 0), w_down])
-    wbl = across_x(wa[:, :mid], 1)
-    wbh = across_x(wa[:, mid:], -1)
+    wbl = ring_x(wa[:, :mid], 1)
+    wbh = ring_x(wa[:, mid:], -1)
     wc = swap(wa, "dp_1")
     wdl = swap(wbl, "dp_1")
     wdh = swap(wbh, "dp_1")
 
-    p, pf, acc, tot = near_forward(where, q_rows, k_rows, v_rows, h1)
-    p2, pf2, attn, inv, *away = far_forward(where, q_rows, h2, acc, tot)
+    p, pf, acc, tot = near_forward(where, q_rows, k_rows, v_rows, h1k, h1v)
+    p2, pf2, attn, inv, *away = far_forward(where, q_rows, h2k, h2v, acc, tot)
     attn_parts = (
         away[0], ring(away[1], "seq_0", 1), ring(away[2], "seq_0", 2), ring(away[3], "seq_0", -1)
     )
 
     d2, g, delta, dscore = far_backward(
-        where, act_scale, q_rows, h2, p2, pf2, inv, attn, m_own, m_oth,
+        where, act_scale, q_rows, h2v, p2, pf2, inv, attn, m_own, m_oth,
         (wa, wc, wbl, wbh, wdl, wdh),
     )
     attn_parts, _ = lax.optimization_barrier((attn_parts, delta))
@@ -369,7 +369,7 @@
 
     r1 = shifted(d2, -1)
     dq, d0, d1, dq_sq = near_backward(
-        act_scale, q_rows, k_rows, v_rows, h1, h2, p, pf, g, delta, dscore
+        act_scale, q_rows, k_rows, v_rows, h1k, h1v, h2k, p, pf, g, delta, dscore
     )
     part = weight_product(
         where, a_own, a_oth, m0, m1, m2, m3

time: 274 us -> 281 us (1.026)
  blocking collectives: 23.6 us -> 0 us
  waiting for transfers between devices: 101 us -> 123 us
  starting transfers between devices: 78.4 us -> 86.7 us
    ppermute x2, waiting for transfers between devices: 33.5 us -> 0.01 us  [next_row(): lax.ppermute(value, SEQ, [(s, s + depth) for s in range(depth - 1, count...]
    all_to_all x1 -> x0, blocking collectives: 23.6 us -> none  [for_each(): lax.all_to_all(jnp.broadcast_to(value[None], (size, *value.shape)), axis,...]
    ppermute x9, starting transfers between devices: 36.2 us -> 15.9 us  [swap(): return lax.ppermute(value, axis, [(0, 1), (1, 0)])]
    ppermute x4, waiting for transfers between devices: 14.4 us -> 33.1 us  [shifted(): lax.ppermute(value, SEQ, [(source, source + steps) for source in range(in...]
    all_to_all x1, starting transfers between devices: 3.53 us -> 20.2 us  [all_steps(): pieces = lax.all_to_all(part, 'seq_2', 0, 0, tiled=True)]
    all_to_all x2 -> x3, waiting for transfers between devices: 12.1 us -> 27.9 us  [for_each(): lax.all_to_all(jnp.broadcast_to(value[None], (size, *value.shape)), axis,...]
    ppermute x3 -> x5, waiting for transfers between devices: 4.06 us -> 17.6 us  [ring_x(): lax.ppermute(value, X_AXES, [(at(s), at((s + steps) % 4)) for s in range(...]
    all_to_all x2 -> x3, starting transfers between devices: 12.3 us -> 22.6 us  [for_each(): lax.all_to_all(jnp.broadcast_to(value[None], (size, *value.shape)), axis,...]
  transfers between devices with their start and end apart: 31 -> 36, of which waited for: 11 -> 15; matrix products, arithmetic and copies ran while one was open for 6% -> 6% of each run, Pallas kernels for 14% -> 14%
where the time goes in v5:
time: 281 us; the launch traced here: 279 us
  waiting for transfers between devices  123 us (44%)
  starting transfers between devices  86.7 us (31%)
  Pallas kernels  38.1 us (14%)
  other arithmetic  14.6 us (5%)
  local copies, waits for them, and re-layouts  10.9 us (4%)
  between operations  6.24 us (2%)
    ppermute x12, waiting for transfers between devices, ring(): lax.ppermute(value, axis, [(s, (s + steps) % count) for s in range(count)])  38.2 us
    ppermute x4, waiting for transfers between devices, shifted(): lax.ppermute(value, SEQ, [(source, source + steps) for source in range(in...  33.1 us
    all_to_all x3, waiting for transfers between devices, for_each(): lax.all_to_all(jnp.broadcast_to(value[None], (size, *value.shape)), axis,...  27.9 us
    all_to_all x3, starting transfers between devices, for_each(): lax.all_to_all(jnp.broadcast_to(value[None], (size, *value.shape)), axis,...  22.6 us
    all_to_all x1, starting transfers between devices, all_steps(): pieces = lax.all_to_all(part, 'seq_2', 0, 0, tiled=True)  20.2 us
    ppermute x5, waiting for transfers between devices, ring_x(): lax.ppermute(value, X_AXES, [(at(s), at((s + steps) % 4)) for s in range(...  17.6 us
    ppermute x12, starting transfers between devices, ring(): lax.ppermute(value, axis, [(s, (s + steps) % count) for s in range(count)])  17.3 us
    ppermute x9, starting transfers between devices, swap(): return lax.ppermute(value, axis, [(0, 1), (1, 0)])  15.9 us
  transfers between devices with their start and end apart: 36, of which 15 were waited for; matrix products, arithmetic and copies ran while one was open for 6% of the time, Pallas kernels for 14%

profile of v5, /device:TPU:1, one launch (start us, length us, event | category | flops | bytes accessed | tf_op | source)
XLA Modules:
  0.0 279.4 jit_solution(16127124810977319690)
XLA Ops:
  0.7 0.9 copy-done
  1.5 0.8 broadcast_in_dim.30
  2.3 9.0 %all-to-all-start = ((bf16[8,32,896]{2,1,0:T(8,128)(2,1)}), bf16[8,32,896]{2,1,0:T(8,128)(2,1)S(1)}, u32[]{:S(2)}, u32[]{:S(2)}) async-start(bf16[8,32,896]{2,1,0:T(8,128)(2,1)} %broadcast_in_dim.30), calls=%async_computation | async-start | bytes 917504 | tf_op jit(solution)/shard_map/all_to_all | solution.py:60
  12.0 15.8 %all-to-all-done = bf16[8,32,896]{2,1,0:T(8,128)(2,1)S(1)} async-done(((bf16[8,32,896]{2,1,0:T(8,128)(2,1)}), bf16[8,32,896]{2,1,0:T(8,128)(2,1)S(1)}, u32[]{:S(2)}, u32[]{:S(2)}) %all-to-all-start) | async-done | bytes 458784 | tf_op jit(solution)/shard_map/all_to_all | solution.py:60
  27.8 2.7 collective-permute-start.10
  30.6 9.3 %collective-permute-done.10 = bf16[256,896]{1,0:T(8,128)(2,1)S(1)} collective-permute-done((bf16[256,896]{1,0:T(8,128)(2,1)S(1)}, bf16[256,896]{1,0:T(8,128)(2,1)S(1)}, u32[]{:S(2)}, u32[]{:S(2)}) %collective-permute-start.10) | collective-permute-done | bytes 458784 | tf_op jit(solution)/shard_map/ppermute | solution.py:38
  39.9 3.5 %collective-permute-start.11 = (bf16[128,896]{1,0:T(8,128)(2,1)S(1)}, bf16[128,896]{1,0:T(8,128)(2,1)S(1)}, u32[]{:S(2)}, u32[]{:S(2)}) collective-permute-start(bf16[128,896]{1,0:T(8,128)(2,1)S(1)} %slice.61), channel_id=1, source_target_pairs={{0,192},{64,0},{128,64},{192,128},{1,193},{65,1},{129,65},{193,129... | collective-permute-start | bytes 688136 | tf_op jit(solution)/shard_map/ppermute | solution.py:38
  43.5 0.9 broadcast_select_fusion.1
  44.4 2.5 collective-permute-done.11
  46.9 3.2 %collective-permute-done.9 = bf16[128,896]{1,0:T(8,128)(2,1)S(1)} collective-permute-done((bf16[128,896]{1,0:T(8,128)(2,1)S(1)}, bf16[128,896]{1,0:T(8,128)(2,1)S(1)}, u32[]{:S(2)}, u32[]{:S(2)}) %collective-permute-start.9) | collective-permute-done | bytes 229408 | tf_op jit(solution)/shard_map/ppermute | solution.py:38
  50.2 1.3 pad_maximum_fusion.wa_ref
  51.5 2.7 collective-permute-start.12
  54.2 1.5 fusion.4
  55.6 1.2 collective-permute-start.13
  56.9 1.5 collective-permute-start.14
  59.0 1.8 collective-permute-start
  60.8 1.3 collective-permute-start.2
  62.1 0.7 collective-permute-start.6
  63.1 10.5 %collective-permute-done.2.k1_ref = bf16[256,1024]{1,0:T(8,128)(2,1)S(1)} collective-permute-done((bf16[256,1024]{1,0:T(8,128)(2,1)}, bf16[256,1024]{1,0:T(8,128)(2,1)S(1)}, u32[]{:S(2)}, u32[]{:S(2)}) %collective-permute-start.2) | collective-permute-done | bytes 524320 | tf_op jit(solution)/shard_map/ppermute | solution.py:33
  73.6 0.9 collective-permute-start.22
  74.5 13.3 %collective-permute-done.13.wbl_ref = bf16[4,128,896]{2,1,0:T(8,128)(2,1)} collective-permute-done((bf16[4,128,896]{2,1,0:T(8,128)(2,1)}, bf16[4,128,896]{2,1,0:T(8,128)(2,1)}, u32[]{:S(2)}, u32[]{:S(2)}) %collective-permute-start.13) | collective-permute-done | bytes 917536 | tf_op jit(solution)/shard_map/ppermute | solution.py:43
  87.8 1.2 collective-permute-start.15
  89.0 1.3 collective-permute-start.5
  90.3 0.9 collective-permute-start.16
  91.2 0.8 broadcast_select_fusion
  92.0 1.0 pad_maximum_fusion.2.m0_ref
  93.1 8.7 %collective-permute-done.5.k2_ref = bf16[256,1024]{1,0:T(8,128)(2,1)S(1)} collective-permute-done((bf16[256,1024]{1,0:T(8,128)(2,1)S(1)}, bf16[256,1024]{1,0:T(8,128)(2,1)S(1)}, u32[]{:S(2)}, u32[]{:S(2)}) %collective-permute-start.5) | collective-permute-done | bytes 524320 | tf_op jit(solution)/shard_map/ppermute | solution.py:33
  101.8 5.4 %collective-permute-start.24 = (bf16[512,896]{1,0:T(8,128)(2,1)}, bf16[512,896]{1,0:T(8,128)(2,1)}, u32[]{:S(2)}, u32[]{:S(2)}) collective-permute-start(bf16[512,896]{1,0:T(8,128)(2,1)} %pad_maximum_fusion.2.m0_ref), channel_id=1, source_target_pairs={{0,192},{64,0},{128,64},{192,128},{1,193},{65,1},{129,65},{193,129... | collective-permute-start | bytes 2752520 | tf_op jit(solution)/shard_map/ppermute | solution.py:38
  108.6 6.8 %shard_map.101 = (bf16[4,512,512]{2,1,0:T(8,128)(2,1)}, bf16[4,512,512]{2,1,0:T(8,128)(2,1)}, f32[4,256,512]{2,1,0:T(8,128)}, f32[4,8,512]{2,1,0:T(8,128)}) custom-call(s32[4]{0:T(128)} %pad_add_fusion.at_ref, bf16[256,2048]{1,0:T(8,128)(2,1)} %bitcast.49, bf16[256,1024]{1,0:T(8,128)(2,1)} %bitcast.62, bf16[256,1024]{1,0:T(8,128)(2,1)} %bitcast.54, ...), custom_call_target="tpu_custom_call" | custom-call | flops 1073741824 | bytes 9437184 | tf_op jit(solution)/shard_map/pallas_call | solution.py:245
  115.4 3.3 %collective-permute-done.7.v2_ref = bf16[256,1024]{1,0:T(8,128)(2,1)S(1)} collective-permute-done((bf16[256,1024]{1,0:T(8,128)(2,1)}, bf16[256,1024]{1,0:T(8,128)(2,1)S(1)}, u32[]{:S(2)}, u32[]{:S(2)}) %collective-permute-start.7) | collective-permute-done | bytes 524320 | tf_op jit(solution)/shard_map/ppermute | solution.py:38
  118.7 3.2 %collective-permute-start.1 = (f32[1]{0:T(128)}, f32[1]{0:T(128)}, u32[]{:S(2)}, u32[]{:S(2)}) collective-permute-start(f32[1]{0:T(128)} %add.53), channel_id=1, source_target_pairs={{0,2},{2,0},{1,3},{3,1},{4,6},{6,4},{5,7},{7,5},{8,10},{10,8},{9,1... | collective-permute-start | bytes 20 | tf_op jit(solution)/shard_map/ppermute | solution.py:55
  121.9 6.7 %shard_map.102 = (bf16[4,256,512]{2,1,0:T(8,128)(2,1)}, bf16[4,256,512]{2,1,0:T(8,128)(2,1)}, bf16[4,512,256]{2,1,0:T(8,128)(2,1)}, f32[4,8,512]{2,1,0:T(8,128)}...) custom-call(s32[4]{0:T(128)} %pad_add_fusion.at_ref, ...), custom_call_target="tpu_custom_call" | custom-call | flops 536870912 | bytes 7340032 | tf_op jit(solution)/shard_map/pallas_call | solution.py:256
  128.7 1.2 collective-permute-start.19
  129.8 1.6 collective-permute-start.20
  132.1 10.4 %shard_map.103 = (bf16[512,1024]{1,0:T(8,128)(2,1)}, bf16[4,256,512]{2,1,0:T(8,128)(2,1)}, f32[4,8,512]{2,1,0:T(8,128)}, bf16[4,256,512]{2,1,0:T(8,128)(2,1)}) custom-call(s32[4]{0:T(128)} %pad_add_fusion.at_ref, f32[1]{0:T(128)S(6)} %div.6.scale_ref, bf16[256,2048]{1,0:T(8,128)(2,1)} %bitcast.51, bf16[256,1024]{1,0:T(8,128)(2,1)} %copy-done.4, ...), custom_call_target="tpu_custom_call" | custom-call | flops 2684354560 | bytes 15728640 | tf_op jit(solution)/shard_map/pallas_call | solution.py:271
  143.3 2.0 collective-permute-start.21
  145.6 2.4 collective-permute-start.25
  148.0 1.3 collective-permute-start.17
  149.2 19.3 %collective-permute-done.23.m1_ref = bf16[512,896]{1,0:T(8,128)(2,1)S(1)} collective-permute-done((bf16[512,896]{1,0:T(8,128)(2,1)}, bf16[512,896]{1,0:T(8,128)(2,1)S(1)}, u32[]{:S(2)}, u32[]{:S(2)}) %collective-permute-start.23) | collective-permute-done | bytes 917536 | tf_op jit(solution)/shard_map/ppermute | solution.py:38
  168.5 0.9 copy-done.16
  169.4 0.9 copy-done.17
  170.4 1.1 copy-done.15
  171.4 5.9 %weight_product.1 = bf16[4,128,896]{2,1,0:T(8,128)(2,1)} custom-call(s32[4]{0:T(128)} %pad_add_fusion.at_ref, bf16[4,512,256]{2,1,0:T(8,128)(2,1)} %copy-done.10, bf16[4,512,256]{2,1,0:T(8,128)(2,1)} %copy-done.15, bf16[512,896]{1,0:T(8,128)(2,1)} %pad_maximum_fusion.2.m0_ref, bf16[512,896]{1,0:T(8,128)(2,1)} %copy-done.16, bf16[512,896]{1,0:T(8,128)(2,1)} %copy-done.17, ...), custom_call_target="tpu_custom_call" | custom-call | flops 1879048192 | bytes 7340032 | tf_op jit(solution)/shard_map/weight_product/pallas_call | solution.py:295
  177.4 1.2 slice_bitcast_fusion.4
  178.8 1.2 collective-permute-start.28
  180.1 8.3 %shard_map.104 = (bf16[256,2048]{1,0:T(8,128)(2,1)}, f32[512,1024]{1,0:T(8,128)}, bf16[512,1024]{1,0:T(8,128)(2,1)}, f32[32,128]{1,0:T(8,128)}) custom-call(f32[1]{0:T(128)S(6)} %div.6.scale_ref, bf16[256,2048]{1,0:T(8,128)(2,1)} %bitcast.52, bf16[256,1024]{1,0:T(8,128)(2,1)} %bitcast.63, bf16[256,1024]{1,0:T(8,128)(2,1)} %bitcast.55, ...), custom_call_target="tpu_custom_call" | custom-call | flops 2415919104 | bytes 13631488 | tf_op jit(solution)/shard_map/pallas_call | solution.py:282
  188.4 4.3 %collective-permute-done.27 = bf16[128,896]{1,0:T(8,128)(2,1)S(1)} collective-permute-done((bf16[128,896]{1,0:T(8,128)(2,1)S(1)}, bf16[128,896]{1,0:T(8,128)(2,1)S(1)}, u32[]{:S(2)}, u32[]{:S(2)}) %collective-permute-start.27) | collective-permute-done | bytes 229408 | tf_op jit(solution)/shard_map/ppermute | solution.py:43
  192.7 1.7 fusion.3
  194.5 20.2 %all-to-all-start.1 = ((bf16[8,16,896]{2,1,0:T(8,128)(2,1)}), bf16[8,16,896]{2,1,0:T(8,128)(2,1)S(1)}, u32[]{:S(2)}, u32[]{:S(2)}) async-start(bf16[8,16,896]{2,1,0:T(8,128)(2,1)} %bitcast.26), calls=%async_computation.1 | async-start | bytes 458752 | tf_op jit(solution)/shard_map/all_to_all | solution.py:390
  214.7 2.8 add_convert_fusion
  217.4 1.3 collective-permute-start.26
  218.7 5.9 %all-to-all-done.1 = bf16[8,16,896]{2,1,0:T(8,128)(2,1)S(1)} async-done(((bf16[8,16,896]{2,1,0:T(8,128)(2,1)}), bf16[8,16,896]{2,1,0:T(8,128)(2,1)S(1)}, u32[]{:S(2)}, u32[]{:S(2)}) %all-to-all-start.1) | async-done | bytes 229408 | tf_op jit(solution)/shard_map/all_to_all | solution.py:390
  225.3 2.1 collective-permute-start.30
  227.4 1.3 slice_reduce_fusion
  228.8 1.3 collective-permute-start.31
  230.1 13.9 %collective-permute-done.26 = bf16[512,1024]{1,0:T(8,128)(2,1)S(1)} collective-permute-done((bf16[512,1024]{1,0:T(8,128)(2,1)}, bf16[512,1024]{1,0:T(8,128)(2,1)S(1)}, u32[]{:S(2)}, u32[]{:S(2)}) %collective-permute-start.26) | collective-permute-done | bytes 1048608 | tf_op jit(solution)/shard_map/ppermute | solution.py:33
  244.0 1.0 copy-done.9
  245.0 2.4 multiply_reduce_fusion
  249.9 4.6 %all-to-all-start.2 = ((f32[8,8,128]{2,1,0:T(8,128)}), f32[8,8,128]{2,1,0:T(8,128)S(1)}, u32[]{:S(2)}, u32[]{:S(2)}) async-start(f32[8,8,128]{2,1,0:T(8,128)} %broadcast_in_dim_broadcast_in_dim_broadcast_in_dim.6), calls=%async_computation.2 | async-start | bytes 65536 | tf_op jit(solution)/shard_map/all_to_all | solution.py:60
  254.5 0.7 maximum_select_fusion
  255.2 4.0 %all-to-all-done.2 = f32[8,8,128]{2,1,0:T(8,128)S(1)} async-done(((f32[8,8,128]{2,1,0:T(8,128)}), f32[8,8,128]{2,1,0:T(8,128)S(1)}, u32[]{:S(2)}, u32[]{:S(2)}) %all-to-all-start.2) | async-done | bytes 32800 | tf_op jit(solution)/shard_map/all_to_all | solution.py:60
  260.0 9.0 %all-to-all-start.3 = ((f32[32,8,128]{2,1,0:T(8,128)}), f32[32,8,128]{2,1,0:T(8,128)S(1)}, u32[]{:S(2)}, u32[]{:S(2)}) async-start(f32[32,8,128]{2,1,0:T(8,128)} %broadcast_in_dim_broadcast_in_dim_broadcast_in_dim.7), calls=%async_computation.3 | async-start | bytes 262144 | tf_op jit(solution)/shard_map/all_to_all | solution.py:60
  269.0 1.0 slice_bitcast_fusion
  270.0 8.1 %all-to-all-done.3 = f32[32,8,128]{2,1,0:T(8,128)S(1)} async-done(((f32[32,8,128]{2,1,0:T(8,128)}), f32[32,8,128]{2,1,0:T(8,128)S(1)}, u32[]{:S(2)}, u32[]{:S(2)}) %all-to-all-start.3) | async-done | bytes 131104 | tf_op jit(solution)/shard_map/all_to_all | solution.py:60
  (80 shorter events, 5.4 us)
Async XLA Ops:
  0.6 0.9 copy-start
  0.6 42.8 %copy-start.5 = (bf16[1,256,1024]{2,1,0:T(8,128)(2,1)S(1)}, bf16[1,256,1024]{2,1,0:T(8,128)(2,1)}, u32[]{:S(2)}) copy-start(bf16[1,256,1024]{2,1,0:T(8,128)(2,1)} %param.8) | copy-start | bytes 1572868
  2.3 25.5 %all-to-all-start = ((bf16[8,32,896]{2,1,0:T(8,128)(2,1)}), bf16[8,32,896]{2,1,0:T(8,128)(2,1)S(1)}, u32[]{:S(2)}, u32[]{:S(2)}) async-start(bf16[8,32,896]{2,1,0:T(8,128)(2,1)} %broadcast_in_dim.30), calls=%async_computation | async-start | bytes 917504 | tf_op jit(solution)/shard_map/all_to_all | solution.py:60
  11.3 32.1 %collective-permute-start.3 = (bf16[256,1024]{1,0:T(8,128)(2,1)}, bf16[256,1024]{1,0:T(8,128)(2,1)S(1)}, u32[]{:S(2)}, u32[]{:S(2)}) collective-permute-start(bf16[256,1024]{1,0:T(8,128)(2,1)} %bitcast.53), channel_id=1, source_target_pairs={{28,60},{60,92},{92,124},{124,156},{156,188},{188,220},{220,252},{... | collective-permute-start | bytes 1572872 | tf_op jit(solution)/shard_map/ppermute | solution.py:49
  27.8 12.0 %collective-permute-start.10 = (bf16[256,896]{1,0:T(8,128)(2,1)S(1)}, bf16[256,896]{1,0:T(8,128)(2,1)S(1)}, u32[]{:S(2)}, u32[]{:S(2)}) collective-permute-start(bf16[256,896]{1,0:T(8,128)(2,1)S(1)} %bitcast.56), channel_id=1, source_target_pairs={{0,192},{64,0},{128,64},{192,128},{1,193},{65,1},{129,65},{193,129... | collective-permute-start | bytes 1376264 | tf_op jit(solution)/shard_map/ppermute | solution.py:38
  30.5 12.8 %collective-permute-start.8 = (bf16[256,896]{1,0:T(8,128)(2,1)S(1)}, bf16[256,896]{1,0:T(8,128)(2,1)S(1)}, u32[]{:S(2)}, u32[]{:S(2)}) collective-permute-start(bf16[256,896]{1,0:T(8,128)(2,1)S(1)} %bitcast.57), channel_id=1, source_target_pairs={{0,64},{64,128},{128,192},{192,0},{1,65},{65,129},{129,193},{193,1... | collective-permute-start | bytes 1376264 | tf_op jit(solution)/shard_map/ppermute | solution.py:38
  39.9 7.0 %collective-permute-start.11 = (bf16[128,896]{1,0:T(8,128)(2,1)S(1)}, bf16[128,896]{1,0:T(8,128)(2,1)S(1)}, u32[]{:S(2)}, u32[]{:S(2)}) collective-permute-start(bf16[128,896]{1,0:T(8,128)(2,1)S(1)} %slice.61), channel_id=1, source_target_pairs={{0,192},{64,0},{128,64},{192,128},{1,193},{65,1},{129,65},{193,129... | collective-permute-start | bytes 688136 | tf_op jit(solution)/shard_map/ppermute | solution.py:38
  43.4 6.8 %copy-start.11 = (bf16[256,896]{1,0:T(8,128)(2,1)}, bf16[256,896]{1,0:T(8,128)(2,1)S(1)}, u32[]{:S(2)}) copy-start(bf16[256,896]{1,0:T(8,128)(2,1)S(1)} %collective-permute-done.8) | copy-start | bytes 1376260
  43.4 6.7 %collective-permute-start.9 = (bf16[128,896]{1,0:T(8,128)(2,1)S(1)}, bf16[128,896]{1,0:T(8,128)(2,1)S(1)}, u32[]{:S(2)}, u32[]{:S(2)}) collective-permute-start(bf16[128,896]{1,0:T(8,128)(2,1)S(1)} %slice.60), channel_id=1, source_target_pairs={{0,64},{64,128},{128,192},{192,0},{1,65},{65,129},{129,193},{193,1... | collective-permute-start | bytes 688136 | tf_op jit(solution)/shard_map/ppermute | solution.py:38
  44.3 17.7 %collective-permute-start.4 = (bf16[256,1024]{1,0:T(8,128)(2,1)}, bf16[256,1024]{1,0:T(8,128)(2,1)S(1)}, u32[]{:S(2)}, u32[]{:S(2)}) collective-permute-start(bf16[256,1024]{1,0:T(8,128)(2,1)} %broadcast_select_fusion.1), channel_id=1, source_target_pairs={{0,4},{4,8},{8,12},{12,16},{16,20},{20,24},{24,28},{28,0},{1,5},{5... | collective-permute-start | bytes 1572872 | tf_op jit(solution)/shard_map/ppermute | solution.py:38
  51.5 4.2 %copy-start.1 = (bf16[4,256,896]{2,1,0:T(8,128)(2,1)}, bf16[4,256,896]{2,1,0:T(8,128)(2,1)S(1)}, u32[]{:S(2)}) copy-start(bf16[4,256,896]{2,1,0:T(8,128)(2,1)S(1)} %pad_maximum_fusion.wa_ref) | copy-start | bytes 5505028
  51.5 11.3 %copy-start.12 = (bf16[1,256,1792]{2,1,0:T(8,128)(2,1)S(1)}, bf16[1,256,1792]{2,1,0:T(8,128)(2,1)}, u32[]{:S(2)}) copy-start(bf16[1,256,1792]{2,1,0:T(8,128)(2,1)} %param.9) | copy-start | bytes 2752516
  51.5 77.2 %collective-permute-start.12 = (bf16[4,256,896]{2,1,0:T(8,128)(2,1)S(1)}, bf16[4,256,896]{2,1,0:T(8,128)(2,1)}, u32[]{:S(2)}, u32[]{:S(2)}) collective-permute-start(bf16[4,256,896]{2,1,0:T(8,128)(2,1)S(1)} %pad_maximum_fusion.wa_ref), channel_id=1, source_target_pairs={{0,1},{1,0},{2,3},{3,2},{4,5},{5,4},{6,7},{7,6},{8,9},{9,8},{10,11... | collective-permute-start | bytes 5505032 | tf_op jit(solution)/shard_map/ppermute | solution.py:55
  55.6 32.2 %collective-permute-start.13 = (bf16[4,128,896]{2,1,0:T(8,128)(2,1)}, bf16[4,128,896]{2,1,0:T(8,128)(2,1)}, u32[]{:S(2)}, u32[]{:S(2)}) collective-permute-start(bf16[4,128,896]{2,1,0:T(8,128)(2,1)} %get-tuple-element.60), channel_id=1, source_target_pairs={{0,32},{32,2},{2,34},{34,0},{1,33},{33,3},{3,35},{35,1},{4,36},{36... | collective-permute-start | bytes 2752520 | tf_op jit(solution)/shard_map/ppermute | solution.py:43
  56.9 33.4 %collective-permute-start.14 = (bf16[4,128,896]{2,1,0:T(8,128)(2,1)}, bf16[4,128,896]{2,1,0:T(8,128)(2,1)}, u32[]{:S(2)}, u32[]{:S(2)}) collective-permute-start(bf16[4,128,896]{2,1,0:T(8,128)(2,1)} %get-tuple-element.59), channel_id=1, source_target_pairs={{0,34},{32,0},{2,32},{34,2},{1,35},{33,1},{3,33},{35,3},{4,38},{36... | collective-permute-start | bytes 2752520 | tf_op jit(solution)/shard_map/ppermute | solution.py:43
  59.0 1.8 collective-permute-start
  60.8 12.8 %collective-permute-start.2 = (bf16[256,1024]{1,0:T(8,128)(2,1)}, bf16[256,1024]{1,0:T(8,128)(2,1)S(1)}, u32[]{:S(2)}, u32[]{:S(2)}) collective-permute-start(bf16[256,1024]{1,0:T(8,128)(2,1)} %bitcast.61), channel_id=1, source_target_pairs={{0,4},{4,8},{8,12},{12,16},{16,20},{20,24},{24,28},{28,32},{32,36}... | collective-permute-start | bytes 1572872 | tf_op jit(solution)/shard_map/ppermute | solution.py:33
  62.1 29.1 %copy-start.6 = (bf16[256,1024]{1,0:T(8,128)(2,1)}, bf16[256,1024]{1,0:T(8,128)(2,1)S(1)}, u32[]{:S(2)}) copy-start(bf16[256,1024]{1,0:T(8,128)(2,1)S(1)} %collective-permute-done.4.v1_ref) | copy-start | bytes 1572868
  62.1 26.9 %collective-permute-start.6 = (bf16[256,1024]{1,0:T(8,128)(2,1)S(1)}, bf16[256,1024]{1,0:T(8,128)(2,1)S(1)}, u32[]{:S(2)}, u32[]{:S(2)}) collective-permute-start(bf16[256,1024]{1,0:T(8,128)(2,1)S(1)} %collective-permute-done.4.v1_ref), channel_id=1, source_target_pairs={{28,60},{60,92},{92,124},{124,156},{156,188},{188,220},{220,252},{... | collective-permute-start | bytes 1572872 | tf_op jit(solution)/shard_map/ppermute | solution.py:49
  63.1 28.9 %copy-start.8 = (bf16[256,896]{1,0:T(8,128)(2,1)}, bf16[256,896]{1,0:T(8,128)(2,1)S(1)}, u32[]{:S(2)}) copy-start(bf16[256,896]{1,0:T(8,128)(2,1)S(1)} %get-tuple-element.66.m_oth_ref) | copy-start | bytes 1376260
  63.1 52.3 %copy-start.2 = (bf16[256,896]{1,0:T(8,128)(2,1)}, bf16[256,896]{1,0:T(8,128)(2,1)S(1)}, u32[]{:S(2)}) copy-start(bf16[256,896]{1,0:T(8,128)(2,1)S(1)} %get-tuple-element.67.m_own_ref) | copy-start | bytes 1376260
  73.6 28.2 %copy-start.13 = (bf16[256,1024]{1,0:T(8,128)(2,1)}, bf16[256,1024]{1,0:T(8,128)(2,1)S(1)}, u32[]{:S(2)}) copy-start(bf16[256,1024]{1,0:T(8,128)(2,1)S(1)} %collective-permute-done.2.k1_ref) | copy-start | bytes 1572868
  73.6 18.4 %collective-permute-start.22 = (bf16[256,896]{1,0:T(8,128)(2,1)S(1)}, bf16[256,896]{1,0:T(8,128)(2,1)S(1)}, u32[]{:S(2)}, u32[]{:S(2)}) collective-permute-start(bf16[256,896]{1,0:T(8,128)(2,1)S(1)} %get-tuple-element.66.m_oth_ref), channel_id=1, source_target_pairs={{0,1},{1,0},{2,3},{3,2},{4,5},{5,4},{6,7},{7,6},{8,9},{9,8},{10,11... | collective-permute-start | bytes 1376264 | tf_op jit(solution)/shard_map/ppermute | solution.py:55
  87.8 42.0 %collective-permute-start.15 = (bf16[4,128,896]{2,1,0:T(8,128)(2,1)}, bf16[4,128,896]{2,1,0:T(8,128)(2,1)}, u32[]{:S(2)}, u32[]{:S(2)}) collective-permute-start(bf16[4,128,896]{2,1,0:T(8,128)(2,1)} %collective-permute-done.13.wbl_ref), channel_id=1, source_target_pairs={{0,1},{1,0},{2,3},{3,2},{4,5},{5,4},{6,7},{7,6},{8,9},{9,8},{10,11... | collective-permute-start | bytes 2752520 | tf_op jit(solution)/shard_map/ppermute | solution.py:55
  89.0 12.8 %collective-permute-start.5 = (bf16[256,1024]{1,0:T(8,128)(2,1)S(1)}, bf16[256,1024]{1,0:T(8,128)(2,1)S(1)}, u32[]{:S(2)}, u32[]{:S(2)}) collective-permute-start(bf16[256,1024]{1,0:T(8,128)(2,1)S(1)} %collective-permute-done.2.k1_ref), channel_id=1, source_target_pairs={{0,4},{4,8},{8,12},{12,16},{16,20},{20,24},{24,28},{28,32},{32,36}... | collective-permute-start | bytes 1572872 | tf_op jit(solution)/shard_map/ppermute | solution.py:33
  90.3 41.8 %collective-permute-start.16 = (bf16[4,128,896]{2,1,0:T(8,128)(2,1)}, bf16[4,128,896]{2,1,0:T(8,128)(2,1)}, u32[]{:S(2)}, u32[]{:S(2)}) collective-permute-start(bf16[4,128,896]{2,1,0:T(8,128)(2,1)} %collective-permute-done.14.wbh_ref), channel_id=1, source_target_pairs={{0,1},{1,0},{2,3},{3,2},{4,5},{5,4},{6,7},{7,6},{8,9},{9,8},{10,11... | collective-permute-start | bytes 2752520 | tf_op jit(solution)/shard_map/ppermute | solution.py:55
  92.0 26.7 %collective-permute-start.7 = (bf16[256,1024]{1,0:T(8,128)(2,1)}, bf16[256,1024]{1,0:T(8,128)(2,1)S(1)}, u32[]{:S(2)}, u32[]{:S(2)}) collective-permute-start(bf16[256,1024]{1,0:T(8,128)(2,1)} %broadcast_select_fusion), channel_id=1, source_target_pairs={{0,4},{4,8},{8,12},{12,16},{16,20},{20,24},{24,28},{28,0},{1,5},{5... | collective-permute-start | bytes 1572872 | tf_op jit(solution)/shard_map/ppermute | solution.py:38
  101.8 13.6 %copy-start.3 = (bf16[256,1024]{1,0:T(8,128)(2,1)}, bf16[256,1024]{1,0:T(8,128)(2,1)S(1)}, u32[]{:S(2)}) copy-start(bf16[256,1024]{1,0:T(8,128)(2,1)S(1)} %collective-permute-done.5.k2_ref) | copy-start | bytes 1572868
  101.8 43.8 %collective-permute-start.24 = (bf16[512,896]{1,0:T(8,128)(2,1)}, bf16[512,896]{1,0:T(8,128)(2,1)}, u32[]{:S(2)}, u32[]{:S(2)}) collective-permute-start(bf16[512,896]{1,0:T(8,128)(2,1)} %pad_maximum_fusion.2.m0_ref), channel_id=1, source_target_pairs={{0,192},{64,0},{128,64},{192,128},{1,193},{65,1},{129,65},{193,129... | collective-permute-start | bytes 2752520 | tf_op jit(solution)/shard_map/ppermute | solution.py:38
  118.7 3.2 %copy-start.4 = (bf16[256,1024]{1,0:T(8,128)(2,1)}, bf16[256,1024]{1,0:T(8,128)(2,1)S(1)}, u32[]{:S(2)}) copy-start(bf16[256,1024]{1,0:T(8,128)(2,1)S(1)} %collective-permute-done.7.v2_ref) | copy-start | bytes 1572868
  118.7 9.9 %collective-permute-start.1 = (f32[1]{0:T(128)}, f32[1]{0:T(128)}, u32[]{:S(2)}, u32[]{:S(2)}) collective-permute-start(f32[1]{0:T(128)} %add.53), channel_id=1, source_target_pairs={{0,2},{2,0},{1,3},{3,1},{4,6},{6,4},{5,7},{7,5},{8,10},{10,8},{9,1... | collective-permute-start | bytes 20 | tf_op jit(solution)/shard_map/ppermute | solution.py:55
  128.6 14.0 %collective-permute-start.18 = (bf16[512,256]{1,0:T(8,128)(2,1)}, bf16[512,256]{1,0:T(8,128)(2,1)S(1)}, u32[]{:S(2)}, u32[]{:S(2)}) collective-permute-start(bf16[512,256]{1,0:T(8,128)(2,1)} %get-tuple-element.46), channel_id=1, source_target_pairs={{0,64},{64,128},{128,192},{192,0},{1,65},{65,129},{129,193},{193,1... | collective-permute-start | bytes 786440 | tf_op jit(solution)/shard_map/ppermute | solution.py:38
  128.7 13.9 %collective-permute-start.19 = (bf16[512,256]{1,0:T(8,128)(2,1)}, bf16[512,256]{1,0:T(8,128)(2,1)S(1)}, u32[]{:S(2)}, u32[]{:S(2)}) collective-permute-start(bf16[512,256]{1,0:T(8,128)(2,1)} %get-tuple-element.47), channel_id=1, source_target_pairs={{0,128},{64,192},{128,0},{192,64},{1,129},{65,193},{129,1},{193,65... | collective-permute-start | bytes 786440 | tf_op jit(solution)/shard_map/ppermute | solution.py:38
  129.8 13.3 %collective-permute-start.20 = (bf16[512,256]{1,0:T(8,128)(2,1)}, bf16[512,256]{1,0:T(8,128)(2,1)S(1)}, u32[]{:S(2)}, u32[]{:S(2)}) collective-permute-start(bf16[512,256]{1,0:T(8,128)(2,1)} %get-tuple-element.48), channel_id=1, source_target_pairs={{0,192},{64,0},{128,64},{192,128},{1,193},{65,1},{129,65},{193,129... | collective-permute-start | bytes 786440 | tf_op jit(solution)/shard_map/ppermute | solution.py:38
  132.1 11.1 %copy-start.14 = (bf16[512,256]{1,0:T(8,128)(2,1)S(1)}, bf16[512,256]{1,0:T(8,128)(2,1)}, u32[]{:S(2)}) copy-start(bf16[512,256]{1,0:T(8,128)(2,1)} %get-tuple-element.49) | copy-start | bytes 786436
  143.3 27.1 %copy-start.10 = (bf16[4,512,256]{2,1,0:T(8,128)(2,1)}, bf16[4,512,256]{2,1,0:T(8,128)(2,1)S(1)}, u32[]{:S(2)}) copy-start(bf16[4,512,256]{2,1,0:T(8,128)(2,1)S(1)} %pad_maximum_fusion.1.a_own_ref) | copy-start | bytes 3145732
  143.3 27.1 %collective-permute-start.21 = (bf16[4,512,256]{2,1,0:T(8,128)(2,1)S(1)}, bf16[4,512,256]{2,1,0:T(8,128)(2,1)S(1)}, u32[]{:S(2)}, u32[]{:S(2)}) collective-permute-start(bf16[4,512,256]{2,1,0:T(8,128)(2,1)S(1)} %pad_maximum_fusion.1.a_own_ref), channel_id=1, source_target_pairs={{0,1},{1,0},{2,3},{3,2},{4,5},{5,4},{6,7},{7,6},{8,9},{9,8},{10,11... | collective-permute-start | bytes 3145736 | tf_op jit(solution)/shard_map/ppermute | solution.py:55
  145.3 23.2 %collective-permute-start.23 = (bf16[512,896]{1,0:T(8,128)(2,1)}, bf16[512,896]{1,0:T(8,128)(2,1)S(1)}, u32[]{:S(2)}, u32[]{:S(2)}) collective-permute-start(bf16[512,896]{1,0:T(8,128)(2,1)} %pad_maximum_fusion.2.m0_ref), channel_id=1, source_target_pairs={{0,64},{64,128},{128,192},{192,0},{1,65},{65,129},{129,193},{193,1... | collective-permute-start | bytes 2752520 | tf_op jit(solution)/shard_map/ppermute | solution.py:38
  145.6 23.9 %collective-permute-start.25 = (bf16[512,896]{1,0:T(8,128)(2,1)}, bf16[512,896]{1,0:T(8,128)(2,1)S(1)}, u32[]{:S(2)}, u32[]{:S(2)}) collective-permute-start(bf16[512,896]{1,0:T(8,128)(2,1)} %collective-permute-done.24.m3_ref), channel_id=1, source_target_pairs={{0,192},{64,0},{128,64},{192,128},{1,193},{65,1},{129,65},{193,129... | collective-permute-start | bytes 2752520 | tf_op jit(solution)/shard_map/ppermute | solution.py:38
  148.0 40.4 %collective-permute-start.17 = (bf16[512,1024]{1,0:T(8,128)(2,1)}, bf16[512,1024]{1,0:T(8,128)(2,1)S(1)}, u32[]{:S(2)}, u32[]{:S(2)}) collective-permute-start(bf16[512,1024]{1,0:T(8,128)(2,1)} %get-tuple-element.44), channel_id=1, source_target_pairs={{4,0},{8,4},{12,8},{16,12},{20,16},{24,20},{28,24},{32,28},{36,32}... | collective-permute-start | bytes 3145736 | tf_op jit(solution)/shard_map/ppermute | solution.py:33
  168.5 0.9 copy-start.16
  169.4 0.9 copy-start.17
  170.4 1.1 copy-start.15
  178.6 9.8 %collective-permute-start.29 = (bf16[128,896]{1,0:T(8,128)(2,1)S(1)}, bf16[128,896]{1,0:T(8,128)(2,1)S(1)}, u32[]{:S(2)}, u32[]{:S(2)}) collective-permute-start(bf16[128,896]{1,0:T(8,128)(2,1)S(1)} %get-tuple-element.64), channel_id=1, source_target_pairs={{0,34},{32,0},{2,32},{34,2},{1,35},{33,1},{3,33},{35,3},{4,38},{36... | collective-permute-start | bytes 688136 | tf_op jit(solution)/shard_map/ppermute | solution.py:43
  178.8 9.6 %collective-permute-start.28 = (bf16[128,896]{1,0:T(8,128)(2,1)S(1)}, bf16[128,896]{1,0:T(8,128)(2,1)S(1)}, u32[]{:S(2)}, u32[]{:S(2)}) collective-permute-start(bf16[128,896]{1,0:T(8,128)(2,1)S(1)} %get-tuple-element.65), channel_id=1, source_target_pairs={{0,2},{32,34},{2,0},{34,32},{1,3},{33,35},{3,1},{35,33},{4,6},{36,... | collective-permute-start | bytes 688136 | tf_op jit(solution)/shard_map/ppermute | solution.py:43
  180.0 12.7 %collective-permute-start.27 = (bf16[128,896]{1,0:T(8,128)(2,1)S(1)}, bf16[128,896]{1,0:T(8,128)(2,1)S(1)}, u32[]{:S(2)}, u32[]{:S(2)}) collective-permute-start(bf16[128,896]{1,0:T(8,128)(2,1)S(1)} %get-tuple-element.63), channel_id=1, source_target_pairs={{0,32},{32,2},{2,34},{34,0},{1,33},{33,3},{3,35},{35,1},{4,36},{36... | collective-permute-start | bytes 688136 | tf_op jit(solution)/shard_map/ppermute | solution.py:43
  194.5 30.2 %all-to-all-start.1 = ((bf16[8,16,896]{2,1,0:T(8,128)(2,1)}), bf16[8,16,896]{2,1,0:T(8,128)(2,1)S(1)}, u32[]{:S(2)}, u32[]{:S(2)}) async-start(bf16[8,16,896]{2,1,0:T(8,128)(2,1)} %bitcast.26), calls=%async_computation.1 | async-start | bytes 458752 | tf_op jit(solution)/shard_map/all_to_all | solution.py:390
  214.6 30.3 %copy-start.7 = (f32[512,1024]{1,0:T(8,128)S(1)}, f32[512,1024]{1,0:T(8,128)}, u32[]{:S(2)}) copy-start(f32[512,1024]{1,0:T(8,128)} %get-tuple-element.42) | copy-start | bytes 6291460
  217.4 26.6 %collective-permute-start.26 = (bf16[512,1024]{1,0:T(8,128)(2,1)}, bf16[512,1024]{1,0:T(8,128)(2,1)S(1)}, u32[]{:S(2)}, u32[]{:S(2)}) collective-permute-start(bf16[512,1024]{1,0:T(8,128)(2,1)} %add_convert_fusion), channel_id=1, source_target_pairs={{4,0},{8,4},{12,8},{16,12},{20,16},{24,20},{28,24},{32,28},{36,32}... | collective-permute-start | bytes 3145736 | tf_op jit(solution)/shard_map/ppermute | solution.py:33
  225.3 3.4 %collective-permute-start.30 = (f32[16,896]{1,0:T(8,128)S(1)}, f32[16,896]{1,0:T(8,128)S(1)}, u32[]{:S(2)}, u32[]{:S(2)}) collective-permute-start(f32[16,896]{1,0:T(8,128)S(1)} %get-tuple-element.56), channel_id=1, source_target_pairs={{0,1},{1,0},{2,3},{3,2},{4,5},{5,4},{6,7},{7,6},{8,9},{9,8},{10,11... | collective-permute-start | bytes 172040 | tf_op jit(solution)/shard_map/ppermute | solution.py:55
  228.8 25.8 %collective-permute-start.31 = (f32[16,1792]{1,0:T(8,128)S(1)}, f32[16,1792]{1,0:T(8,128)S(1)}, u32[]{:S(2)}, u32[]{:S(2)}) collective-permute-start(f32[16,1792]{1,0:T(8,128)S(1)} %maximum_select_fusion.1), channel_id=1, source_target_pairs={{0,2},{2,0},{1,3},{3,1},{4,6},{6,4},{5,7},{7,5},{8,10},{10,8},{9,1... | collective-permute-start | bytes 344072 | tf_op jit(solution)/shard_map/ppermute | solution.py:55
  244.0 1.0 copy-start.9
  249.9 9.3 %all-to-all-start.2 = ((f32[8,8,128]{2,1,0:T(8,128)}), f32[8,8,128]{2,1,0:T(8,128)S(1)}, u32[]{:S(2)}, u32[]{:S(2)}) async-start(f32[8,8,128]{2,1,0:T(8,128)} %broadcast_in_dim_broadcast_in_dim_broadcast_in_dim.6), calls=%async_computation.2 | async-start | bytes 65536 | tf_op jit(solution)/shard_map/all_to_all | solution.py:60
  260.0 18.1 %all-to-all-start.3 = ((f32[32,8,128]{2,1,0:T(8,128)}), f32[32,8,128]{2,1,0:T(8,128)S(1)}, u32[]{:S(2)}, u32[]{:S(2)}) async-start(f32[32,8,128]{2,1,0:T(8,128)} %broadcast_in_dim_broadcast_in_dim_broadcast_in_dim.7), calls=%async_computation.3 | async-start | bytes 262144 | tf_op jit(solution)/shard_map/all_to_all | solution.py:60

commit v6 on v5

--- a/solution.py
+++ b/solution.py
@@ -165,24 +165,31 @@
     d2_ref[TOK_DEV:] = (dot(p_ref[0], g, NT) * act_scale).astype(BF16)
 
 
-def near_grad_kernel(
-    scale_ref, q_ref, k0_ref, v0_ref, k1_ref, v1_ref, k2_ref, p_ref, pf_ref, g_ref, delta_ref, ds_ref,
-    dq_ref, d0_ref, d1_ref, sq_ref,
+def mid_grad_kernel(
+    scale_ref, q_ref, v1_ref, p_ref, pf_ref, g_ref, delta_ref, d1_ref, ds_ref,
 ):
     act_scale = scale_ref[0]
-    q = two_heads(q_ref)
     g = g_ref[0]
-    delta = delta_ref[0, :1]
-    dq = dot(k2_ref[...], ds_ref[0], TN)
-    for k, v, at, out in (
-        (k1_ref[...], v1_ref[...], 0, d1_ref),
-        (k0_ref[...], v0_ref[...], TOK_DEV, d0_ref),
-    ):
-        dscore = score_terms(v, g, delta, pf_ref[0, at : at + TOK_DEV])
-        dq = dq + dot(k, dscore, TN)
-        out[:TOK_DEV] = (dot(dscore, q, NN) * (SCALE * act_scale)).astype(out.dtype)
-        out[TOK_DEV:] = (dot(p_ref[0, at : at + TOK_DEV], g, NT) * act_scale).astype(out.dtype)
-    dq = dq * (SCALE * act_scale)
+    dscore = score_terms(v1_ref[...], g, delta_ref[0, :1], pf_ref[0])
+    d1_ref[:TOK_DEV] = (dot(dscore, two_heads(q_ref), NN) * (SCALE * act_scale)).astype(BF16)
+    d1_ref[TOK_DEV:] = (dot(p_ref[0], g, NT) * act_scale).astype(BF16)
+    ds_ref[0] = dscore
+
+
+def near_grad_kernel(
+    scale_ref, q_ref, k0_ref, v0_ref, k1_ref, k2_ref, p_ref, pf_ref, g_ref, delta_ref, ds1_ref,
+    ds2_ref, dq_ref, d0_ref, sq_ref,
+):
+    act_scale = scale_ref[0]
+    g = g_ref[0]
+    dscore = score_terms(v0_ref[...], g, delta_ref[0, :1], pf_ref[0])
+    d0_ref[:TOK_DEV] = dot(dscore, two_heads(q_ref), NN) * (SCALE * act_scale)
+    d0_ref[TOK_DEV:] = dot(p_ref[0], g, NT) * act_scale
+    dq = (
+        dot(k2_ref[...], ds2_ref[0], TN)
+        + dot(k1_ref[...], ds1_ref[0], TN)
+        + dot(k0_ref[...], dscore, TN)
+    ) * (SCALE * act_scale)
     sq_ref[...] = jnp.broadcast_to(jnp.sum(dq * dq), sq_ref.shape)
     for h in range(GROUP):
         dq_ref[:, h * HEAD_DIM : (h + 1) * HEAD_DIM] = dq[
@@ -190,7 +197,7 @@
         ].T.astype(BF16)
 
 
-def weight_kernel(at_ref, a_own_ref, a_oth_ref, m0_ref, m1_ref, m2_ref, m3_ref, out_ref):
+def weight_kernel(at_ref, a_own_ref, a_oth_ref, m0_ref, m1_ref, m2_ref, m3_ref, *out_refs):
     acc = None
     for back, m_ref in enumerate((m0_ref, m1_ref, m2_ref, m3_ref)):
         both = dot(a_own_ref[back], m_ref[:TOK_DEV], NN) + dot(
@@ -201,7 +208,12 @@
     for low in range(2):
         for high in range(2):
             away = (2 * high + low + 4 - at_ref[3]) % 4
-            out_ref[away] = acc[low, :, high].reshape(128, HALF).astype(BF16)
+            rows = acc[low, :, high].reshape(128, HALF).astype(BF16)
+            for place, out_ref in enumerate(out_refs):
+
+                @pl.when(away == place)
+                def _(out_ref=out_ref, rows=rows):
+                    out_ref[...] = rows
 
 
 D = HEAD_DIM
@@ -278,16 +290,31 @@
     )(where, scale, q, v2, p, pf, inv, attn, m_own, m_oth, *weights)
 
 
-def near_backward(scale, q, k, v, k1, v1, k2, p, pf, g, delta, dscore):
+def part_of_head(which):
+    return pl.BlockSpec((1, TOK_DEV, SCORES), lambda h, *_: (h, which, 0))
+
+
+def mid_backward(scale, q, v1, p, pf, g, delta):
+    return call(
+        mid_grad_kernel, 1,
+        [HEAD_COLS, KV_COLS, part_of_head(0), part_of_head(0), of_head(D), of_head(8)],
+        [BOTH_COLS, of_head(TOK_DEV)],
+        [flat(2 * TOK_DEV, BF16), per_head(TOK_DEV, BF16)],
+        3, 7,
+    )(scale, q, v1, p, pf, g, delta)
+
+
+def near_backward(scale, q, k, v, k1, k2, p, pf, g, delta, ds1, ds2):
     return call(
         near_grad_kernel, 1,
-        [HEAD_COLS] + [KV_COLS] * 5
-        + [of_head(2 * TOK_DEV), of_head(2 * TOK_DEV), of_head(D), of_head(8), of_head(TOK_DEV)],
-        [HEAD_COLS, BOTH_COLS, BOTH_COLS, pl.BlockSpec((8, 128), lambda h, *_: (h, 0))],
+        [HEAD_COLS] + [KV_COLS] * 4
+        + [part_of_head(1), part_of_head(1), of_head(D), of_head(8), of_head(TOK_DEV),
+           of_head(TOK_DEV)],
+        [HEAD_COLS, BOTH_COLS, pl.BlockSpec((8, 128), lambda h, *_: (h, 0))],
         [jax.ShapeDtypeStruct((TOK_DEV, WIDTH), BF16), flat(2 * TOK_DEV, F32),
-         flat(2 * TOK_DEV, BF16), jax.ShapeDtypeStruct((8 * KV_HEADS, 128), F32)],
-        9, 13,
-    )(scale, q, k, v, k1, v1, k2, p, pf, g, delta, dscore)
+         jax.ShapeDtypeStruct((8 * KV_HEADS, 128), F32)],
+        5, 10,
+    )(scale, q, k, v, k1, k2, p, pf, g, delta, ds1, ds2)
 
 
 def weight_product(where, a_own, a_oth, m0, m1, m2, m3):
@@ -295,8 +322,8 @@
     return pl.pallas_call(
         weight_kernel,
         in_specs=[pl.BlockSpec(memory_space=pltpu.SMEM)] + [vmem] * 6,
-        out_specs=vmem,
-        out_shape=jax.ShapeDtypeStruct((4, 128, HALF), BF16),
+        out_specs=[vmem] * 4,
+        out_shape=[jax.ShapeDtypeStruct((128, HALF), BF16)] * 4,
         cost_estimate=pl.CostEstimate(
             flops=2 * 512 * HALF * 2048, transcendentals=0, bytes_accessed=7 << 20
         ),
@@ -368,8 +395,9 @@
     a_oth = swap(a_own, "dp_1")
 
     r1 = shifted(d2, -1)
-    dq, d0, d1, dq_sq = near_backward(
-        act_scale, q_rows, k_rows, v_rows, h1k, h1v, h2k, p, pf, g, delta, dscore
+    d1, dscore1 = mid_backward(act_scale, q_rows, h1v, p, pf, g, delta)
+    dq, d0, dq_sq = near_backward(
+        act_scale, q_rows, k_rows, v_rows, h1k, h2k, p, pf, g, delta, dscore1, dscore
     )
     part = weight_product(
         where, a_own, a_oth, m0, m1, m2, m3
@@ -389,7 +417,8 @@
     ).astype(BF16)
     pieces = lax.all_to_all(part, "seq_2", 0, 0, tiled=True)
     piece = jnp.sum(pieces.reshape(8, 16, HALF).astype(F32), axis=0) * weight_scale
-    square = square + jnp.sum(piece * piece)
+    piece_square = jnp.sum(piece * piece)
+    square = square + piece_square
 
     other = swap(piece, "dp_1")
     row = jnp.where(

time: 281 us -> 277 us (0.986)
  other arithmetic: 14.6 us -> 10.9 us
  Pallas kernels: 38.1 us -> 41.8 us
    all_to_all x1, waiting for transfers between devices: 5.92 us -> 1.42 us  [all_steps(): pieces = lax.all_to_all(part, 'seq_2', 0, 0, tiled=True)]
    ppermute x5, waiting for transfers between devices: 17.6 us -> 21.2 us  [ring_x(): lax.ppermute(value, X_AXES, [(at(s), at((s + steps) % 4)) for s in range(...]
    pallas_call x1 -> x2, Pallas kernels: 8.26 us -> 11.7 us  [the longest x1 6.83 us: near_backward(): call(near_grad_kernel, 1, [HEAD_COLS] + [KV_COLS] * 4 + [part_of_head(1),...]
  transfers between devices with their start and end apart: 36 -> 36, of which waited for: 15 -> 16; matrix products, arithmetic and copies ran while one was open for 6% -> 5% of each run, Pallas kernels for 14% -> 15%
where the time goes in v6:
time: 277 us; the launch traced here: 276 us
  waiting for transfers between devices  122 us (44%)
  starting transfers between devices  86 us (31%)
  Pallas kernels  41.8 us (15%)
  other arithmetic  10.9 us (4%)
  local copies, waits for them, and re-layouts  8.55 us (3%)
  between operations  6.32 us (2%)
    ppermute x12, waiting for transfers between devices, ring(): lax.ppermute(value, axis, [(s, (s + steps) % count) for s in range(count)])  38 us
    ppermute x4, waiting for transfers between devices, shifted(): lax.ppermute(value, SEQ, [(source, source + steps) for source in range(in...  33.8 us
    all_to_all x3, waiting for transfers between devices, for_each(): lax.all_to_all(jnp.broadcast_to(value[None], (size, *value.shape)), axis,...  27.9 us
    all_to_all x3, starting transfers between devices, for_each(): lax.all_to_all(jnp.broadcast_to(value[None], (size, *value.shape)), axis,...  21.7 us
    ppermute x5, waiting for transfers between devices, ring_x(): lax.ppermute(value, X_AXES, [(at(s), at((s + steps) % 4)) for s in range(...  21.2 us
    all_to_all x1, starting transfers between devices, all_steps(): pieces = lax.all_to_all(part, 'seq_2', 0, 0, tiled=True)  20 us
    ppermute x12, starting transfers between devices, ring(): lax.ppermute(value, axis, [(s, (s + steps) % count) for s in range(count)])  17.4 us
    ppermute x9, starting transfers between devices, swap(): return lax.ppermute(value, axis, [(0, 1), (1, 0)])  15.3 us
  transfers between devices with their start and end apart: 36, of which 16 were waited for; matrix products, arithmetic and copies ran while one was open for 5% of the time, Pallas kernels for 15%

profile of v6, /device:TPU:1, one launch (start us, length us, event | category | flops | bytes accessed | tf_op | source)
XLA Modules:
  0.0 275.9 jit_solution(11470808845397341341)
XLA Ops:
  0.7 0.9 copy-done
  1.5 0.8 broadcast_in_dim.30
  2.3 9.0 %all-to-all-start = ((bf16[8,32,896]{2,1,0:T(8,128)(2,1)}), bf16[8,32,896]{2,1,0:T(8,128)(2,1)S(1)}, u32[]{:S(2)}, u32[]{:S(2)}) async-start(bf16[8,32,896]{2,1,0:T(8,128)(2,1)} %broadcast_in_dim.30), calls=%async_computation | async-start | bytes 917504 | tf_op jit(solution)/shard_map/all_to_all | solution.py:60
  11.3 0.7 collective-permute-start.4
  12.0 15.8 %all-to-all-done = bf16[8,32,896]{2,1,0:T(8,128)(2,1)S(1)} async-done(((bf16[8,32,896]{2,1,0:T(8,128)(2,1)}), bf16[8,32,896]{2,1,0:T(8,128)(2,1)S(1)}, u32[]{:S(2)}, u32[]{:S(2)}) %all-to-all-start) | async-done | bytes 458784 | tf_op jit(solution)/shard_map/all_to_all | solution.py:60
  27.8 2.7 collective-permute-start.10
  30.6 9.3 %collective-permute-done.10 = bf16[256,896]{1,0:T(8,128)(2,1)S(1)} collective-permute-done((bf16[256,896]{1,0:T(8,128)(2,1)S(1)}, bf16[256,896]{1,0:T(8,128)(2,1)S(1)}, u32[]{:S(2)}, u32[]{:S(2)}) %collective-permute-start.10) | collective-permute-done | bytes 458784 | tf_op jit(solution)/shard_map/ppermute | solution.py:38
  39.9 3.5 %collective-permute-start.11 = (bf16[128,896]{1,0:T(8,128)(2,1)S(1)}, bf16[128,896]{1,0:T(8,128)(2,1)S(1)}, u32[]{:S(2)}, u32[]{:S(2)}) collective-permute-start(bf16[128,896]{1,0:T(8,128)(2,1)S(1)} %slice.45), channel_id=1, source_target_pairs={{0,192},{64,0},{128,64},{192,128},{1,193},{65,1},{129,65},{193,129... | collective-permute-start | bytes 688136 | tf_op jit(solution)/shard_map/ppermute | solution.py:38
  43.5 0.9 broadcast_select_fusion.1
  44.4 2.5 collective-permute-done.11
  46.9 3.2 %collective-permute-done.9 = bf16[128,896]{1,0:T(8,128)(2,1)S(1)} collective-permute-done((bf16[128,896]{1,0:T(8,128)(2,1)S(1)}, bf16[128,896]{1,0:T(8,128)(2,1)S(1)}, u32[]{:S(2)}, u32[]{:S(2)}) %collective-permute-start.9) | collective-permute-done | bytes 229408 | tf_op jit(solution)/shard_map/ppermute | solution.py:38
  50.2 1.3 pad_maximum_fusion.wa_ref
  51.5 2.7 collective-permute-start.12
  54.2 1.4 fusion.1
  55.6 1.2 collective-permute-start.13
  56.8 1.5 collective-permute-start.14
  58.9 1.8 collective-permute-start
  60.8 1.3 collective-permute-start.2
  62.1 0.7 collective-permute-start.6
  63.1 10.5 %collective-permute-done.2.k1_ref = bf16[256,1024]{1,0:T(8,128)(2,1)S(1)} collective-permute-done((bf16[256,1024]{1,0:T(8,128)(2,1)}, bf16[256,1024]{1,0:T(8,128)(2,1)S(1)}, u32[]{:S(2)}, u32[]{:S(2)}) %collective-permute-start.2) | collective-permute-done | bytes 524320 | tf_op jit(solution)/shard_map/ppermute | solution.py:33
  73.6 0.9 collective-permute-start.22
  74.5 13.2 %collective-permute-done.13.wbl_ref = bf16[4,128,896]{2,1,0:T(8,128)(2,1)} collective-permute-done((bf16[4,128,896]{2,1,0:T(8,128)(2,1)}, bf16[4,128,896]{2,1,0:T(8,128)(2,1)}, u32[]{:S(2)}, u32[]{:S(2)}) %collective-permute-start.13) | collective-permute-done | bytes 917536 | tf_op jit(solution)/shard_map/ppermute | solution.py:43
  87.7 1.2 collective-permute-start.15
  88.9 2.1 collective-permute-start.3
  91.3 1.0 pad_maximum_fusion.2.m0_ref
  92.3 9.4 %collective-permute-done.3.k2_ref = bf16[256,1024]{1,0:T(8,128)(2,1)} collective-permute-done((bf16[256,1024]{1,0:T(8,128)(2,1)S(1)}, bf16[256,1024]{1,0:T(8,128)(2,1)}, u32[]{:S(2)}, u32[]{:S(2)}) %collective-permute-start.3) | collective-permute-done | bytes 524320 | tf_op jit(solution)/shard_map/ppermute | solution.py:33
  101.7 5.5 %collective-permute-start.24 = (bf16[512,896]{1,0:T(8,128)(2,1)}, bf16[512,896]{1,0:T(8,128)(2,1)}, u32[]{:S(2)}, u32[]{:S(2)}) collective-permute-start(bf16[512,896]{1,0:T(8,128)(2,1)} %pad_maximum_fusion.2.m0_ref), channel_id=1, source_target_pairs={{0,192},{64,0},{128,64},{192,128},{1,193},{65,1},{129,65},{193,129... | collective-permute-start | bytes 2752520 | tf_op jit(solution)/shard_map/ppermute | solution.py:38
  107.3 0.7 pad_add_fusion.at_ref
  108.6 6.8 %shard_map.101 = (bf16[4,512,512]{2,1,0:T(8,128)(2,1)}, bf16[4,512,512]{2,1,0:T(8,128)(2,1)}, f32[4,256,512]{2,1,0:T(8,128)}, f32[4,8,512]{2,1,0:T(8,128)}) custom-call(s32[4]{0:T(128)} %pad_add_fusion.at_ref, bf16[256,2048]{1,0:T(8,128)(2,1)} %bitcast.38, bf16[256,1024]{1,0:T(8,128)(2,1)} %bitcast.52, bf16[256,1024]{1,0:T(8,128)(2,1)} %bitcast.44, ...), custom_call_target="tpu_custom_call" | custom-call | flops 1073741824 | bytes 9437184 | tf_op jit(solution)/shard_map/pallas_call | solution.py:257
  115.5 3.2 %collective-permute-done.7.v2_ref = bf16[256,1024]{1,0:T(8,128)(2,1)S(1)} collective-permute-done((bf16[256,1024]{1,0:T(8,128)(2,1)S(1)}, bf16[256,1024]{1,0:T(8,128)(2,1)S(1)}, u32[]{:S(2)}, u32[]{:S(2)}) %collective-permute-start.7) | collective-permute-done | bytes 524320 | tf_op jit(solution)/shard_map/ppermute | solution.py:38
  118.6 3.2 %collective-permute-start.1 = (f32[1]{0:T(128)}, f32[1]{0:T(128)}, u32[]{:S(2)}, u32[]{:S(2)}) collective-permute-start(f32[1]{0:T(128)} %add.53), channel_id=1, source_target_pairs={{0,2},{2,0},{1,3},{3,1},{4,6},{6,4},{5,7},{7,5},{8,10},{10,8},{9,1... | collective-permute-start | bytes 20 | tf_op jit(solution)/shard_map/ppermute | solution.py:55
  121.8 6.7 %shard_map.102 = (bf16[4,256,512]{2,1,0:T(8,128)(2,1)}, bf16[4,256,512]{2,1,0:T(8,128)(2,1)}, bf16[4,512,256]{2,1,0:T(8,128)(2,1)}, f32[4,8,512]{2,1,0:T(8,128)}...) custom-call(s32[4]{0:T(128)} %pad_add_fusion.at_ref, ...), custom_call_target="tpu_custom_call" | custom-call | flops 536870912 | bytes 7340032 | tf_op jit(solution)/shard_map/pallas_call | solution.py:268
  128.6 1.2 collective-permute-start.19
  129.8 1.6 collective-permute-start.20
  132.1 10.5 %shard_map.103 = (bf16[512,1024]{1,0:T(8,128)(2,1)}, bf16[4,256,512]{2,1,0:T(8,128)(2,1)}, f32[4,8,512]{2,1,0:T(8,128)}, bf16[4,256,512]{2,1,0:T(8,128)(2,1)}) custom-call(s32[4]{0:T(128)} %pad_add_fusion.at_ref, f32[1]{0:T(128)S(6)} %div.6.scale_ref, bf16[256,2048]{1,0:T(8,128)(2,1)} %bitcast.40, bf16[256,1024]{1,0:T(8,128)(2,1)} %copy-done.3, ...), custom_call_target="tpu_custom_call" | custom-call | flops 2684354560 | bytes 15728640 | tf_op jit(solution)/shard_map/pallas_call | solution.py:283
  143.3 2.0 collective-permute-start.21
  145.7 2.2 collective-permute-start.25
  147.9 1.3 collective-permute-start.17
  149.2 19.3 %collective-permute-done.23.m1_ref = bf16[512,896]{1,0:T(8,128)(2,1)S(1)} collective-permute-done((bf16[512,896]{1,0:T(8,128)(2,1)}, bf16[512,896]{1,0:T(8,128)(2,1)S(1)}, u32[]{:S(2)}, u32[]{:S(2)}) %collective-permute-start.23) | collective-permute-done | bytes 917536 | tf_op jit(solution)/shard_map/ppermute | solution.py:38
  168.5 0.9 copy-done.15
  169.4 0.9 copy-done.16
  170.4 1.0 copy-done.14
  171.3 6.1 %weight_product.1 = (bf16[128,896]{1,0:T(8,128)(2,1)}, bf16[128,896]{1,0:T(8,128)(2,1)}, bf16[128,896]{1,0:T(8,128)(2,1)}, bf16[128,896]{1,0:T(8,128)(2,1)}) custom-call(s32[4]{0:T(128)} %pad_add_fusion.at_ref, bf16[4,512,256]{2,1,0:T(8,128)(2,1)} %copy-done.8, bf16[4,512,256]{2,1,0:T(8,128)(2,1)} %copy-done.14, bf16[512,896]{1,0:T(8,128)(2,1)} %pad_maximum_fusion.2.m0_ref, ...), custom_call_target="tpu_custom_call" | custom-call | flops 1879048192 | bytes 7340032 | tf_op jit(solution)/shard_map/weight_product/pallas_call | solution.py:322
  177.8 1.2 collective-permute-start.28
  179.0 4.9 %shard_map.104 = (bf16[512,1024]{1,0:T(8,128)(2,1)}, bf16[4,256,512]{2,1,0:T(8,128)(2,1)}) custom-call(f32[1]{0:T(128)S(6)} %div.6.scale_ref, bf16[256,2048]{1,0:T(8,128)(2,1)} %bitcast.41, bf16[256,1024]{1,0:T(8,128)(2,1)} %copy-done.4, bf16[4,512,512]{2,1,0:T(8,128)(2,1)} %get-tuple-element.35.p_ref, bf16[4,512,512]{2,1,0:T(8,128)(2,1)} %get-tuple-element.36.pf_ref, ...), custom_call_target="tpu_custom_call" | custom-call | flops 805306368 | bytes 7340032 | tf_op jit(solution)/shard_map/pallas_call | solution.py:298
  183.9 1.5 collective-permute-done.28
  185.5 6.5 %collective-permute-done.27 = bf16[128,896]{1,0:T(8,128)(2,1)S(1)} collective-permute-done((bf16[128,896]{1,0:T(8,128)(2,1)}, bf16[128,896]{1,0:T(8,128)(2,1)S(1)}, u32[]{:S(2)}, u32[]{:S(2)}) %collective-permute-start.27) | collective-permute-done | bytes 229408 | tf_op jit(solution)/shard_map/ppermute | solution.py:43
  191.9 0.8 add_convert_fusion.1
  192.7 20.0 %all-to-all-start.1 = ((bf16[8,16,896]{2,1,0:T(8,128)(2,1)}), bf16[8,16,896]{2,1,0:T(8,128)(2,1)S(1)}, u32[]{:S(2)}, u32[]{:S(2)}) async-start(bf16[8,16,896]{2,1,0:T(8,128)(2,1)} %bitcast.22), calls=%async_computation.1 | async-start | bytes 458752 | tf_op jit(solution)/shard_map/all_to_all | solution.py:418
  213.1 1.3 collective-permute-start.26
  214.5 6.8 %shard_map.105 = (bf16[256,2048]{1,0:T(8,128)(2,1)}, f32[512,1024]{1,0:T(8,128)}, f32[32,128]{1,0:T(8,128)}) custom-call(f32[1]{0:T(128)S(6)} %div.6.scale_ref, bf16[256,2048]{1,0:T(8,128)(2,1)} %bitcast.42, bf16[256,1024]{1,0:T(8,128)(2,1)} %bitcast.53, bf16[256,1024]{1,0:T(8,128)(2,1)} %bitcast.45, bf16[256,1024]{1,0:T(8,128)(2,1)} %copy-done.11, ...), custom_call_target="tpu_custom_call" | custom-call | flops 1342177280 | bytes 10485760 | tf_op jit(solution)/shard_map/pallas_call | solution.py:308
  221.3 1.4 all-to-all-done.1
  223.4 2.1 collective-permute-start.30
  225.5 1.3 slice_reduce_fusion
  226.8 1.3 collective-permute-start.31
  228.1 13.9 %collective-permute-done.26 = bf16[512,1024]{1,0:T(8,128)(2,1)S(1)} collective-permute-done((bf16[512,1024]{1,0:T(8,128)(2,1)S(1)}, bf16[512,1024]{1,0:T(8,128)(2,1)S(1)}, u32[]{:S(2)}, u32[]{:S(2)}) %collective-permute-start.26) | collective-permute-done | bytes 1048608 | tf_op jit(solution)/shard_map/ppermute | solution.py:33
  242.0 2.8 multiply_reduce_fusion
  247.3 4.6 %all-to-all-start.2 = ((f32[8,8,128]{2,1,0:T(8,128)}), f32[8,8,128]{2,1,0:T(8,128)S(1)}, u32[]{:S(2)}, u32[]{:S(2)}) async-start(f32[8,8,128]{2,1,0:T(8,128)} %broadcast_in_dim_broadcast_in_dim_broadcast_in_dim.6), calls=%async_computation.2 | async-start | bytes 65536 | tf_op jit(solution)/shard_map/all_to_all | solution.py:60
  251.9 0.7 maximum_select_fusion
  252.7 4.0 %all-to-all-done.2 = f32[8,8,128]{2,1,0:T(8,128)S(1)} async-done(((f32[8,8,128]{2,1,0:T(8,128)}), f32[8,8,128]{2,1,0:T(8,128)S(1)}, u32[]{:S(2)}, u32[]{:S(2)}) %all-to-all-start.2) | async-done | bytes 32800 | tf_op jit(solution)/shard_map/all_to_all | solution.py:60
  256.7 0.7 broadcast_in_dim_broadcast_in_dim_broadcast_in_dim.7
  257.4 8.1 %all-to-all-start.3 = ((f32[32,8,128]{2,1,0:T(8,128)}), f32[32,8,128]{2,1,0:T(8,128)S(1)}, u32[]{:S(2)}, u32[]{:S(2)}) async-start(f32[32,8,128]{2,1,0:T(8,128)} %broadcast_in_dim_broadcast_in_dim_broadcast_in_dim.7), calls=%async_computation.3 | async-start | bytes 262144 | tf_op jit(solution)/shard_map/all_to_all | solution.py:60
  265.5 1.0 slice_bitcast_fusion
  266.5 8.1 %all-to-all-done.3 = f32[32,8,128]{2,1,0:T(8,128)S(1)} async-done(((f32[32,8,128]{2,1,0:T(8,128)}), f32[32,8,128]{2,1,0:T(8,128)S(1)}, u32[]{:S(2)}, u32[]{:S(2)}) %all-to-all-start.3) | async-done | bytes 131104 | tf_op jit(solution)/shard_map/all_to_all | solution.py:60
  (78 shorter events, 4.1 us)
Async XLA Ops:
  0.6 0.9 copy-start
  0.6 42.8 %copy-start.5 = (bf16[1,256,1024]{2,1,0:T(8,128)(2,1)S(1)}, bf16[1,256,1024]{2,1,0:T(8,128)(2,1)}, u32[]{:S(2)}) copy-start(bf16[1,256,1024]{2,1,0:T(8,128)(2,1)} %param.8) | copy-start | bytes 1572868
  2.3 25.5 %all-to-all-start = ((bf16[8,32,896]{2,1,0:T(8,128)(2,1)}), bf16[8,32,896]{2,1,0:T(8,128)(2,1)S(1)}, u32[]{:S(2)}, u32[]{:S(2)}) async-start(bf16[8,32,896]{2,1,0:T(8,128)(2,1)} %broadcast_in_dim.30), calls=%async_computation | async-start | bytes 917504 | tf_op jit(solution)/shard_map/all_to_all | solution.py:60
  11.3 32.1 %collective-permute-start.4 = (bf16[256,1024]{1,0:T(8,128)(2,1)}, bf16[256,1024]{1,0:T(8,128)(2,1)S(1)}, u32[]{:S(2)}, u32[]{:S(2)}) collective-permute-start(bf16[256,1024]{1,0:T(8,128)(2,1)} %bitcast.43), channel_id=1, source_target_pairs={{28,60},{60,92},{92,124},{124,156},{156,188},{188,220},{220,252},{... | collective-permute-start | bytes 1572872 | tf_op jit(solution)/shard_map/ppermute | solution.py:49
  27.8 12.0 %collective-permute-start.10 = (bf16[256,896]{1,0:T(8,128)(2,1)S(1)}, bf16[256,896]{1,0:T(8,128)(2,1)S(1)}, u32[]{:S(2)}, u32[]{:S(2)}) collective-permute-start(bf16[256,896]{1,0:T(8,128)(2,1)S(1)} %bitcast.46), channel_id=1, source_target_pairs={{0,192},{64,0},{128,64},{192,128},{1,193},{65,1},{129,65},{193,129... | collective-permute-start | bytes 1376264 | tf_op jit(solution)/shard_map/ppermute | solution.py:38
  30.5 12.8 %collective-permute-start.8 = (bf16[256,896]{1,0:T(8,128)(2,1)S(1)}, bf16[256,896]{1,0:T(8,128)(2,1)S(1)}, u32[]{:S(2)}, u32[]{:S(2)}) collective-permute-start(bf16[256,896]{1,0:T(8,128)(2,1)S(1)} %bitcast.47), channel_id=1, source_target_pairs={{0,64},{64,128},{128,192},{192,0},{1,65},{65,129},{129,193},{193,1... | collective-permute-start | bytes 1376264 | tf_op jit(solution)/shard_map/ppermute | solution.py:38
  39.9 7.0 %collective-permute-start.11 = (bf16[128,896]{1,0:T(8,128)(2,1)S(1)}, bf16[128,896]{1,0:T(8,128)(2,1)S(1)}, u32[]{:S(2)}, u32[]{:S(2)}) collective-permute-start(bf16[128,896]{1,0:T(8,128)(2,1)S(1)} %slice.45), channel_id=1, source_target_pairs={{0,192},{64,0},{128,64},{192,128},{1,193},{65,1},{129,65},{193,129... | collective-permute-start | bytes 688136 | tf_op jit(solution)/shard_map/ppermute | solution.py:38
  43.4 6.8 %copy-start.9 = (bf16[256,896]{1,0:T(8,128)(2,1)}, bf16[256,896]{1,0:T(8,128)(2,1)S(1)}, u32[]{:S(2)}) copy-start(bf16[256,896]{1,0:T(8,128)(2,1)S(1)} %collective-permute-done.8) | copy-start | bytes 1376260
  43.4 6.7 %collective-permute-start.9 = (bf16[128,896]{1,0:T(8,128)(2,1)S(1)}, bf16[128,896]{1,0:T(8,128)(2,1)S(1)}, u32[]{:S(2)}, u32[]{:S(2)}) collective-permute-start(bf16[128,896]{1,0:T(8,128)(2,1)S(1)} %slice.44), channel_id=1, source_target_pairs={{0,64},{64,128},{128,192},{192,0},{1,65},{65,129},{129,193},{193,1... | collective-permute-start | bytes 688136 | tf_op jit(solution)/shard_map/ppermute | solution.py:38
  44.3 17.7 %collective-permute-start.5 = (bf16[256,1024]{1,0:T(8,128)(2,1)}, bf16[256,1024]{1,0:T(8,128)(2,1)S(1)}, u32[]{:S(2)}, u32[]{:S(2)}) collective-permute-start(bf16[256,1024]{1,0:T(8,128)(2,1)} %broadcast_select_fusion.1), channel_id=1, source_target_pairs={{0,4},{4,8},{8,12},{12,16},{16,20},{20,24},{24,28},{28,0},{1,5},{5... | collective-permute-start | bytes 1572872 | tf_op jit(solution)/shard_map/ppermute | solution.py:38
  51.5 4.1 %copy-start.1 = (bf16[4,256,896]{2,1,0:T(8,128)(2,1)}, bf16[4,256,896]{2,1,0:T(8,128)(2,1)S(1)}, u32[]{:S(2)}) copy-start(bf16[4,256,896]{2,1,0:T(8,128)(2,1)S(1)} %pad_maximum_fusion.wa_ref) | copy-start | bytes 5505028
  51.5 11.3 %copy-start.10 = (bf16[1,256,1792]{2,1,0:T(8,128)(2,1)S(1)}, bf16[1,256,1792]{2,1,0:T(8,128)(2,1)}, u32[]{:S(2)}) copy-start(bf16[1,256,1792]{2,1,0:T(8,128)(2,1)} %param.9) | copy-start | bytes 2752516
  51.5 77.1 %collective-permute-start.12 = (bf16[4,256,896]{2,1,0:T(8,128)(2,1)S(1)}, bf16[4,256,896]{2,1,0:T(8,128)(2,1)}, u32[]{:S(2)}, u32[]{:S(2)}) collective-permute-start(bf16[4,256,896]{2,1,0:T(8,128)(2,1)S(1)} %pad_maximum_fusion.wa_ref), channel_id=1, source_target_pairs={{0,1},{1,0},{2,3},{3,2},{4,5},{5,4},{6,7},{7,6},{8,9},{9,8},{10,11... | collective-permute-start | bytes 5505032 | tf_op jit(solution)/shard_map/ppermute | solution.py:55
  55.6 32.1 %collective-permute-start.13 = (bf16[4,128,896]{2,1,0:T(8,128)(2,1)}, bf16[4,128,896]{2,1,0:T(8,128)(2,1)}, u32[]{:S(2)}, u32[]{:S(2)}) collective-permute-start(bf16[4,128,896]{2,1,0:T(8,128)(2,1)} %get-tuple-element.70), channel_id=1, source_target_pairs={{0,32},{32,2},{2,34},{34,0},{1,33},{33,3},{3,35},{35,1},{4,36},{36... | collective-permute-start | bytes 2752520 | tf_op jit(solution)/shard_map/ppermute | solution.py:43
  56.8 34.2 %collective-permute-start.14 = (bf16[4,128,896]{2,1,0:T(8,128)(2,1)}, bf16[4,128,896]{2,1,0:T(8,128)(2,1)}, u32[]{:S(2)}, u32[]{:S(2)}) collective-permute-start(bf16[4,128,896]{2,1,0:T(8,128)(2,1)} %get-tuple-element.69), channel_id=1, source_target_pairs={{0,34},{32,0},{2,32},{34,2},{1,35},{33,1},{3,33},{35,3},{4,38},{36... | collective-permute-start | bytes 2752520 | tf_op jit(solution)/shard_map/ppermute | solution.py:43
  58.9 1.8 collective-permute-start
  60.8 12.8 %collective-permute-start.2 = (bf16[256,1024]{1,0:T(8,128)(2,1)}, bf16[256,1024]{1,0:T(8,128)(2,1)S(1)}, u32[]{:S(2)}, u32[]{:S(2)}) collective-permute-start(bf16[256,1024]{1,0:T(8,128)(2,1)} %bitcast.51), channel_id=1, source_target_pairs={{0,4},{4,8},{8,12},{12,16},{16,20},{20,24},{24,28},{28,32},{32,36}... | collective-permute-start | bytes 1572872 | tf_op jit(solution)/shard_map/ppermute | solution.py:33
  62.1 29.0 %copy-start.4 = (bf16[256,1024]{1,0:T(8,128)(2,1)}, bf16[256,1024]{1,0:T(8,128)(2,1)S(1)}, u32[]{:S(2)}) copy-start(bf16[256,1024]{1,0:T(8,128)(2,1)S(1)} %collective-permute-done.5.v1_ref) | copy-start | bytes 1572868
  62.1 26.8 %collective-permute-start.6 = (bf16[256,1024]{1,0:T(8,128)(2,1)S(1)}, bf16[256,1024]{1,0:T(8,128)(2,1)S(1)}, u32[]{:S(2)}, u32[]{:S(2)}) collective-permute-start(bf16[256,1024]{1,0:T(8,128)(2,1)S(1)} %collective-permute-done.5.v1_ref), channel_id=1, source_target_pairs={{28,60},{60,92},{92,124},{124,156},{156,188},{188,220},{220,252},{... | collective-permute-start | bytes 1572872 | tf_op jit(solution)/shard_map/ppermute | solution.py:49
  63.1 28.1 %copy-start.6 = (bf16[256,896]{1,0:T(8,128)(2,1)}, bf16[256,896]{1,0:T(8,128)(2,1)S(1)}, u32[]{:S(2)}) copy-start(bf16[256,896]{1,0:T(8,128)(2,1)S(1)} %get-tuple-element.73.m_oth_ref) | copy-start | bytes 1376260
  63.1 52.4 %copy-start.2 = (bf16[256,896]{1,0:T(8,128)(2,1)}, bf16[256,896]{1,0:T(8,128)(2,1)S(1)}, u32[]{:S(2)}) copy-start(bf16[256,896]{1,0:T(8,128)(2,1)S(1)} %get-tuple-element.74.m_own_ref) | copy-start | bytes 1376260
  73.6 17.7 %copy-start.11 = (bf16[256,1024]{1,0:T(8,128)(2,1)}, bf16[256,1024]{1,0:T(8,128)(2,1)S(1)}, u32[]{:S(2)}) copy-start(bf16[256,1024]{1,0:T(8,128)(2,1)S(1)} %collective-permute-done.2.k1_ref) | copy-start | bytes 1572868
  73.6 17.6 %collective-permute-start.22 = (bf16[256,896]{1,0:T(8,128)(2,1)S(1)}, bf16[256,896]{1,0:T(8,128)(2,1)S(1)}, u32[]{:S(2)}, u32[]{:S(2)}) collective-permute-start(bf16[256,896]{1,0:T(8,128)(2,1)S(1)} %get-tuple-element.73.m_oth_ref), channel_id=1, source_target_pairs={{0,1},{1,0},{2,3},{3,2},{4,5},{5,4},{6,7},{7,6},{8,9},{9,8},{10,11... | collective-permute-start | bytes 1376264 | tf_op jit(solution)/shard_map/ppermute | solution.py:55
  87.7 42.1 %collective-permute-start.15 = (bf16[4,128,896]{2,1,0:T(8,128)(2,1)}, bf16[4,128,896]{2,1,0:T(8,128)(2,1)}, u32[]{:S(2)}, u32[]{:S(2)}) collective-permute-start(bf16[4,128,896]{2,1,0:T(8,128)(2,1)} %collective-permute-done.13.wbl_ref), channel_id=1, source_target_pairs={{0,1},{1,0},{2,3},{3,2},{4,5},{5,4},{6,7},{7,6},{8,9},{9,8},{10,11... | collective-permute-start | bytes 2752520 | tf_op jit(solution)/shard_map/ppermute | solution.py:55
  88.9 12.8 %collective-permute-start.3 = (bf16[256,1024]{1,0:T(8,128)(2,1)S(1)}, bf16[256,1024]{1,0:T(8,128)(2,1)}, u32[]{:S(2)}, u32[]{:S(2)}) collective-permute-start(bf16[256,1024]{1,0:T(8,128)(2,1)S(1)} %collective-permute-done.2.k1_ref), channel_id=1, source_target_pairs={{0,4},{4,8},{8,12},{12,16},{16,20},{20,24},{24,28},{28,32},{32,36}... | collective-permute-start | bytes 1572872 | tf_op jit(solution)/shard_map/ppermute | solution.py:33
  91.0 41.1 %collective-permute-start.16 = (bf16[4,128,896]{2,1,0:T(8,128)(2,1)}, bf16[4,128,896]{2,1,0:T(8,128)(2,1)}, u32[]{:S(2)}, u32[]{:S(2)}) collective-permute-start(bf16[4,128,896]{2,1,0:T(8,128)(2,1)} %collective-permute-done.14.wbh_ref), channel_id=1, source_target_pairs={{0,1},{1,0},{2,3},{3,2},{4,5},{5,4},{6,7},{7,6},{8,9},{9,8},{10,11... | collective-permute-start | bytes 2752520 | tf_op jit(solution)/shard_map/ppermute | solution.py:55
  91.2 27.4 %collective-permute-start.7 = (bf16[256,1024]{1,0:T(8,128)(2,1)S(1)}, bf16[256,1024]{1,0:T(8,128)(2,1)S(1)}, u32[]{:S(2)}, u32[]{:S(2)}) collective-permute-start(bf16[256,1024]{1,0:T(8,128)(2,1)S(1)} %broadcast_select_fusion), channel_id=1, source_target_pairs={{0,4},{4,8},{8,12},{12,16},{16,20},{20,24},{24,28},{28,0},{1,5},{5... | collective-permute-start | bytes 1572872 | tf_op jit(solution)/shard_map/ppermute | solution.py:38
  101.7 44.0 %collective-permute-start.24 = (bf16[512,896]{1,0:T(8,128)(2,1)}, bf16[512,896]{1,0:T(8,128)(2,1)}, u32[]{:S(2)}, u32[]{:S(2)}) collective-permute-start(bf16[512,896]{1,0:T(8,128)(2,1)} %pad_maximum_fusion.2.m0_ref), channel_id=1, source_target_pairs={{0,192},{64,0},{128,64},{192,128},{1,193},{65,1},{129,65},{193,129... | collective-permute-start | bytes 2752520 | tf_op jit(solution)/shard_map/ppermute | solution.py:38
  118.6 3.2 %copy-start.3 = (bf16[256,1024]{1,0:T(8,128)(2,1)}, bf16[256,1024]{1,0:T(8,128)(2,1)S(1)}, u32[]{:S(2)}) copy-start(bf16[256,1024]{1,0:T(8,128)(2,1)S(1)} %collective-permute-done.7.v2_ref) | copy-start | bytes 1572868
  118.6 9.9 %collective-permute-start.1 = (f32[1]{0:T(128)}, f32[1]{0:T(128)}, u32[]{:S(2)}, u32[]{:S(2)}) collective-permute-start(f32[1]{0:T(128)} %add.53), channel_id=1, source_target_pairs={{0,2},{2,0},{1,3},{3,1},{4,6},{6,4},{5,7},{7,5},{8,10},{10,8},{9,1... | collective-permute-start | bytes 20 | tf_op jit(solution)/shard_map/ppermute | solution.py:55
  128.5 14.1 %collective-permute-start.18 = (bf16[512,256]{1,0:T(8,128)(2,1)}, bf16[512,256]{1,0:T(8,128)(2,1)S(1)}, u32[]{:S(2)}, u32[]{:S(2)}) collective-permute-start(bf16[512,256]{1,0:T(8,128)(2,1)} %get-tuple-element.52), channel_id=1, source_target_pairs={{0,64},{64,128},{128,192},{192,0},{1,65},{65,129},{129,193},{193,1... | collective-permute-start | bytes 786440 | tf_op jit(solution)/shard_map/ppermute | solution.py:38
  128.6 14.0 %collective-permute-start.19 = (bf16[512,256]{1,0:T(8,128)(2,1)}, bf16[512,256]{1,0:T(8,128)(2,1)S(1)}, u32[]{:S(2)}, u32[]{:S(2)}) collective-permute-start(bf16[512,256]{1,0:T(8,128)(2,1)} %get-tuple-element.53), channel_id=1, source_target_pairs={{0,128},{64,192},{128,0},{192,64},{1,129},{65,193},{129,1},{193,65... | collective-permute-start | bytes 786440 | tf_op jit(solution)/shard_map/ppermute | solution.py:38
  129.8 13.3 %collective-permute-start.20 = (bf16[512,256]{1,0:T(8,128)(2,1)}, bf16[512,256]{1,0:T(8,128)(2,1)S(1)}, u32[]{:S(2)}, u32[]{:S(2)}) collective-permute-start(bf16[512,256]{1,0:T(8,128)(2,1)} %get-tuple-element.54), channel_id=1, source_target_pairs={{0,192},{64,0},{128,64},{192,128},{1,193},{65,1},{129,65},{193,129... | collective-permute-start | bytes 786440 | tf_op jit(solution)/shard_map/ppermute | solution.py:38
  132.1 11.0 %copy-start.12 = (bf16[512,256]{1,0:T(8,128)(2,1)S(1)}, bf16[512,256]{1,0:T(8,128)(2,1)}, u32[]{:S(2)}) copy-start(bf16[512,256]{1,0:T(8,128)(2,1)} %get-tuple-element.55) | copy-start | bytes 786436
  143.3 27.1 %copy-start.8 = (bf16[4,512,256]{2,1,0:T(8,128)(2,1)}, bf16[4,512,256]{2,1,0:T(8,128)(2,1)S(1)}, u32[]{:S(2)}) copy-start(bf16[4,512,256]{2,1,0:T(8,128)(2,1)S(1)} %pad_maximum_fusion.1.a_own_ref) | copy-start | bytes 3145732
  143.3 27.1 %collective-permute-start.21 = (bf16[4,512,256]{2,1,0:T(8,128)(2,1)S(1)}, bf16[4,512,256]{2,1,0:T(8,128)(2,1)S(1)}, u32[]{:S(2)}, u32[]{:S(2)}) collective-permute-start(bf16[4,512,256]{2,1,0:T(8,128)(2,1)S(1)} %pad_maximum_fusion.1.a_own_ref), channel_id=1, source_target_pairs={{0,1},{1,0},{2,3},{3,2},{4,5},{5,4},{6,7},{7,6},{8,9},{9,8},{10,11... | collective-permute-start | bytes 3145736 | tf_op jit(solution)/shard_map/ppermute | solution.py:55
  145.2 23.2 %collective-permute-start.23 = (bf16[512,896]{1,0:T(8,128)(2,1)}, bf16[512,896]{1,0:T(8,128)(2,1)S(1)}, u32[]{:S(2)}, u32[]{:S(2)}) collective-permute-start(bf16[512,896]{1,0:T(8,128)(2,1)} %pad_maximum_fusion.2.m0_ref), channel_id=1, source_target_pairs={{0,64},{64,128},{128,192},{192,0},{1,65},{65,129},{129,193},{193,1... | collective-permute-start | bytes 2752520 | tf_op jit(solution)/shard_map/ppermute | solution.py:38
  145.7 23.7 %collective-permute-start.25 = (bf16[512,896]{1,0:T(8,128)(2,1)}, bf16[512,896]{1,0:T(8,128)(2,1)S(1)}, u32[]{:S(2)}, u32[]{:S(2)}) collective-permute-start(bf16[512,896]{1,0:T(8,128)(2,1)} %collective-permute-done.24.m3_ref), channel_id=1, source_target_pairs={{0,192},{64,0},{128,64},{192,128},{1,193},{65,1},{129,65},{193,129... | collective-permute-start | bytes 2752520 | tf_op jit(solution)/shard_map/ppermute | solution.py:38
  147.9 36.0 %collective-permute-start.17 = (bf16[512,1024]{1,0:T(8,128)(2,1)}, bf16[512,1024]{1,0:T(8,128)(2,1)S(1)}, u32[]{:S(2)}, u32[]{:S(2)}) collective-permute-start(bf16[512,1024]{1,0:T(8,128)(2,1)} %get-tuple-element.50), channel_id=1, source_target_pairs={{4,0},{8,4},{12,8},{16,12},{20,16},{24,20},{28,24},{32,28},{36,32}... | collective-permute-start | bytes 3145736 | tf_op jit(solution)/shard_map/ppermute | solution.py:33
  168.5 0.9 copy-start.15
  169.4 0.9 copy-start.16
  170.4 1.0 copy-start.14
  177.4 6.5 %collective-permute-start.29 = (bf16[128,896]{1,0:T(8,128)(2,1)}, bf16[128,896]{1,0:T(8,128)(2,1)S(1)}, u32[]{:S(2)}, u32[]{:S(2)}) collective-permute-start(bf16[128,896]{1,0:T(8,128)(2,1)} %get-tuple-element.62), channel_id=1, source_target_pairs={{0,34},{32,0},{2,32},{34,2},{1,35},{33,1},{3,33},{35,3},{4,38},{36... | collective-permute-start | bytes 688136 | tf_op jit(solution)/shard_map/ppermute | solution.py:43
  177.8 7.7 %collective-permute-start.28 = (bf16[128,896]{1,0:T(8,128)(2,1)}, bf16[128,896]{1,0:T(8,128)(2,1)S(1)}, u32[]{:S(2)}, u32[]{:S(2)}) collective-permute-start(bf16[128,896]{1,0:T(8,128)(2,1)} %get-tuple-element.61), channel_id=1, source_target_pairs={{0,2},{32,34},{2,0},{34,32},{1,3},{33,35},{3,1},{35,33},{4,6},{36,... | collective-permute-start | bytes 688136 | tf_op jit(solution)/shard_map/ppermute | solution.py:43
  179.0 12.9 %collective-permute-start.27 = (bf16[128,896]{1,0:T(8,128)(2,1)}, bf16[128,896]{1,0:T(8,128)(2,1)S(1)}, u32[]{:S(2)}, u32[]{:S(2)}) collective-permute-start(bf16[128,896]{1,0:T(8,128)(2,1)} %get-tuple-element.60), channel_id=1, source_target_pairs={{0,32},{32,2},{2,34},{34,0},{1,33},{33,3},{3,35},{35,1},{4,36},{36... | collective-permute-start | bytes 688136 | tf_op jit(solution)/shard_map/ppermute | solution.py:43
  179.0 12.9 %copy-start.13 = (bf16[128,896]{1,0:T(8,128)(2,1)S(1)}, bf16[128,896]{1,0:T(8,128)(2,1)}, u32[]{:S(2)}) copy-start(bf16[128,896]{1,0:T(8,128)(2,1)} %get-tuple-element.59) | copy-start | bytes 688132
  183.9 28.8 %copy-start.7 = (bf16[512,1024]{1,0:T(8,128)(2,1)S(1)}, bf16[512,1024]{1,0:T(8,128)(2,1)}, u32[]{:S(2)}) copy-start(bf16[512,1024]{1,0:T(8,128)(2,1)} %get-tuple-element.49) | copy-start | bytes 3145732
  192.7 30.0 %all-to-all-start.1 = ((bf16[8,16,896]{2,1,0:T(8,128)(2,1)}), bf16[8,16,896]{2,1,0:T(8,128)(2,1)S(1)}, u32[]{:S(2)}, u32[]{:S(2)}) async-start(bf16[8,16,896]{2,1,0:T(8,128)(2,1)} %bitcast.22), calls=%async_computation.1 | async-start | bytes 458752 | tf_op jit(solution)/shard_map/all_to_all | solution.py:418
  213.1 28.9 %collective-permute-start.26 = (bf16[512,1024]{1,0:T(8,128)(2,1)S(1)}, bf16[512,1024]{1,0:T(8,128)(2,1)S(1)}, u32[]{:S(2)}, u32[]{:S(2)}) collective-permute-start(bf16[512,1024]{1,0:T(8,128)(2,1)S(1)} %add_convert_fusion), channel_id=1, source_target_pairs={{4,0},{8,4},{12,8},{16,12},{20,16},{24,20},{28,24},{32,28},{36,32}... | collective-permute-start | bytes 3145736 | tf_op jit(solution)/shard_map/ppermute | solution.py:33
  223.4 3.4 %collective-permute-start.30 = (f32[16,896]{1,0:T(8,128)S(1)}, f32[16,896]{1,0:T(8,128)S(1)}, u32[]{:S(2)}, u32[]{:S(2)}) collective-permute-start(f32[16,896]{1,0:T(8,128)S(1)} %get-tuple-element.66), channel_id=1, source_target_pairs={{0,1},{1,0},{2,3},{3,2},{4,5},{5,4},{6,7},{7,6},{8,9},{9,8},{10,11... | collective-permute-start | bytes 172040 | tf_op jit(solution)/shard_map/ppermute | solution.py:55
  226.8 25.1 %collective-permute-start.31 = (f32[16,1792]{1,0:T(8,128)S(1)}, f32[16,1792]{1,0:T(8,128)S(1)}, u32[]{:S(2)}, u32[]{:S(2)}) collective-permute-start(f32[16,1792]{1,0:T(8,128)S(1)} %maximum_select_fusion.1), channel_id=1, source_target_pairs={{0,2},{2,0},{1,3},{3,1},{4,6},{6,4},{5,7},{7,5},{8,10},{10,8},{9,1... | collective-permute-start | bytes 344072 | tf_op jit(solution)/shard_map/ppermute | solution.py:55
  247.3 9.3 %all-to-all-start.2 = ((f32[8,8,128]{2,1,0:T(8,128)}), f32[8,8,128]{2,1,0:T(8,128)S(1)}, u32[]{:S(2)}, u32[]{:S(2)}) async-start(f32[8,8,128]{2,1,0:T(8,128)} %broadcast_in_dim_broadcast_in_dim_broadcast_in_dim.6), calls=%async_computation.2 | async-start | bytes 65536 | tf_op jit(solution)/shard_map/all_to_all | solution.py:60
  257.4 17.2 %all-to-all-start.3 = ((f32[32,8,128]{2,1,0:T(8,128)}), f32[32,8,128]{2,1,0:T(8,128)S(1)}, u32[]{:S(2)}, u32[]{:S(2)}) async-start(f32[32,8,128]{2,1,0:T(8,128)} %broadcast_in_dim_broadcast_in_dim_broadcast_in_dim.7), calls=%async_computation.3 | async-start | bytes 262144 | tf_op jit(solution)/shard_map/all_to_all | solution.py:60
